TPU v7x, 32 devices: a whole 2x2x4 slice. The times are simulated.
32 devices in a mesh: fsdp: 4 (over x, core), ctx: 2 (over y), tp: 4 (over z).
Axes of the slice: x: 2, y: 2, z: 4, core: 2. Of those that a mesh axis runs over, the one named last changes fastest.
Arguments:
- inputs: bfloat16 [8, 1024, 1024], P('fsdp', 'ctx'), may hold values from -6 to 6
- encoder: bfloat16 [8, 512, 1024], P('fsdp', 'ctx'), may hold values from -6 to 6
- lengths: int32 [8], P('fsdp'), may hold values from 256 to 1024, as said below
- cotangent: bfloat16 [8, 1024, 1024], P('fsdp', 'ctx'), may hold values from -6 to 6
- norm_self: bfloat16 [1024], P(('fsdp', 'ctx')), may hold values from 0.5 to 1.5
- self_query: bfloat16 [1024, 1024], P(('fsdp', 'ctx'), 'tp'), may hold values from -0.046875 to 0.046875
- self_key_matrix: bfloat16 [1024, 512], P(('fsdp', 'ctx'), 'tp'), may hold values from -0.1875 to 0.1875
- self_value_matrix: bfloat16 [1024, 512], P(('fsdp', 'ctx'), 'tp'), may hold values from -0.1875 to 0.1875
- self_out: bfloat16 [1024, 1024], P(('fsdp', 'ctx'), 'tp'), may hold values from -0.75 to 0.75
- bias_table: bfloat16 [32, 16], P(('fsdp', 'ctx'), 'tp'), may hold values from -4 to 4
- norm_cross: bfloat16 [1024], P(('fsdp', 'ctx')), may hold values from 0.5 to 1.5
- cross_query: bfloat16 [1024, 1024], P(('fsdp', 'ctx'), 'tp'), may hold values from -0.046875 to 0.046875
- cross_key_matrix: bfloat16 [1024, 512], P(('fsdp', 'ctx'), 'tp'), may hold values from -0.1875 to 0.1875
- cross_value_matrix: bfloat16 [1024, 512], P(('fsdp', 'ctx'), 'tp'), may hold values from -0.1875 to 0.1875
- cross_out: bfloat16 [1024, 1024], P(('fsdp', 'ctx'), 'tp'), may hold values from -0.75 to 0.75
- norm_feed: bfloat16 [1024], P(('fsdp', 'ctx')), may hold values from 0.5 to 1.5
- feed_gate: bfloat16 [1024, 2816], P(('fsdp', 'ctx'), 'tp'), may hold values from -0.1875 to 0.1875
- feed_up: bfloat16 [1024, 2816], P(('fsdp', 'ctx'), 'tp'), may hold values from -0.1875 to 0.1875
- feed_out: bfloat16 [1024, 2816], P(('fsdp', 'ctx'), 'tp'), may hold values from -0.109375 to 0.109375
Outputs:
- output: bfloat16 [8, 1024, 1024], P('fsdp', 'ctx')
- grad_inputs: float32 [8, 1024, 1024], P('fsdp', 'ctx')
- grad_encoder: float32 [8, 512, 1024], P('fsdp', 'ctx')
- grad_norm_self: float32 [1024], P(('fsdp', 'ctx'))
- grad_self_query: float32 [1024, 1024], P(('fsdp', 'ctx'), 'tp')
- grad_self_key: float32 [1024, 512], P(('fsdp', 'ctx'), 'tp')
- grad_self_value: float32 [1024, 512], P(('fsdp', 'ctx'), 'tp')
- grad_self_out: float32 [1024, 1024], P(('fsdp', 'ctx'), 'tp')
- grad_bias_table: float32 [32, 16], P(('fsdp', 'ctx'), 'tp')
- grad_norm_cross: float32 [1024], P(('fsdp', 'ctx'))
- grad_cross_query: float32 [1024, 1024], P(('fsdp', 'ctx'), 'tp')
- grad_cross_key: float32 [1024, 512], P(('fsdp', 'ctx'), 'tp')
- grad_cross_value: float32 [1024, 512], P(('fsdp', 'ctx'), 'tp')
- grad_cross_out: float32 [1024, 1024], P(('fsdp', 'ctx'), 'tp')
- grad_norm_feed: float32 [1024], P(('fsdp', 'ctx'))
- grad_feed_gate: float32 [1024, 2816], P(('fsdp', 'ctx'), 'tp')
- grad_feed_up: float32 [1024, 2816], P(('fsdp', 'ctx'), 'tp')
- grad_feed_out: float32 [1024, 2816], P(('fsdp', 'ctx'), 'tp')
Inputs may be any that keep to these rules, and one draw needn't show every extreme that they name: `lengths`: number of real tokens of each sequence; slots from there on are padding; some sequence is full and some has the fewest.
All inputs are finite; a program needn't handle non-finite values.
Results may differ from a plain program's by a relative error of at most 0.03.
The roundings to bfloat16 on the way count: a program that leaves them out, or rounds other values in their place, can miss the bound.
Values may be sent and summed in bfloat16 or wider, within the bound.
A program may use at most 192 MiB of HBM per device.

v0:
```python
import math

import jax
import jax.numpy as jnp
from jax import lax
from jax.sharding import PartitionSpec as P

HEAD_SIZE = 64
BUCKETS = 32
MAXDIST = 128


EPSILON = 1e-06
MASKED = -1000000000.0
TOP_PRECISION = lax.Precision.HIGHEST


def rms_scale(values, gain_row):
    inverse = lax.rsqrt(jnp.mean(values * values, axis=-1, keepdims=True) + EPSILON)
    return values * inverse * gain_row


def gated_product(gate_in, up_in):
    return jax.nn.gelu(gate_in, approximate=True) * up_in


def project(operand_array, weight_arrays):
    return jnp.einsum(
        "spd,dk->spk", operand_array, weight_arrays, preferred_element_type=jnp.float32
    )


def project_back(grad_cols, weight_arrays):
    return jnp.einsum("spk,dk->spd", grad_cols, weight_arrays, preferred_element_type=jnp.float32)


def weight_grad(operand_array, grad_cols):
    return jnp.einsum("spd,spk->dk", operand_array, grad_cols, preferred_element_type=jnp.float32)


def bucket_index(distance):
    exact_count = BUCKETS // 2
    counter = jnp.zeros(distance.shape, jnp.int32)
    for level_index in range(1, BUCKETS - exact_count):
        border = math.ceil(
            exact_count * (MAXDIST / exact_count) ** (level_index / (BUCKETS - exact_count))
        )
        counter = counter + (distance >= border).astype(jnp.int32)
    return jnp.where(distance < exact_count, distance, exact_count + counter)


def reduce_rows(partial_sum):
    return lax.psum(partial_sum, "tp")


def block_scores(queries, key_rows, bias_rows, allowed):
    scores = jnp.einsum("gpkrd,gjkd->gkrpj", queries, key_rows, preferred_element_type=jnp.float32)
    if bias_rows is not None:
        scores = jnp.where(allowed[:, None, None], scores + bias_rows[None], MASKED)
    return scores


def forward_block(queries, key_rows, value_rows, bias_rows, allowed):
    scores = block_scores(queries, key_rows, bias_rows, allowed)
    row_peak = jnp.max(scores, axis=-1, keepdims=True)
    log_total = row_peak + jnp.log(jnp.sum(jnp.exp(scores - row_peak), axis=-1, keepdims=True))
    weights_low = jnp.exp(scores - log_total).astype(jnp.bfloat16)
    output = jnp.einsum(
        "gkrpj,gjkd->gpkrd", weights_low, value_rows, preferred_element_type=jnp.float32
    )
    return (output.astype(jnp.bfloat16), log_total)


def backward_block(queries, key_rows, value_rows, bias_rows, allowed, log_total, grad_out):
    scores = block_scores(queries, key_rows, bias_rows, allowed)
    softmax_rows = jnp.exp(scores - log_total)
    grad_probs = jnp.einsum(
        "gpkrd,gjkd->gkrpj", grad_out, value_rows, preferred_element_type=jnp.float32
    )
    grad_scores = softmax_rows * (
        grad_probs - jnp.sum(grad_probs * softmax_rows, axis=-1, keepdims=True)
    )
    scores_low = grad_scores.astype(jnp.bfloat16)
    grad_query = jnp.einsum(
        "gkrpj,gjkd->gpkrd", scores_low, key_rows, preferred_element_type=jnp.float32
    )
    grad_key = jnp.einsum(
        "gkrpj,gpkrd->gjkd", scores_low, queries, preferred_element_type=jnp.float32
    )
    grad_value = jnp.einsum(
        "gkrpj,gpkrd->gjkd",
        softmax_rows.astype(jnp.bfloat16),
        grad_out,
        preferred_element_type=jnp.float32,
    )
    if bias_rows is None:
        grad_bias = jnp.zeros((1,), jnp.float32)
    else:
        grad_bias = jnp.sum(grad_scores, axis=0)
    return (grad_query.astype(jnp.bfloat16), grad_key, grad_value, grad_bias)


def block_shapes(queries, key_rows, block_seqs):
    seq_count, row_total_count, query_cols = queries.shape
    key_total_count, key_cols = (key_rows.shape[1], key_rows.shape[2])
    kv_heads = key_cols // HEAD_SIZE
    repeats = query_cols // key_cols
    blocks = seq_count // block_seqs
    query_shape = (blocks, block_seqs, row_total_count, kv_heads, repeats, HEAD_SIZE)
    key_shape = (blocks, block_seqs, key_total_count, kv_heads, HEAD_SIZE)
    mask_shape = (blocks, block_seqs, row_total_count, key_total_count)
    return (query_shape, key_shape, mask_shape)


def attention_forward(queries, key_rows, value_rows, bias_rows, allowed, block_seqs):
    query_shape, key_shape, mask_shape = block_shapes(queries, key_rows, block_seqs)
    sources = (
        queries.reshape(query_shape),
        key_rows.reshape(key_shape),
        value_rows.reshape(key_shape),
    )
    if allowed is not None:
        sources = sources + (allowed.reshape(mask_shape),)

    def one_block(piece_list):
        mask_block = piece_list[3] if allowed is not None else None
        return forward_block(piece_list[0], piece_list[1], piece_list[2], bias_rows, mask_block)

    outputs, log_totals = lax.map(one_block, sources)
    return (outputs.reshape(queries.shape), log_totals)


def attention_backward(
    queries, key_rows, value_rows, bias_rows, allowed, log_totals, grad_out, block_seqs
):
    query_shape, key_shape, mask_shape = block_shapes(queries, key_rows, block_seqs)
    sources = (
        queries.reshape(query_shape),
        key_rows.reshape(key_shape),
        value_rows.reshape(key_shape),
        log_totals,
        grad_out.reshape(query_shape),
    )
    if allowed is not None:
        sources = sources + (allowed.reshape(mask_shape),)
    if bias_rows is None:
        initial = jnp.zeros((1,), jnp.float32)
    else:
        initial = jnp.zeros(bias_rows.shape, jnp.float32)

    def one_block(running, piece_list):
        mask_block = piece_list[5] if allowed is not None else None
        grad_query, grad_key, grad_value, grad_bias = backward_block(
            piece_list[0],
            piece_list[1],
            piece_list[2],
            bias_rows,
            mask_block,
            piece_list[3],
            piece_list[4],
        )
        return (running + grad_bias, (grad_query, grad_key, grad_value))

    bias_total, grad_list = lax.scan(one_block, initial, sources)
    return (
        grad_list[0].reshape(queries.shape),
        grad_list[1].reshape(key_rows.shape),
        grad_list[2].reshape(value_rows.shape),
        bias_total,
    )


def shards(
    inputs,
    encoder,
    lengths,
    cotangent,
    norm_self,
    self_query,
    self_key_matrix,
    self_value_matrix,
    self_out,
    bias_table,
    norm_cross,
    cross_query,
    cross_key_matrix,
    cross_value_matrix,
    cross_out,
    norm_feed,
    feed_gate,
    feed_up,
    feed_out,
):
    self_group = (
        lax.all_gather(norm_self, ("fsdp", "ctx"), axis=0, tiled=True),
        lax.all_gather(self_query, ("fsdp", "ctx"), axis=0, tiled=True),
        lax.all_gather(self_key_matrix, ("fsdp", "ctx"), axis=0, tiled=True),
        lax.all_gather(self_value_matrix, ("fsdp", "ctx"), axis=0, tiled=True),
        lax.all_gather(self_out, ("fsdp", "ctx"), axis=0, tiled=True),
        lax.all_gather(bias_table, ("fsdp", "ctx"), axis=0, tiled=True),
    )
    seq_count, row_total_count = (inputs.shape[0], inputs.shape[1])
    block_seqs = max((trial for trial in (1, 2, 3, 4) if seq_count % trial == 0))
    start_row = lax.axis_index("ctx") * row_total_count
    key_total_count = row_total_count * lax.axis_size("ctx")
    row_pos = start_row + jnp.arange(row_total_count, dtype=jnp.int32)
    col_pos = jnp.arange(key_total_count, dtype=jnp.int32)
    buckets = bucket_index(jnp.maximum(row_pos[:, None] - col_pos[None, :], 0))
    one_hot = (buckets[:, :, None] == jnp.arange(BUCKETS, dtype=jnp.int32)[None, None, :]).astype(
        jnp.float32
    )
    causal = col_pos[None, :] <= row_pos[:, None]
    allowed = causal[None] & (col_pos[None, None, :] < lengths[:, None, None])
    hidden_in = inputs.astype(jnp.float32)
    normed_one, norm_pull_one = jax.vjp(rms_scale, hidden_in, self_group[0].astype(jnp.float32))
    self_in = normed_one.astype(jnp.bfloat16)
    self_q = project(self_in, self_group[1]).astype(jnp.bfloat16)
    self_k = project(self_in, self_group[2]).astype(jnp.bfloat16)
    self_v = project(self_in, self_group[3]).astype(jnp.bfloat16)
    keys_self, values_self = (
        lax.all_gather(self_k, "ctx", axis=1, tiled=True),
        lax.all_gather(self_v, "ctx", axis=1, tiled=True),
    )
    heads_local = self_group[1].shape[1] // HEAD_SIZE
    kv_local = self_group[2].shape[1] // HEAD_SIZE
    table_rows = self_group[5].astype(jnp.float32)
    bias_rows = jnp.einsum("ijb,bh->hij", one_hot, table_rows, precision=TOP_PRECISION).reshape(
        kv_local, heads_local // kv_local, row_total_count, key_total_count
    )
    self_att, lse_self = attention_forward(
        self_q, keys_self, values_self, bias_rows, allowed, block_seqs
    )
    hidden_two = hidden_in + reduce_rows(project_back(self_att, self_group[4]))
    cross_group = (
        lax.all_gather(norm_cross, ("fsdp", "ctx"), axis=0, tiled=True),
        lax.all_gather(cross_query, ("fsdp", "ctx"), axis=0, tiled=True),
        lax.all_gather(cross_key_matrix, ("fsdp", "ctx"), axis=0, tiled=True),
        lax.all_gather(cross_value_matrix, ("fsdp", "ctx"), axis=0, tiled=True),
        lax.all_gather(cross_out, ("fsdp", "ctx"), axis=0, tiled=True),
    )
    normed_two, norm_pull_two = jax.vjp(rms_scale, hidden_two, cross_group[0].astype(jnp.float32))
    cross_in = normed_two.astype(jnp.bfloat16)
    cross_q = project(cross_in, cross_group[1]).astype(jnp.bfloat16)
    enc_keys = project(encoder, cross_group[2]).astype(jnp.bfloat16)
    enc_values = project(encoder, cross_group[3]).astype(jnp.bfloat16)
    keys_cross, values_cross = (
        lax.all_gather(enc_keys, "ctx", axis=1, tiled=True),
        lax.all_gather(enc_values, "ctx", axis=1, tiled=True),
    )
    cross_att, lse_cross = attention_forward(
        cross_q, keys_cross, values_cross, None, None, block_seqs
    )
    hidden_three = hidden_two + reduce_rows(project_back(cross_att, cross_group[4]))
    feed_group = (
        lax.all_gather(norm_feed, ("fsdp", "ctx"), axis=0, tiled=True),
        lax.all_gather(feed_gate, ("fsdp", "ctx"), axis=0, tiled=True),
        lax.all_gather(feed_up, ("fsdp", "ctx"), axis=0, tiled=True),
        lax.all_gather(feed_out, ("fsdp", "ctx"), axis=0, tiled=True),
    )
    normed_three, norm_pull_three = jax.vjp(
        rms_scale, hidden_three, feed_group[0].astype(jnp.float32)
    )
    feed_in = normed_three.astype(jnp.bfloat16)
    gate_value = project(feed_in, feed_group[1])
    up_value = project(feed_in, feed_group[2])
    gated_value, gated_pull = jax.vjp(gated_product, gate_value, up_value)
    feed_hidden = gated_value.astype(jnp.bfloat16)
    hidden_four = hidden_three + reduce_rows(project_back(feed_hidden, feed_group[3]))
    output = hidden_four.astype(jnp.bfloat16)
    valid_rows = (row_pos[None, :] < lengths[:, None]).astype(jnp.float32)
    grad_full = cotangent.astype(jnp.float32) * valid_rows[:, :, None]
    branch_low = grad_full.astype(jnp.bfloat16)
    grad_hidden = grad_full
    grad_feed_out = weight_grad(branch_low, feed_hidden)
    grad_gated = project(branch_low, feed_group[3])
    grad_gate, grad_up = gated_pull(grad_gated)
    gate_low = grad_gate.astype(jnp.bfloat16)
    up_low = grad_up.astype(jnp.bfloat16)
    grad_feed_gate = weight_grad(feed_in, gate_low)
    grad_feed_up = weight_grad(feed_in, up_low)
    grad_feed_in = reduce_rows(
        project_back(gate_low, feed_group[1]) + project_back(up_low, feed_group[2])
    )
    grad_three, grad_gain_three = norm_pull_three(grad_feed_in)
    grad_hidden = grad_hidden + grad_three
    feed_grads = (
        lax.psum_scatter(
            grad_gain_three.astype(jnp.bfloat16), ("fsdp", "ctx"), scatter_dimension=0, tiled=True
        ).astype(jnp.float32),
        lax.psum_scatter(
            grad_feed_gate.astype(jnp.bfloat16), ("fsdp", "ctx"), scatter_dimension=0, tiled=True
        ).astype(jnp.float32),
        lax.psum_scatter(
            grad_feed_up.astype(jnp.bfloat16), ("fsdp", "ctx"), scatter_dimension=0, tiled=True
        ).astype(jnp.float32),
        lax.psum_scatter(
            grad_feed_out.astype(jnp.bfloat16), ("fsdp", "ctx"), scatter_dimension=0, tiled=True
        ).astype(jnp.float32),
    )
    cross_low = grad_hidden.astype(jnp.bfloat16)
    grad_cross_out = weight_grad(cross_low, cross_att)
    grad_cross_att = project(cross_low, cross_group[4]).astype(jnp.bfloat16)
    grad_cq, grad_ck_part, grad_cv_part, unused_bias = attention_backward(
        cross_q, keys_cross, values_cross, None, None, lse_cross, grad_cross_att, block_seqs
    )
    grad_ck, grad_cv = (
        lax.psum_scatter(
            grad_ck_part.astype(jnp.bfloat16), "ctx", scatter_dimension=1, tiled=True
        ).astype(jnp.float32),
        lax.psum_scatter(
            grad_cv_part.astype(jnp.bfloat16), "ctx", scatter_dimension=1, tiled=True
        ).astype(jnp.float32),
    )
    ck_low = grad_ck.astype(jnp.bfloat16)
    cv_low = grad_cv.astype(jnp.bfloat16)
    grad_cross_query = weight_grad(cross_in, grad_cq)
    grad_cross_key = weight_grad(encoder, ck_low)
    grad_cross_value = weight_grad(encoder, cv_low)
    grad_cross_in, grad_encoder = reduce_rows(
        (
            project_back(grad_cq, cross_group[1]),
            project_back(ck_low, cross_group[2]) + project_back(cv_low, cross_group[3]),
        )
    )
    grad_two, grad_gain_two = norm_pull_two(grad_cross_in)
    grad_hidden = grad_hidden + grad_two
    cross_grads = (
        lax.psum_scatter(
            grad_gain_two.astype(jnp.bfloat16), ("fsdp", "ctx"), scatter_dimension=0, tiled=True
        ).astype(jnp.float32),
        lax.psum_scatter(
            grad_cross_query.astype(jnp.bfloat16), ("fsdp", "ctx"), scatter_dimension=0, tiled=True
        ).astype(jnp.float32),
        lax.psum_scatter(
            grad_cross_key.astype(jnp.bfloat16), ("fsdp", "ctx"), scatter_dimension=0, tiled=True
        ).astype(jnp.float32),
        lax.psum_scatter(
            grad_cross_value.astype(jnp.bfloat16), ("fsdp", "ctx"), scatter_dimension=0, tiled=True
        ).astype(jnp.float32),
        lax.psum_scatter(
            grad_cross_out.astype(jnp.bfloat16), ("fsdp", "ctx"), scatter_dimension=0, tiled=True
        ).astype(jnp.float32),
    )
    self_low = grad_hidden.astype(jnp.bfloat16)
    grad_self_out = weight_grad(self_low, self_att)
    grad_self_att = project(self_low, self_group[4]).astype(jnp.bfloat16)
    grad_sq, grad_sk_part, grad_sv_part, bias_total = attention_backward(
        self_q, keys_self, values_self, bias_rows, allowed, lse_self, grad_self_att, block_seqs
    )
    grad_sk, grad_sv = (
        lax.psum_scatter(
            grad_sk_part.astype(jnp.bfloat16), "ctx", scatter_dimension=1, tiled=True
        ).astype(jnp.float32),
        lax.psum_scatter(
            grad_sv_part.astype(jnp.bfloat16), "ctx", scatter_dimension=1, tiled=True
        ).astype(jnp.float32),
    )
    sk_low = grad_sk.astype(jnp.bfloat16)
    sv_low = grad_sv.astype(jnp.bfloat16)
    grad_table = jnp.einsum(
        "ijb,hij->bh",
        one_hot,
        bias_total.reshape(heads_local, row_total_count, key_total_count),
        precision=TOP_PRECISION,
    )
    grad_self_query = weight_grad(self_in, grad_sq)
    grad_self_key = weight_grad(self_in, sk_low)
    grad_self_value = weight_grad(self_in, sv_low)
    grad_self_in = reduce_rows(
        project_back(grad_sq, self_group[1])
        + project_back(sk_low, self_group[2])
        + project_back(sv_low, self_group[3])
    )
    grad_one, grad_gain_one = norm_pull_one(grad_self_in)
    grad_inputs = grad_hidden + grad_one
    self_grads = (
        lax.psum_scatter(
            grad_gain_one.astype(jnp.bfloat16), ("fsdp", "ctx"), scatter_dimension=0, tiled=True
        ).astype(jnp.float32),
        lax.psum_scatter(
            grad_self_query.astype(jnp.bfloat16), ("fsdp", "ctx"), scatter_dimension=0, tiled=True
        ).astype(jnp.float32),
        lax.psum_scatter(
            grad_self_key.astype(jnp.bfloat16), ("fsdp", "ctx"), scatter_dimension=0, tiled=True
        ).astype(jnp.float32),
        lax.psum_scatter(
            grad_self_value.astype(jnp.bfloat16), ("fsdp", "ctx"), scatter_dimension=0, tiled=True
        ).astype(jnp.float32),
        lax.psum_scatter(
            grad_self_out.astype(jnp.bfloat16), ("fsdp", "ctx"), scatter_dimension=0, tiled=True
        ).astype(jnp.float32),
        lax.psum_scatter(
            grad_table.astype(jnp.bfloat16), ("fsdp", "ctx"), scatter_dimension=0, tiled=True
        ).astype(jnp.float32),
    )
    gain_shares = jnp.stack((self_grads[0], cross_grads[0], feed_grads[0]), axis=0)
    return (
        output,
        grad_inputs,
        grad_encoder,
        gain_shares[0],
        self_grads[1],
        self_grads[2],
        self_grads[3],
        self_grads[4],
        self_grads[5],
        gain_shares[1],
        cross_grads[1],
        cross_grads[2],
        cross_grads[3],
        cross_grads[4],
        gain_shares[2],
        feed_grads[1],
        feed_grads[2],
        feed_grads[3],
    )


def solution(mesh):
    return jax.shard_map(
        shards,
        mesh=mesh,
        in_specs=(
            P("fsdp", "ctx", None),
            P("fsdp", "ctx", None),
            P("fsdp"),
            P("fsdp", "ctx", None),
            P(("fsdp", "ctx")),
            P(("fsdp", "ctx"), "tp"),
            P(("fsdp", "ctx"), "tp"),
            P(("fsdp", "ctx"), "tp"),
            P(("fsdp", "ctx"), "tp"),
            P(("fsdp", "ctx"), "tp"),
            P(("fsdp", "ctx")),
            P(("fsdp", "ctx"), "tp"),
            P(("fsdp", "ctx"), "tp"),
            P(("fsdp", "ctx"), "tp"),
            P(("fsdp", "ctx"), "tp"),
            P(("fsdp", "ctx")),
            P(("fsdp", "ctx"), "tp"),
            P(("fsdp", "ctx"), "tp"),
            P(("fsdp", "ctx"), "tp"),
        ),
        out_specs=(
            P("fsdp", "ctx", None),
            P("fsdp", "ctx", None),
            P("fsdp", "ctx", None),
            P(("fsdp", "ctx")),
            P(("fsdp", "ctx"), "tp"),
            P(("fsdp", "ctx"), "tp"),
            P(("fsdp", "ctx"), "tp"),
            P(("fsdp", "ctx"), "tp"),
            P(("fsdp", "ctx"), "tp"),
            P(("fsdp", "ctx")),
            P(("fsdp", "ctx"), "tp"),
            P(("fsdp", "ctx"), "tp"),
            P(("fsdp", "ctx"), "tp"),
            P(("fsdp", "ctx"), "tp"),
            P(("fsdp", "ctx")),
            P(("fsdp", "ctx"), "tp"),
            P(("fsdp", "ctx"), "tp"),
            P(("fsdp", "ctx"), "tp"),
        ),
        check_vma=False,
    )
```

profile of v0, /device:TPU:12, one launch (start us, length us, event | category | flops | bytes accessed | tf_op | source)
XLA Modules:
  0.0 1427.4 jit_solution(12687213085237631720)
XLA Ops:
  16.0 11.4 all-gather
  27.5 13.5 all-gather.1
  41.2 16.7 %all_gather.60 = bf16[1024,128]{1,0:T(8,128)(2,1)S(1)} all-gather(bf16[128,128]{1,0:T(8,128)(2,1)S(1)} %copy-done.60), channel_id=1, replica_groups=mesh['fsdp'=4,'ctx'=2,'tp'=4] {'fsdp','ctx'}, dimensions={0}, use_global_device_ids=true | all-gather | bytes 294912 | tf_op jit(solution)/shard_map/all_gather | solution.py:197
  57.9 16.2 %all_gather.58 = bf16[1024,128]{1,0:T(8,128)(2,1)S(1)} all-gather(bf16[128,128]{1,0:T(8,128)(2,1)S(1)} %copy-done.61), channel_id=1, replica_groups=mesh['fsdp'=4,'ctx'=2,'tp'=4] {'fsdp','ctx'}, dimensions={0}, use_global_device_ids=true | all-gather | bytes 294912 | tf_op jit(solution)/shard_map/all_gather | solution.py:198
  98.4 18.0 %all_gather.62 = bf16[1024,256]{0,1:T(8,128)(2,1)S(1)} all-gather(bf16[128,256]{0,1:T(8,128)(2,1)S(1)} %copy.126), channel_id=1, replica_groups=mesh['fsdp'=4,'ctx'=2,'tp'=4] {'fsdp','ctx'}, dimensions={0}, use_global_device_ids=true | all-gather | bytes 589824 | tf_op jit(solution)/shard_map/all_gather | solution.py:196
  116.4 18.9 %all_gather.64 = bf16[1024,256]{1,0:T(8,128)(2,1)} all-gather(bf16[128,256]{1,0:T(8,128)(2,1)S(1)} %copy-done.50), channel_id=1, replica_groups=mesh['fsdp'=4,'ctx'=2,'tp'=4] {'fsdp','ctx'}, dimensions={0}, use_global_device_ids=true | all-gather | bytes 589824 | tf_op jit(solution)/shard_map/all_gather | solution.py:199
  139.3 14.3 %fusion.16 = f32[4,512,1024]{2,0,1:T(4,128)} fusion(bf16[32,4,1]{1,0,2:T(8,128)(2,1)S(1)} %bitcast.360, s32[512,1024]{1,0:T(8,128)} %compare_select_fusion), kind=kOutput, calls=%fused_computation.36 | convolution fusion | flops 150994944 | bytes 10486016 | tf_op jit(solution)/shard_map/ijb,bh->hij/dot_general | solution.py:227
  165.3 10.4 fusion.8
  200.7 11.1 all-gather.2
  211.9 16.6 %all_gather.67 = bf16[1024,128]{1,0:T(8,128)(2,1)S(1)} all-gather(bf16[128,128]{1,0:T(8,128)(2,1)S(1)} %copy-done.62), channel_id=1, replica_groups=mesh['fsdp'=4,'ctx'=2,'tp'=4] {'fsdp','ctx'}, dimensions={0}, use_global_device_ids=true | all-gather | bytes 294912 | tf_op jit(solution)/shard_map/all_gather | solution.py:237
  237.5 16.7 %all_gather.65 = bf16[1024,128]{1,0:T(8,128)(2,1)S(1)} all-gather(bf16[128,128]{1,0:T(8,128)(2,1)S(1)} %copy-done.63), channel_id=1, replica_groups=mesh['fsdp'=4,'ctx'=2,'tp'=4] {'fsdp','ctx'}, dimensions={0}, use_global_device_ids=true | all-gather | bytes 294912 | tf_op jit(solution)/shard_map/all_gather | solution.py:238
  261.5 19.1 %all_gather.70 = bf16[1024,256]{0,1:T(8,128)(2,1)} all-gather(bf16[128,256]{0,1:T(8,128)(2,1)S(1)} %copy.133), channel_id=1, replica_groups=mesh['fsdp'=4,'ctx'=2,'tp'=4] {'fsdp','ctx'}, dimensions={0}, use_global_device_ids=true | all-gather | bytes 589824 | tf_op jit(solution)/shard_map/all_gather | solution.py:236
  280.6 19.8 %all_gather.71 = bf16[1024,256]{1,0:T(8,128)(2,1)} all-gather(bf16[128,256]{1,0:T(8,128)(2,1)S(1)} %copy-done.51), channel_id=1, replica_groups=mesh['fsdp'=4,'ctx'=2,'tp'=4] {'fsdp','ctx'}, dimensions={0}, use_global_device_ids=true | all-gather | bytes 589824 | tf_op jit(solution)/shard_map/all_gather | solution.py:239
  300.4 54.2 %all-reduce.12.cloned.1.call-done = f32[2,512,1024]{2,1,0:T(8,128)} async-done(((f32[2,512,1024]{2,1,0:T(8,128)}), f32[2,512,1024]{2,1,0:T(8,128)}) %all-reduce.12.cloned.1.call-update) | async-done | bytes 4194320 | tf_op jit(solution)/shard_map/psum | solution.py:53
  370.7 11.8 all-gather.3
  382.6 140.4 %all-reduce.14.cloned.1.call-done = f32[2,512,1024]{2,1,0:T(8,128)} async-done(((f32[2,512,1024]{2,1,0:T(8,128)}), f32[2,512,1024]{2,1,0:T(8,128)}) %all-reduce.14.cloned.1.call-update) | async-done | bytes 4194320 | tf_op jit(solution)/shard_map/psum | solution.py:53
  556.5 153.9 %all-reduce.16.cloned.1.call-done = f32[2,512,1024]{2,1,0:T(8,128)} async-done(((f32[2,512,1024]{2,1,0:T(8,128)}), f32[2,512,1024]{2,1,0:T(8,128)}) %all-reduce.16.cloned.1.call-update) | async-done | bytes 4194320 | tf_op jit(solution)/shard_map/psum | solution.py:53
  742.5 143.0 %all-reduce.18.cloned.1.call-done = f32[2,512,1024]{2,1,0:T(8,128)} async-done(((f32[2,512,1024]{2,1,0:T(8,128)}), f32[2,512,1024]{2,1,0:T(8,128)}) %all-reduce.18.cloned.1.call-update) | async-done | bytes 4194320 | tf_op jit(solution)/shard_map/psum | solution.py:53
  899.3 14.2 fusion.4
  920.7 19.2 %fusion.129 = (f32[2,2,512,1024]{2,3,1,0:T(8,128)}, bf16[2,2,2,512,1024]{3,4,2,1,0:T(8,128)(2,1)S(1)}) fusion(f32[2,2,2,512]{3,2,1,0:T(2,128)S(1)} %get-tuple-element.205, f32[2,2,1024,512,2]{3,2,4,1,0:T(8,128)} %get-tuple-element.206, f32[2,2,2,512]{3,2,1,0:T(2,128)S(1)} %log_add_fusion.1, f32[2,2,512,1024]{2,3,1,0:T(8,128)} %bitcast.308, ...), kind=kLoop, calls=%fused_computation.192 | loop fusion | flops 27262976 | bytes 59801600 | tf_op jit(solution)/shard_map/while/body/eval_jaxpr/reduce_sum | solution.py:99
  1016.0 26.7 %reduce-scatter.50.cloned.1.call-done = bf16[128,704]{1,0:T(8,128)(2,1)} async-done(((bf16[1024,704]{1,0:T(8,128)(2,1)}), bf16[128,704]{1,0:T(8,128)(2,1)}) %reduce-scatter.50.cloned.1.call-update) | async-done | bytes 180240
  1044.5 39.8 %reduce-scatter.54.cloned.1.call-done = bf16[128,704]{1,0:T(8,128)(2,1)} async-done(((bf16[1024,704]{1,0:T(8,128)(2,1)}), bf16[128,704]{1,0:T(8,128)(2,1)}) %reduce-scatter.54.cloned.1.call-update) | async-done | bytes 180240
  1086.2 35.2 %reduce-scatter.44.cloned.1.call-done = bf16[128,256]{1,0:T(8,128)(2,1)} async-done(((bf16[1024,256]{1,0:T(8,128)(2,1)}), bf16[128,256]{1,0:T(8,128)(2,1)}) %reduce-scatter.44.cloned.1.call-update) | async-done | bytes 65552 | tf_op jit(solution)/shard_map/reduce_scatter | solution.py:340
  1122.9 35.7 %reduce-scatter.42.cloned.1.call-done = bf16[128,256]{1,0:T(8,128)(2,1)} async-done(((bf16[1024,256]{1,0:T(8,128)(2,1)}), bf16[128,256]{1,0:T(8,128)(2,1)}) %reduce-scatter.42.cloned.1.call-update) | async-done | bytes 65552 | tf_op jit(solution)/shard_map/reduce_scatter | solution.py:331
  1160.1 35.1 %reduce-scatter.48.cloned.1.call-done = bf16[128,128]{1,0:T(8,128)(2,1)} async-done(((bf16[1024,128]{1,0:T(8,128)(2,1)}), bf16[128,128]{1,0:T(8,128)(2,1)}) %reduce-scatter.48.cloned.1.call-update) | async-done | bytes 32784
  1196.8 35.2 %reduce-scatter.46.cloned.1.call-done = bf16[128,128]{1,0:T(8,128)(2,1)} async-done(((bf16[1024,128]{1,0:T(8,128)(2,1)}), bf16[128,128]{1,0:T(8,128)(2,1)}) %reduce-scatter.46.cloned.1.call-update) | async-done | bytes 32784
  1233.6 10.7 copy.158
  1244.3 32.9 %fusion.93 = bf16[32,4]{1,0:T(8,128)(2,1)S(1)} fusion(f32[4,512,1024]{2,0,1:T(4,128)} %copy.158, s32[512,1024]{1,0:T(8,128)} %compare_select_fusion), kind=kOutput, calls=%fused_computation.149 | convolution fusion | flops 822083712 | bytes 10486016 | tf_op jit(solution)/shard_map/ijb,hij->bh/dot_general | solution.py:360
  1278.7 27.8 %reduce-scatter.34.cloned.1.call-done = bf16[128,256]{1,0:T(8,128)(2,1)} async-done(((bf16[1024,256]{1,0:T(8,128)(2,1)}), bf16[128,256]{1,0:T(8,128)(2,1)}) %reduce-scatter.34.cloned.1.call-update) | async-done | bytes 65552 | tf_op jit(solution)/shard_map/reduce_scatter | solution.py:380
  1308.1 35.3 %reduce-scatter.38.cloned.1.call-done = bf16[128,128]{1,0:T(8,128)(2,1)} async-done(((bf16[1024,128]{1,0:T(8,128)(2,1)}), bf16[128,128]{1,0:T(8,128)(2,1)}) %reduce-scatter.38.cloned.1.call-update) | async-done | bytes 32784 | tf_op jit(solution)/shard_map/reduce_scatter | solution.py:386
  1344.7 35.4 %reduce-scatter.36.cloned.1.call-done = bf16[128,128]{1,0:T(8,128)(2,1)} async-done(((bf16[1024,128]{1,0:T(8,128)(2,1)}), bf16[128,128]{1,0:T(8,128)(2,1)}) %reduce-scatter.36.cloned.1.call-update) | async-done | bytes 32784 | tf_op jit(solution)/shard_map/reduce_scatter | solution.py:383
  1391.9 23.2 %all-reduce.5 = (bf16[1024]{0:T(1024)(128)(2,1)S(1)}, bf16[32,4]{1,0:T(8,128)(2,1)S(1)}, bf16[1024]{0:T(1024)(128)(2,1)S(1)}, bf16[1024]{0:T(1024)(128)(2,1)S(1)}) all-reduce(bf16[1024]{0:T(1024)(128)(2,1)S(1)} %get-tuple-element.181, bf16[32,4]{1,0:T(8,128)(2,1)S(1)} %fusion.93, ...), channel_id=6, replica_groups=mesh['fsdp'=4,'ctx'=2,'tp'=4] {'fsdp','ctx'}, use_global_device_ids=true, to_apply=%region_24.25.clone | all-reduce | flops 3200 | bytes 12800
  (337 shorter events, 297.1 us)
Async XLA Ops:
  8.0 221.2 %copy-start = (bf16[2,256,1024]{2,1,0:T(8,128)(2,1)S(1)}, bf16[2,256,1024]{2,1,0:T(8,128)(2,1)}, u32[]{:S(2)}) copy-start(bf16[2,256,1024]{2,1,0:T(8,128)(2,1)} %param.20) | copy-start | bytes 3145732
  8.0 66.8 %copy-start.14 = (bf16[2,512,1024]{2,1,0:T(8,128)(2,1)S(1)}, bf16[2,512,1024]{2,1,0:T(8,128)(2,1)}, u32[]{:S(2)}) copy-start(bf16[2,512,1024]{2,1,0:T(8,128)(2,1)} %param.19) | copy-start | bytes 6291460
  8.1 33.1 %copy-start.60 = (bf16[128,128]{1,0:T(8,128)(2,1)S(1)}, bf16[128,128]{1,0:T(8,128)(2,1)}, u32[]{:S(2)}) copy-start(bf16[128,128]{1,0:T(8,128)(2,1)} %param.25) | copy-start | bytes 98308
  8.1 49.8 %copy-start.61 = (bf16[128,128]{1,0:T(8,128)(2,1)S(1)}, bf16[128,128]{1,0:T(8,128)(2,1)}, u32[]{:S(2)}) copy-start(bf16[128,128]{1,0:T(8,128)(2,1)} %param.26) | copy-start | bytes 98308
  8.1 346.5 %all-reduce.12.cloned.1.call-start = ((), (), s32[]{:S(2)}) async-start(), calls=%async_computation.15 | async-start | bytes 8388608 | tf_op jit(solution)/shard_map/psum | solution.py:53
  15.9 119.4 %copy-start.56 = (f32[2,512]{1,0:T(2,128)}, f32[2,512]{1,0:T(2,128)S(1)}, u32[]{:S(2)}) copy-start(f32[2,512]{1,0:T(2,128)S(1)} %fusion.120) | copy-start | bytes 12292
  27.4 107.9 %copy-start.58 = (f32[8,1,128]{2,1,0:T(1,128)}, f32[8,1,128]{2,1,0:T(1,128)S(1)}, u32[]{:S(2)}) copy-start(f32[8,1,128]{2,1,0:T(1,128)S(1)} %convert_element_type.466) | copy-start | bytes 12292
  98.4 40.9 %copy-start.64 = (bf16[8,4,4]{2,1,0:T(4,128)(2,1)S(1)}, bf16[8,4,4]{2,1,0:T(4,128)(2,1)}, u32[]{:S(2)}) copy-start(bf16[8,4,4]{2,1,0:T(4,128)(2,1)} %all-gather.1) | copy-start | bytes 772
  200.6 36.9 %copy-start.63 = (bf16[128,128]{1,0:T(8,128)(2,1)S(1)}, bf16[128,128]{1,0:T(8,128)(2,1)}, u32[]{:S(2)}) copy-start(bf16[128,128]{1,0:T(8,128)(2,1)} %param.32) | copy-start | bytes 98308
  200.6 80.0 %copy-start.51 = (bf16[128,256]{1,0:T(8,128)(2,1)S(1)}, bf16[128,256]{1,0:T(8,128)(2,1)}, u32[]{:S(2)}) copy-start(bf16[128,256]{1,0:T(8,128)(2,1)} %param.33) | copy-start | bytes 196612
  200.6 322.3 %all-reduce.14.cloned.1.call-start = ((), (), s32[]{:S(2)}) async-start(), calls=%async_computation.16 | async-start | bytes 8388608 | tf_op jit(solution)/shard_map/psum | solution.py:53
  368.9 161.9 %all-gather.10.cloned.1.call-start = ((), (), s32[]{:S(2)}) async-start(), calls=%async_computation.18 | async-start | bytes 1622016 | tf_op jit(solution)/shard_map/all_gather | solution.py:257
  369.4 166.6 %all-gather.8.cloned.1.call-start = ((), (), s32[]{:S(2)}) async-start(), calls=%async_computation.17 | async-start | bytes 1622016 | tf_op jit(solution)/shard_map/all_gather | solution.py:256
  370.0 171.3 %all-gather.12.cloned.1.call-start = ((), (), s32[]{:S(2)}) async-start(), calls=%async_computation.19 | async-start | bytes 1622016 | tf_op jit(solution)/shard_map/all_gather | solution.py:258
  370.6 339.8 %all-reduce.16.cloned.1.call-start = ((), (), s32[]{:S(2)}) async-start(), calls=%async_computation.20 | async-start | bytes 8388608 | tf_op jit(solution)/shard_map/psum | solution.py:53
  556.3 329.2 %all-reduce.18.cloned.1.call-start = ((), (), s32[]{:S(2)}) async-start(), calls=%async_computation.21 | async-start | bytes 8388608 | tf_op jit(solution)/shard_map/psum | solution.py:53
  731.3 242.1 %reduce-scatter.32.cloned.1.call-start = ((), (), s32[]{:S(2)}) async-start(), calls=%async_computation.25 | async-start | bytes 393216 | tf_op jit(solution)/shard_map/reduce_scatter | solution.py:310
  737.1 238.5 %reduce-scatter.30.cloned.1.call-start = ((), (), s32[]{:S(2)}) async-start(), calls=%async_computation.24 | async-start | bytes 393216 | tf_op jit(solution)/shard_map/reduce_scatter | solution.py:307
  742.2 254.7 %reduce-scatter.28.cloned.1.call-start = ((), (), s32[]{:S(2)}) async-start(), calls=%async_computation.23 | async-start | bytes 786432 | tf_op jit(solution)/shard_map/reduce_scatter | solution.py:354
  920.6 83.0 %reduce-scatter.26.cloned.1.call-start = ((), (), s32[]{:S(2)}) async-start(), calls=%async_computation.22 | async-start | bytes 786432 | tf_op jit(solution)/shard_map/reduce_scatter | solution.py:351
  944.2 70.0 %reduce-scatter.52.cloned.1.call-start = ((), (), s32[]{:S(2)}) async-start(), calls=%async_computation.35 | async-start | bytes 1769472
  951.8 90.9 %reduce-scatter.50.cloned.1.call-start = ((), (), s32[]{:S(2)}) async-start(), calls=%async_computation.34 | async-start | bytes 1769472
  958.8 125.5 %reduce-scatter.54.cloned.1.call-start = ((), (), s32[]{:S(2)}) async-start(), calls=%async_computation.36 | async-start | bytes 1769472
  965.7 155.7 %reduce-scatter.44.cloned.1.call-start = ((), (), s32[]{:S(2)}) async-start(), calls=%async_computation.31 | async-start | bytes 589824 | tf_op jit(solution)/shard_map/reduce_scatter | solution.py:340
  969.0 189.6 %reduce-scatter.42.cloned.1.call-start = ((), (), s32[]{:S(2)}) async-start(), calls=%async_computation.30 | async-start | bytes 589824 | tf_op jit(solution)/shard_map/reduce_scatter | solution.py:331
  973.3 221.9 %reduce-scatter.48.cloned.1.call-start = ((), (), s32[]{:S(2)}) async-start(), calls=%async_computation.33 | async-start | bytes 294912
  975.5 256.5 %reduce-scatter.46.cloned.1.call-start = ((), (), s32[]{:S(2)}) async-start(), calls=%async_computation.32 | async-start | bytes 294912
  977.7 299.5 %reduce-scatter.40.cloned.1.call-start = ((), (), s32[]{:S(2)}) async-start(), calls=%async_computation.29 | async-start | bytes 589824 | tf_op jit(solution)/shard_map/reduce_scatter | solution.py:389
  984.8 321.8 %reduce-scatter.34.cloned.1.call-start = ((), (), s32[]{:S(2)}) async-start(), calls=%async_computation.26 | async-start | bytes 589824 | tf_op jit(solution)/shard_map/reduce_scatter | solution.py:380
  992.7 350.6 %reduce-scatter.38.cloned.1.call-start = ((), (), s32[]{:S(2)}) async-start(), calls=%async_computation.28 | async-start | bytes 294912 | tf_op jit(solution)/shard_map/reduce_scatter | solution.py:386
  999.6 380.5 %reduce-scatter.36.cloned.1.call-start = ((), (), s32[]{:S(2)}) async-start(), calls=%async_computation.27 | async-start | bytes 294912 | tf_op jit(solution)/shard_map/reduce_scatter | solution.py:383
  1006.4 375.1 %all-reduce.20.cloned.1.call-start = ((), (), s32[]{:S(2)}) async-start(), calls=%async_computation.37 | async-start | bytes 20971520 | tf_op jit(solution)/shard_map/psum | solution.py:53
  (73 other events, 480.6 us)
Sparse Core Ops, SparseCore 0:
  200.8 153.7 all-reduce.11
  369.0 153.9 all-reduce.13
  556.4 153.9 all-reduce.15
  731.5 153.9 all-reduce.17
  1011.7 357.4 all-reduce.19
Sparse Core Ops, SparseCore 1:
  371.2 25.8 all-gather.9
  398.8 25.0 all-gather.7
  425.7 25.0 all-gather.11
  737.2 11.7 reduce-scatter.31
  751.7 11.7 reduce-scatter.29
  920.7 14.5 reduce-scatter.27
  944.2 14.6 reduce-scatter.25
  962.0 39.1 reduce-scatter.51
  1004.4 38.2 reduce-scatter.49
  1046.0 38.2 reduce-scatter.53
  1087.2 34.1 reduce-scatter.43
  1124.5 34.1 reduce-scatter.41
  1161.5 33.7 reduce-scatter.47
  1198.3 33.7 reduce-scatter.45
  1235.1 34.2 reduce-scatter.39
  1272.4 34.1 reduce-scatter.33
  1309.6 33.7 reduce-scatter.37
  1346.4 33.7 reduce-scatter.35
where the time goes:
time: 1440 us; the launch traced here: 1430 us
  waiting for transfers between devices  800 us (56%)
  blocking collectives  244 us (17%)
  matrix products  196 us (14%)
  other arithmetic  95.6 us (7%)
  local copies, waits for them, and re-layouts  72.2 us (5%)
  between operations  18 us (1%)
    psum x5, waiting for transfers between devices, reduce_rows(): return lax.psum(partial_sum, 'tp')  491 us
    unnamed x28, waiting for transfers between devices  139 us
    unnamed x180, local copies, waits for them, and re-layouts  42.1 us
    reduce_scatter x1, waiting for transfers between devices, shards(): lax.psum_scatter(grad_cross_query.astype(jnp.bfloat16), ('fsdp', 'ctx'),...  35.7 us
    reduce_scatter x1, waiting for transfers between devices, shards(): lax.psum_scatter(grad_self_key.astype(jnp.bfloat16), ('fsdp', 'ctx'), sca...  35.4 us
    reduce_scatter x1, waiting for transfers between devices, shards(): lax.psum_scatter(grad_self_value.astype(jnp.bfloat16), ('fsdp', 'ctx'), s...  35.3 us
    reduce_scatter x1, waiting for transfers between devices, shards(): lax.psum_scatter(grad_cross_out.astype(jnp.bfloat16), ('fsdp', 'ctx'), sc...  35.2 us
    dot_general x1, matrix products, shards(): jnp.einsum('ijb,hij->bh', one_hot, bias_total.reshape(heads_local, row_to...  32.9 us
  transfers between devices with their start and end apart: 23, of which 13 were waited for; matrix products, arithmetic and copies ran while one was open for 15% of the time, Pallas kernels for 0%

commit v1 on v0

--- a/solution.py
+++ b/solution.py
@@ -1,8 +1,11 @@
+import functools
 import math
 
 import jax
 import jax.numpy as jnp
 from jax import lax
+from jax.experimental import pallas as pl
+from jax.experimental.pallas import tpu as pltpu
 from jax.sharding import PartitionSpec as P
 
 HEAD_SIZE = 64
@@ -416,9 +419,948 @@
     )
 
 
+MESH = pl.DeviceIdType.MESH
+DEPTH = 4
+LINKS = {("x", 0): 0, ("y", 0): 1, ("z", 1): 2, ("z", -1): 3, ("c", 0): 4}
+SIZES = {"x": 2, "y": 2, "z": DEPTH}
+
+
+class Place:
+    def __init__(self):
+        row = lax.axis_index("fsdp")
+        self.y = lax.axis_index("ctx")
+        self.z = lax.axis_index("tp")
+        self.x = lax.div(row, 2)
+        self.c = lax.rem(row, 2)
+
+    def link(self, axis, d):
+        x, y, z, c = self.x, self.y, self.z, self.c
+        if axis == "x":
+            x = 1 - x
+        elif axis == "y":
+            y = 1 - y
+        elif axis == "z":
+            z = z + d
+        else:
+            c = 1 - c
+        return (x * 2 + c, y, z)
+
+    def has(self, link):
+        if link == ("z", 1):
+            return self.z < DEPTH - 1
+        if link == ("z", -1):
+            return self.z > 0
+        return None
+
+    def source(self, src):
+        x = 1 - self.x if src.get("x") else self.x
+        y = 1 - self.y if src.get("y") else self.y
+        return x, y, self.z + src.get("z", 0)
+
+    def exists(self, src):
+        off = src.get("z", 0)
+        if off < 0:
+            return self.z >= -off
+        if off > 0:
+            return self.z < DEPTH - off
+        return None
+
+
+def arrivals(order):
+    events = []
+    for k, axis in enumerate(order):
+        sources = [{}]
+        for a in order[:k]:
+            choice = (0, -1, 1, -2, 2, -3, 3) if a == "z" else (0, 1)
+            sources = [dict(b, **{a: o}) for o in choice for b in sources]
+        for o in (-1, 1, -2, 2, -3, 3) if axis == "z" else (1,):
+            for b in sources:
+                src = dict(b, **{axis: o})
+                d = 0 if axis != "z" else (1 if o < 0 else -1)
+                events.append((k, sum(abs(v) for v in src.values()), src, d))
+    return events
+
+
+def onward(order, k, d):
+    out = [("z", d)] if k >= 0 and order[k] == "z" else []
+    for a in order[k + 1 :]:
+        out += [("z", 1), ("z", -1)] if a == "z" else [(a, 0)]
+    return out
+
+
+def when(cond, action):
+    if cond is None:
+        action()
+    else:
+        pl.when(cond)(action)
+
+
+def number(x, y, z):
+    return (x * 2 + y) * DEPTH + z
+
+
+def greet(place):
+    barrier = pltpu.get_barrier_semaphore()
+
+    def signal(link):
+        pl.semaphore_signal(
+            barrier, inc=1, device_id=place.link(*link), device_id_type=MESH
+        )
+
+    for link in LINKS:
+        when(place.has(link), functools.partial(signal, link))
+    ends = jnp.where(place.z < DEPTH - 1, 1, 0) + jnp.where(place.z > 0, 1, 0)
+    pl.semaphore_wait(barrier, ends + 3)
+
+
+def remote(src, dst, send, recv, device):
+    return pltpu.make_async_remote_copy(
+        src_ref=src, dst_ref=dst, send_sem=send, recv_sem=recv,
+        device_id=device, device_id_type=MESH,
+    )
+
+
+def gather_kernel(orders, rows, count, *refs):
+    ins, outs = refs[:count], refs[count : 2 * count]
+    send, recv, core_recv, local_sem = refs[2 * count :]
+    place = Place()
+    greet(place)
+    me = (place.x, place.y, place.z)
+
+    def slot(j, xyz, c):
+        x, y, z = xyz
+        if len(orders[j]) == 1:
+            return outs[j].at[y if orders[j] == "y" else z]
+        at = ((x * 2 + c) * 2 + y) * rows[j]
+        return outs[j].at[z, pl.ds(pl.multiple_of(at, rows[j]), rows[j]), :]
+
+    def copy(j, xyz, link, own):
+        here = slot(j, xyz, place.c)
+        arrived = core_recv if link[0] == "c" else recv
+        i = number(*xyz)
+        return remote(
+            ins[j] if own else here, here, send.at[j, i, LINKS[link]], arrived.at[j, i],
+            place.link(*link),
+        )
+
+    def routes(j, k, d):
+        links = onward(orders[j], k, d)
+        return links + [("c", 0)] if len(orders[j]) == 3 else links
+
+    for stage in range(2):
+        for j in range(count):
+            for link in routes(j, -1, 0):
+                if (link[0] == "c") == (stage == 1):
+                    when(place.has(link), copy(j, me, link, True).start)
+    local = []
+    for j in range(count):
+        local.append(pltpu.make_async_copy(ins[j], slot(j, me, place.c), local_sem.at[j]))
+        local[-1].start()
+    events = [
+        (k, hops, j, src, d)
+        for j in range(count)
+        for k, hops, src, d in arrivals(orders[j])
+    ]
+    events.sort(key=lambda e: (e[0], e[1]))
+    for k, hops, j, src, d in events:
+        xyz = place.source(src)
+
+        def step():
+            copy(j, xyz, ("x", 0), True).wait_recv()
+            for link in routes(j, k, d):
+                when(place.has(link), copy(j, xyz, link, False).start)
+
+        when(place.exists(src), step)
+    for c in local:
+        c.wait()
+    for j in range(count):
+        for link in routes(j, -1, 0):
+            when(place.has(link), copy(j, me, link, True).wait_send)
+    for k, hops, j, src, d in events:
+        xyz = place.source(src)
+
+        def finish():
+            for link in routes(j, k, d):
+                when(place.has(link), copy(j, xyz, link, False).wait_send)
+
+        when(place.exists(src), finish)
+    for j in range(count):
+        if len(orders[j]) == 3:
+
+            def from_core(i, carry):
+                xyz = (lax.div(i, 2 * DEPTH), lax.rem(lax.div(i, DEPTH), 2), lax.rem(i, DEPTH))
+                there = slot(j, xyz, 1 - place.c)
+                remote(
+                    ins[j], there, send.at[j, i, 4], core_recv.at[j, i], place.link("c", 0)
+                ).wait_recv()
+                return carry
+
+            lax.fori_loop(0, 4 * DEPTH, from_core, 0)
+
+
+def gather(arrays, orders, number_id, name):
+    count = len(arrays)
+    rows = [a.shape[0] for a in arrays]
+    outs = [
+        jax.ShapeDtypeStruct(
+            (SIZES[o],) + a.shape if len(o) == 1 else (DEPTH, 8 * a.shape[0], a.shape[1]),
+            a.dtype,
+        )
+        for a, o in zip(arrays, orders)
+    ]
+    dma = pltpu.SemaphoreType.DMA
+    return pl.pallas_call(
+        functools.partial(gather_kernel, orders, rows, count),
+        out_shape=outs,
+        in_specs=[pl.BlockSpec(memory_space=pltpu.VMEM)] * count,
+        out_specs=[pl.BlockSpec(memory_space=pl.ANY)] * count,
+        scratch_shapes=[
+            dma((count, 4 * DEPTH, 5)), dma((count, 4 * DEPTH)), dma((count, 4 * DEPTH)),
+            dma((count,)),
+        ],
+        compiler_params=pltpu.CompilerParams(collective_id=number_id, has_side_effects=True),
+        name=name,
+    )(*arrays)
+
+
+def child_slots(order):
+    starts, total, before = [], 0, 1
+    for a in order:
+        starts.append(total)
+        total += before * (DEPTH + 1 if a == "z" else 1)
+        before *= SIZES[a]
+    return starts, total
+
+
+def child_slot(order, starts, m, xyz, tail):
+    at = 0
+    for a in order[:m]:
+        at = at * SIZES[a] + xyz["xyz".index(a)]
+    if order[m] == "z":
+        at = at * (DEPTH + 1) + tail
+    return starts[m] + at
+
+
+def scatter_kernel(orders, rows, count, *refs):
+    ins, outs = refs[:count], refs[count : 2 * count]
+    sums, gifts, kids = (refs[i * count : (i + 1) * count] for i in (2, 3, 4))
+    load_sem, give_sem, gift_sem, up_sem, kid_sem = refs[5 * count :]
+    place = Place()
+    greet(place)
+    me = (place.x, place.y, place.z)
+    plans = [child_slots(o) for o in orders]
+    partner = place.link("c", 0)
+
+    def slot(j, xyz, c):
+        x, y, z = xyz
+        at = ((x * 2 + c) * 2 + y) * rows[j]
+        return ins[j].at[z, pl.ds(pl.multiple_of(at, rows[j]), rows[j]), :]
+
+    def load(j, xyz):
+        i = number(*xyz)
+        return pltpu.make_async_copy(slot(j, xyz, place.c), sums[j].at[i], load_sem.at[j, i])
+
+    def give(j, xyz):
+        i = number(*xyz)
+        return remote(
+            slot(j, xyz, 1 - place.c), gifts[j].at[i], give_sem.at[j, i], gift_sem.at[j, i],
+            partner,
+        )
+
+    def up(j, xyz, k, d):
+        axis = orders[j][k]
+        tail = xyz[2]
+        if axis == "z" and d < 0:
+            tail = jnp.where(xyz[2] == place.z - d, DEPTH, xyz[2])
+        at = child_slot(orders[j], plans[j][0], k, xyz, tail)
+        i = number(*xyz)
+        return remote(
+            sums[j].at[i], kids[j].at[at], up_sem.at[j, i], kid_sem.at[j, at],
+            place.link(axis, -d),
+        )
+
+    def kid(j, m, xyz, tail):
+        at = child_slot(orders[j], plans[j][0], m, xyz, tail)
+        ref = kids[j].at[at]
+        remote(ref, ref, up_sem.at[j, 0], kid_sem.at[j, at], partner).wait_recv()
+        return ref
+
+    def add(j, i, terms, out=None):
+        total = sums[j].at[i]
+        step = min(rows[j], 16)
+
+        def body(q, carry):
+            at = pl.ds(pl.multiple_of(q * step, step), step)
+            value = total[at, :].astype(jnp.float32)
+            for term in terms:
+                value = value + term[at, :].astype(jnp.float32)
+            if out is None:
+                total[at, :] = value.astype(total.dtype)
+            else:
+                out[at, :] = value.astype(out.dtype)
+            return carry
+
+        lax.fori_loop(0, rows[j] // step, body, 0)
+
+    def collect(j, xyz, k, d, out=None):
+        i = number(*xyz)
+        order = orders[j]
+        load(j, xyz).wait()
+        give(j, xyz).wait_recv()
+        always, sometimes = [], []
+        if k >= 0 and order[k] == "z":
+            sometimes.append((k, ("z", d), xyz[2]))
+        for m in range(k + 1, len(order)):
+            if order[m] == "z":
+                sometimes += [(m, ("z", 1), xyz[2]), (m, ("z", -1), DEPTH)]
+            else:
+                always.append(m)
+        for m, link, tail in sometimes:
+
+            def more():
+                add(j, i, [kid(j, m, xyz, tail)])
+
+            when(place.has(link), more)
+        add(j, i, [gifts[j].at[i]] + [kid(j, m, xyz, 0) for m in always], out)
+
+    events = [
+        (k, hops, j, src, d)
+        for j in range(count)
+        for k, hops, src, d in arrivals(orders[j])
+    ]
+    events.sort(key=lambda e: (-e[0], -e[1]))
+    for k, hops, j, src, d in events:
+        xyz = place.source(src)
+
+        def begin():
+            give(j, xyz).start()
+            load(j, xyz).start()
+
+        when(place.exists(src), begin)
+    for j in range(count):
+        give(j, me).start()
+        load(j, me).start()
+    for k, hops, j, src, d in events:
+        xyz = place.source(src)
+
+        def step():
+            collect(j, xyz, k, d)
+            up(j, xyz, k, d).start()
+
+        when(place.exists(src), step)
+    for j in range(count):
+        collect(j, me, -1, 0, outs[j])
+    for k, hops, j, src, d in events:
+        xyz = place.source(src)
+
+        def finish():
+            up(j, xyz, k, d).wait_send()
+            give(j, xyz).wait_send()
+
+        when(place.exists(src), finish)
+    for j in range(count):
+        give(j, me).wait_send()
+
+
+def scatter(arrays, orders, number_id, name):
+    count = len(arrays)
+    rows = [a.shape[1] // 8 for a in arrays]
+    plans = [child_slots(o)[1] for o in orders]
+    dma = pltpu.SemaphoreType.DMA
+
+    def room(slots):
+        return [
+            pltpu.VMEM((n, r, a.shape[2]), a.dtype) for n, r, a in zip(slots, rows, arrays)
+        ]
+
+    full = [4 * DEPTH] * count
+    return pl.pallas_call(
+        functools.partial(scatter_kernel, orders, rows, count),
+        out_shape=[
+            jax.ShapeDtypeStruct((r, a.shape[2]), jnp.float32) for r, a in zip(rows, arrays)
+        ],
+        in_specs=[pl.BlockSpec(memory_space=pl.ANY)] * count,
+        out_specs=[pl.BlockSpec(memory_space=pltpu.VMEM)] * count,
+        scratch_shapes=room(full) + room(full) + room(plans)
+        + [dma((count, 4 * DEPTH))] * 4 + [dma((count, max(plans)))],
+        compiler_params=pltpu.CompilerParams(
+            collective_id=number_id, has_side_effects=True, vmem_limit_bytes=67043328
+        ),
+        name=name,
+    )(*arrays)
+
+
+WIDTH = 1024
+QROWS = 256
+KEYS = 1024
+ENC_ROWS = 512
+SPAN = 1280
+CHUNK = 128
+VMEM_MOST = 64000000
+ROWS_OF = (((0,), (0,)), ((), ()))
+LAST = (((1,), (1,)), ((), ()))
+PLAIN = (((1,), (0,)), ((), ()))
+
+
+def mm(a, b, dims=PLAIN):
+    return lax.dot_general(a, b, dims, preferred_element_type=jnp.float32)
+
+
+def norm_rows(v, gain):
+    return v * lax.rsqrt(jnp.mean(v * v, axis=-1, keepdims=True) + EPSILON) * gain
+
+
+def norm_back(v, gain, e):
+    r = lax.rsqrt(jnp.mean(v * v, axis=-1, keepdims=True) + EPSILON)
+    ev = e * v
+    gain_grad = jnp.sum(ev * r, axis=0, keepdims=True)
+    back = r * gain * e - v * (r * r * r) * jnp.mean(ev * gain, axis=-1, keepdims=True)
+    return back, gain_grad
+
+
+def head_rows(cols, a):
+    return jnp.concatenate(
+        [cols[:, a * 128 : a * 128 + 64], cols[:, a * 128 + 64 : a * 128 + 128]], axis=0
+    )
+
+
+def attend(q, kv, p_ref, s_ref, ot_ref, keys, add_bias):
+    for a in range(2):
+        q2 = head_rows(q, a)
+        k = kv[:, a * 64 : a * 64 + 64]
+        v = kv[:, 128 + a * 64 : 192 + a * 64]
+        if add_bias is not None:
+            add_bias(a, None, None)
+        peak = None
+        for c in range(keys // CHUNK):
+            rows = pl.ds(c * CHUNK, CHUNK)
+            s = mm(k[c * CHUNK : (c + 1) * CHUNK], q2, LAST)
+            if add_bias is not None:
+                s = add_bias(a, c, s)
+            s_ref[rows, :] = s
+            top = jnp.max(s, axis=0, keepdims=True)
+            peak = top if peak is None else jnp.maximum(peak, top)
+        total = jnp.zeros_like(peak)
+        for c in range(keys // CHUNK):
+            rows = pl.ds(c * CHUNK, CHUNK)
+            e = jnp.exp(s_ref[rows, :] - peak)
+            s_ref[rows, :] = e
+            total = total + jnp.sum(e, axis=0, keepdims=True)
+        inverse = 1.0 / total
+        for c in range(keys // CHUNK):
+            rows = pl.ds(c * CHUNK, CHUNK)
+            p_ref[0, a, rows, :] = (s_ref[rows, :] * inverse).astype(jnp.bfloat16)
+        ot = mm(v, p_ref[0, a], ROWS_OF)
+        ot_ref[a * 128 : a * 128 + 64, :] = ot[:, :QROWS]
+        ot_ref[a * 128 + 64 : a * 128 + 128, :] = ot[:, QROWS:]
+    return jnp.transpose(ot_ref[...]).astype(jnp.bfloat16)
+
+
+def attend_back(q, kv, p_ref, do, dkv_ref, d_ref, ds_ref, qt_ref, keys, take_bias):
+    for a in range(2):
+        q2 = head_rows(q, a)
+        do2 = head_rows(do, a)
+        k = kv[:, a * 64 : a * 64 + 64]
+        v = kv[:, 128 + a * 64 : 192 + a * 64]
+        total = jnp.zeros((1, 2 * QROWS), jnp.float32)
+        for c in range(keys // CHUNK):
+            rows = pl.ds(c * CHUNK, CHUNK)
+            dp = mm(v[c * CHUNK : (c + 1) * CHUNK], do2, LAST)
+            d_ref[rows, :] = dp
+            total = total + jnp.sum(
+                dp * p_ref[0, a, rows, :].astype(jnp.float32), axis=0, keepdims=True
+            )
+        for c in range(keys // CHUNK):
+            rows = pl.ds(c * CHUNK, CHUNK)
+            ds = p_ref[0, a, rows, :].astype(jnp.float32) * (d_ref[rows, :] - total)
+            if take_bias is not None:
+                take_bias(a, c, ds)
+            ds_ref[rows, :] = ds.astype(jnp.bfloat16)
+        if take_bias is not None:
+            take_bias(a, None, None)
+        dkv_ref[0, :, a * 64 : a * 64 + 64] = mm(ds_ref[...], q2).astype(jnp.bfloat16)
+        dkv_ref[0, :, 128 + a * 64 : 192 + a * 64] = mm(p_ref[0, a], do2).astype(jnp.bfloat16)
+        qt = mm(k, ds_ref[...], ROWS_OF)
+        qt_ref[a * 128 : a * 128 + 64, :] = qt[:, :QROWS]
+        qt_ref[a * 128 + 64 : a * 128 + 128, :] = qt[:, QROWS:]
+    return jnp.transpose(qt_ref[...]).astype(jnp.bfloat16)
+
+
+def self_forward_kernel(
+    info, table, x_ref, gain_ref, w_ref, wkv_ref, bucket_ref,
+    x2_ref, h_ref, q_ref, kv_ref, p_ref, o_ref,
+    h1_ref, s_ref, strip_ref, ot_ref,
+):
+    first = pl.multiple_of(info[0], QROWS)
+    length = info[1]
+
+    @pl.when(pl.program_id(0) == 0)
+    def _():
+        for c in range(KEYS // QROWS):
+            rows = pl.ds(c * QROWS, QROWS)
+            h1_ref[rows, :] = norm_rows(
+                x_ref[rows, :].astype(jnp.float32), gain_ref[...]
+            ).astype(jnp.bfloat16)
+        x2_ref[...] = x_ref[pl.ds(first, QROWS), :].astype(jnp.float32)
+        h_ref[...] = h1_ref[pl.ds(first, QROWS), :]
+
+    kv = mm(h1_ref[...], wkv_ref[0]).astype(jnp.bfloat16)
+    kv_ref[0] = kv
+    q = mm(h1_ref[pl.ds(first, QROWS), :], w_ref[0, :, :QROWS]).astype(jnp.bfloat16)
+    q_ref[0] = q
+    lane = lax.broadcasted_iota(jnp.int32, (1, 2 * QROWS), 1)
+    lane = jnp.where(lane < QROWS, lane, lane - QROWS)
+    last_key = jnp.minimum(lane + first, length - 1)
+
+    def add_bias(a, c, s):
+        if c is None:
+            for b in range(2):
+                head = pl.program_id(0) * 4 + 2 * a + b
+                bucket = bucket_ref[...]
+                near = jnp.full((8, SPAN), table[BUCKETS - 1, head], jnp.float32)
+                for i in range(BUCKETS - 1):
+                    near = jnp.where(bucket == i, table[i, head], near)
+                for g in range(16):
+                    shift = (SPAN - (120 - 8 * g)) % SPAN
+                    strip_ref[b, 8 * g : 8 * g + 8, :] = (
+                        pltpu.roll(near, shift, 1) if shift else near
+                    )
+            return None
+        cols = pl.ds(CHUNK * (7 - c), QROWS)
+        bias = jnp.concatenate([strip_ref[0, :, cols], strip_ref[1, :, cols]], axis=1)
+        key = lax.broadcasted_iota(jnp.int32, s.shape, 0) + c * CHUNK
+        return jnp.where(key <= last_key, s + bias, MASKED)
+
+    o = attend(q, kv, p_ref, s_ref, ot_ref, KEYS, add_bias)
+    o_ref[0] = o
+    x2_ref[...] += mm(o, w_ref[0, :, QROWS:], LAST)
+
+
+def cross_forward_kernel(
+    x2_ref, enc_ref, gain_ref, w_ref, wkv_ref,
+    x3_ref, h_ref, q_ref, kv_ref, p_ref, o_ref,
+    s_ref, ot_ref,
+):
+    @pl.when(pl.program_id(0) == 0)
+    def _():
+        x3_ref[...] = x2_ref[...]
+        h_ref[...] = norm_rows(x2_ref[...], gain_ref[...]).astype(jnp.bfloat16)
+
+    kv = mm(enc_ref[...], wkv_ref[0]).astype(jnp.bfloat16)
+    kv_ref[0] = kv
+    q = mm(h_ref[...], w_ref[0, :, :QROWS]).astype(jnp.bfloat16)
+    q_ref[0] = q
+    o = attend(q, kv, p_ref, s_ref, ot_ref, ENC_ROWS, None)
+    o_ref[0] = o
+    x3_ref[...] += mm(o, w_ref[0, :, QROWS:], LAST)
+
+
+def feed_kernel(
+    info, x3_ref, cot_ref, gain_ref, wg_ref, wu_ref, wo_ref,
+    out_ref, g3_ref, gg_ref, gu_ref, go_ref, gn_ref,
+    h_ref, ht_ref, g_ref, gt_ref, y_ref, dh_ref,
+):
+    step = pl.program_id(0)
+
+    @pl.when(step == 0)
+    def _():
+        h = norm_rows(x3_ref[...], gain_ref[...]).astype(jnp.bfloat16)
+        h_ref[...] = h
+        ht_ref[...] = jnp.transpose(h)
+        row = lax.broadcasted_iota(jnp.int32, (QROWS, 1), 0) + info[0]
+        g4 = jnp.where(row < info[1], cot_ref[...].astype(jnp.float32), 0.0)
+        g = g4.astype(jnp.bfloat16)
+        g_ref[...] = g
+        gt_ref[...] = jnp.transpose(g)
+        y_ref[...] = x3_ref[...]
+        dh_ref[...] = jnp.zeros_like(dh_ref)
+
+    gate = mm(h_ref[...], wg_ref[0])
+    up = mm(h_ref[...], wu_ref[0])
+    root = math.sqrt(2.0 / math.pi)
+    square = gate * gate
+    th = jnp.tanh(root * (gate + 0.044715 * gate * square))
+    half = 0.5 * (1.0 + th)
+    gelu = gate * half
+    slope = half + 0.5 * gate * (1.0 - th * th) * (root * (1.0 + 3 * 0.044715 * square))
+    hidden = (gelu * up).astype(jnp.bfloat16)
+    y_ref[...] += mm(hidden, wo_ref[0], LAST)
+    go_ref[0] = mm(gt_ref[...], hidden).astype(jnp.bfloat16)
+    dhid = mm(g_ref[...], wo_ref[0])
+    dup = (dhid * gelu).astype(jnp.bfloat16)
+    dgate = (dhid * up * slope).astype(jnp.bfloat16)
+    gg_ref[0] = mm(ht_ref[...], dgate).astype(jnp.bfloat16)
+    gu_ref[0] = mm(ht_ref[...], dup).astype(jnp.bfloat16)
+    dh_ref[...] += mm(dgate, wg_ref[0], LAST) + mm(dup, wu_ref[0], LAST)
+
+    @pl.when(step == pl.num_programs(0) - 1)
+    def _():
+        out_ref[...] = y_ref[...].astype(jnp.bfloat16)
+        back, gain_grad = norm_back(x3_ref[...], gain_ref[...], dh_ref[...])
+        g3_ref[...] = g_ref[...].astype(jnp.float32) + back
+        gn_ref[...] = gain_grad
+
+
+def cross_backward_kernel(
+    g3_ref, x2_ref, h_ref, gain_ref, w_ref, q_ref, kv_ref, p_ref, o_ref,
+    g2_ref, dkv_ref, gw_ref, gn_ref,
+    g_ref, gt_ref, ht_ref, dh_ref, d_ref, ds_ref, qt_ref,
+):
+    step = pl.program_id(0)
+
+    @pl.when(step == 0)
+    def _():
+        g = g3_ref[...].astype(jnp.bfloat16)
+        g_ref[...] = g
+        gt_ref[...] = jnp.transpose(g)
+        ht_ref[...] = jnp.transpose(h_ref[...])
+        dh_ref[...] = jnp.zeros_like(dh_ref)
+
+    do = mm(g_ref[...], w_ref[0, :, QROWS:]).astype(jnp.bfloat16)
+    gw_ref[0, :, QROWS:] = mm(gt_ref[...], o_ref[0]).astype(jnp.bfloat16)
+    dq = attend_back(
+        q_ref[0], kv_ref[0], p_ref, do, dkv_ref, d_ref, ds_ref, qt_ref, ENC_ROWS, None
+    )
+    gw_ref[0, :, :QROWS] = mm(ht_ref[...], dq).astype(jnp.bfloat16)
+    dh_ref[...] += mm(dq, w_ref[0, :, :QROWS], LAST)
+
+    @pl.when(step == pl.num_programs(0) - 1)
+    def _():
+        back, gain_grad = norm_back(x2_ref[...], gain_ref[...], dh_ref[...])
+        g2_ref[...] = g3_ref[...] + back
+        gn_ref[...] = gain_grad
+
+
+def self_backward_kernel(
+    g2_ref, h_ref, w_ref, q_ref, kv_ref, p_ref, o_ref,
+    dh_ref, dkv_ref, gw_ref, near_ref,
+    g_ref, gt_ref, ht_ref, d_ref, ds_ref, qt_ref, strip_ref,
+):
+    @pl.when(pl.program_id(0) == 0)
+    def _():
+        g = g2_ref[...].astype(jnp.bfloat16)
+        g_ref[...] = g
+        gt_ref[...] = jnp.transpose(g)
+        ht_ref[...] = jnp.transpose(h_ref[...])
+        dh_ref[...] = jnp.zeros_like(dh_ref)
+
+    def take_bias(a, c, ds):
+        if c is None:
+            for b in range(2):
+                total = jnp.zeros((8, SPAN), jnp.float32)
+                for g in range(16):
+                    part = strip_ref[b, 8 * g : 8 * g + 8, :]
+                    shift = 120 - 8 * g
+                    total = total + (pltpu.roll(part, shift, 1) if shift else part)
+                near_ref[0, 2 * a + b] = total
+            return
+        if c == 0:
+            strip_ref[...] = jnp.zeros_like(strip_ref)
+        cols = pl.ds(CHUNK * (7 - c), QROWS)
+        strip_ref[0, :, cols] += ds[:, :QROWS]
+        strip_ref[1, :, cols] += ds[:, QROWS:]
+
+    do = mm(g_ref[...], w_ref[0, :, QROWS:]).astype(jnp.bfloat16)
+    gw_ref[0, :, QROWS:] = mm(gt_ref[...], o_ref[0]).astype(jnp.bfloat16)
+    dq = attend_back(
+        q_ref[0], kv_ref[0], p_ref, do, dkv_ref, d_ref, ds_ref, qt_ref, KEYS, take_bias
+    )
+    gw_ref[0, :, :QROWS] = mm(ht_ref[...], dq).astype(jnp.bfloat16)
+    dh_ref[...] += mm(dq, w_ref[0, :, :QROWS], LAST)
+
+
+def last_kernel(
+    dh_part_ref, dkv_ref, x_ref, h_ref, gain_ref, g2_ref, ws_ref, wc_ref, dkvc_ref, enc_ref,
+    gx_ref, genc_ref, gw_ref, gn_ref,
+    ht_ref, et_ref, dh_ref, de_ref,
+):
+    step = pl.program_id(0)
+
+    @pl.when(step == 0)
+    def _():
+        ht_ref[...] = jnp.transpose(h_ref[...])
+        et_ref[...] = jnp.transpose(enc_ref[...])
+        dh_ref[...] = dh_part_ref[...]
+        de_ref[...] = jnp.zeros_like(de_ref)
+
+    dkv = dkv_ref[0]
+    dkvc = dkvc_ref[0]
+    gw_ref[0, :, :QROWS] = mm(ht_ref[...], dkv).astype(jnp.bfloat16)
+    gw_ref[0, :, QROWS:] = mm(et_ref[...], dkvc).astype(jnp.bfloat16)
+    dh_ref[...] += mm(dkv, ws_ref[0], LAST)
+    de_ref[...] += mm(dkvc, wc_ref[0], LAST)
+
+    @pl.when(step == pl.num_programs(0) - 1)
+    def _():
+        back, gain_grad = norm_back(
+            x_ref[...].astype(jnp.float32), gain_ref[...], dh_ref[...]
+        )
+        gx_ref[...] = (g2_ref[...] + back).astype(jnp.bfloat16)
+        genc_ref[...] = de_ref[...].astype(jnp.bfloat16)
+        gn_ref[...] = gain_grad
+
+
+def whole(shape):
+    zeros = (0,) * len(shape)
+    return pl.BlockSpec(shape, lambda t: zeros)
+
+
+def part(shape, column=0):
+    tail = (0,) * (len(shape) - 2)
+    return pl.BlockSpec(shape, lambda t: (t,) + tail + (column,))
+
+
+SCALARS = pl.BlockSpec(memory_space=pltpu.SMEM)
+F32 = jnp.float32
+LOW = jnp.bfloat16
+
+
+def run_heads(kernel, name, ins, specs, outs, out_specs, scratch, flops, steps=4):
+    moved = sum(math.prod(a.shape) * a.dtype.itemsize for a in list(ins) + list(outs))
+    return pl.pallas_call(
+        kernel,
+        grid=(steps,),
+        in_specs=specs,
+        out_specs=out_specs,
+        out_shape=outs,
+        scratch_shapes=scratch,
+        compiler_params=pltpu.CompilerParams(
+            dimension_semantics=("arbitrary",), vmem_limit_bytes=VMEM_MOST
+        ),
+        cost_estimate=pl.CostEstimate(flops=flops, bytes_accessed=moved, transcendentals=0),
+        name=name,
+    )(*ins)
+
+
+def shape_of(shape, dtype):
+    return jax.ShapeDtypeStruct(shape, dtype)
+
+
+def self_forward(info, x, gain, w1, w3, table, bucket):
+    return run_heads(
+        self_forward_kernel, "self_forward",
+        (info, table, x, gain, w1, w3, bucket),
+        [SCALARS, SCALARS, whole((KEYS, WIDTH)), whole((1, WIDTH)), part((1, WIDTH, 512)),
+         part((1, WIDTH, 256)), whole((8, SPAN))],
+        [shape_of((QROWS, WIDTH), F32), shape_of((QROWS, WIDTH), LOW),
+         shape_of((4, QROWS, 256), LOW), shape_of((4, KEYS, 256), LOW),
+         shape_of((4, 2, KEYS, 512), LOW), shape_of((4, QROWS, 256), LOW)],
+        [whole((QROWS, WIDTH)), whole((QROWS, WIDTH)), part((1, QROWS, 256)),
+         part((1, KEYS, 256)), part((1, 2, KEYS, 512)), part((1, QROWS, 256))],
+        [pltpu.VMEM((KEYS, WIDTH), LOW), pltpu.VMEM((KEYS, 512), F32),
+         pltpu.VMEM((2, CHUNK, SPAN), F32), pltpu.VMEM((256, QROWS), F32)],
+        5 * 10**9,
+    )
+
+
+def cross_forward(x2, enc, gain, w2, w3):
+    return run_heads(
+        cross_forward_kernel, "cross_forward",
+        (x2, enc, gain, w2, w3),
+        [whole((QROWS, WIDTH)), whole((ENC_ROWS, WIDTH)), whole((1, WIDTH)),
+         part((1, WIDTH, 512)), part((1, WIDTH, 256), 1)],
+        [shape_of((QROWS, WIDTH), F32), shape_of((QROWS, WIDTH), LOW),
+         shape_of((4, QROWS, 256), LOW), shape_of((4, ENC_ROWS, 256), LOW),
+         shape_of((4, 2, ENC_ROWS, 512), LOW), shape_of((4, QROWS, 256), LOW)],
+        [whole((QROWS, WIDTH)), whole((QROWS, WIDTH)), part((1, QROWS, 256)),
+         part((1, ENC_ROWS, 256)), part((1, 2, ENC_ROWS, 512)), part((1, QROWS, 256))],
+        [pltpu.VMEM((ENC_ROWS, 512), F32), pltpu.VMEM((256, QROWS), F32)],
+        3 * 10**9,
+    )
+
+
+def feed(info, x3, cot, gain, wg, wu, wo):
+    units = wg.shape[2]
+    wide = part((1, WIDTH, units))
+    return run_heads(
+        feed_kernel, "feed",
+        (info, x3, cot, gain, wg, wu, wo),
+        [SCALARS, whole((QROWS, WIDTH)), whole((QROWS, WIDTH)), whole((1, WIDTH)),
+         wide, wide, wide],
+        [shape_of((QROWS, WIDTH), LOW), shape_of((QROWS, WIDTH), F32)]
+        + [shape_of((4, WIDTH, units), LOW)] * 3
+        + [shape_of((1, WIDTH), F32)],
+        [whole((QROWS, WIDTH)), whole((QROWS, WIDTH)), wide, wide, wide, whole((1, WIDTH))],
+        [pltpu.VMEM((QROWS, WIDTH), LOW), pltpu.VMEM((WIDTH, QROWS), LOW),
+         pltpu.VMEM((QROWS, WIDTH), LOW), pltpu.VMEM((WIDTH, QROWS), LOW),
+         pltpu.VMEM((QROWS, WIDTH), F32), pltpu.VMEM((QROWS, WIDTH), F32)],
+        13 * 10**9,
+    )
+
+
+def cross_backward(g3, x2, h, gain, w2, q, kv, p, o):
+    return run_heads(
+        cross_backward_kernel, "cross_backward",
+        (g3, x2, h, gain, w2, q, kv, p, o),
+        [whole((QROWS, WIDTH)), whole((QROWS, WIDTH)), whole((QROWS, WIDTH)),
+         whole((1, WIDTH)), part((1, WIDTH, 512)), part((1, QROWS, 256)),
+         part((1, ENC_ROWS, 256)), part((1, 2, ENC_ROWS, 512)), part((1, QROWS, 256))],
+        [shape_of((QROWS, WIDTH), F32), shape_of((4, ENC_ROWS, 256), LOW),
+         shape_of((4, WIDTH, 512), LOW), shape_of((1, WIDTH), F32)],
+        [whole((QROWS, WIDTH)), part((1, ENC_ROWS, 256)), part((1, WIDTH, 512)),
+         whole((1, WIDTH))],
+        [pltpu.VMEM((QROWS, WIDTH), LOW), pltpu.VMEM((WIDTH, QROWS), LOW),
+         pltpu.VMEM((WIDTH, QROWS), LOW), pltpu.VMEM((QROWS, WIDTH), F32),
+         pltpu.VMEM((ENC_ROWS, 512), F32), pltpu.VMEM((ENC_ROWS, 512), LOW),
+         pltpu.VMEM((256, QROWS), F32)],
+        5 * 10**9,
+    )
+
+
+def self_backward(g2, h, w1, q, kv, p, o):
+    return run_heads(
+        self_backward_kernel, "self_backward",
+        (g2, h, w1, q, kv, p, o),
+        [whole((QROWS, WIDTH)), whole((QROWS, WIDTH)), part((1, WIDTH, 512)),
+         part((1, QROWS, 256)), part((1, KEYS, 256)), part((1, 2, KEYS, 512)),
+         part((1, QROWS, 256))],
+        [shape_of((QROWS, WIDTH), F32), shape_of((4, KEYS, 256), LOW),
+         shape_of((4, WIDTH, 512), LOW), shape_of((4, 4, 8, SPAN), F32)],
+        [whole((QROWS, WIDTH)), part((1, KEYS, 256)), part((1, WIDTH, 512)),
+         part((1, 4, 8, SPAN))],
+        [pltpu.VMEM((QROWS, WIDTH), LOW), pltpu.VMEM((WIDTH, QROWS), LOW),
+         pltpu.VMEM((WIDTH, QROWS), LOW), pltpu.VMEM((KEYS, 512), F32),
+         pltpu.VMEM((KEYS, 512), LOW), pltpu.VMEM((256, QROWS), F32),
+         pltpu.VMEM((2, CHUNK, SPAN), F32)],
+        6 * 10**9,
+    )
+
+
+def last_grads(dh, dkv, x, h, gain, g2, w3, dkvc, enc):
+    rows = enc.shape[0]
+    return run_heads(
+        last_kernel, "last_grads",
+        (dh, dkv, x, h, gain, g2, w3, w3, dkvc, enc),
+        [whole((QROWS, WIDTH)), part((1, QROWS, 256)), whole((QROWS, WIDTH)),
+         whole((QROWS, WIDTH)), whole((1, WIDTH)), whole((QROWS, WIDTH)),
+         part((1, WIDTH, 256)), part((1, WIDTH, 256), 1), part((1, rows, 256)),
+         whole((rows, WIDTH))],
+        [shape_of((QROWS, WIDTH), LOW), shape_of((rows, WIDTH), LOW),
+         shape_of((4, WIDTH, 512), LOW), shape_of((1, WIDTH), F32)],
+        [whole((QROWS, WIDTH)), whole((rows, WIDTH)), part((1, WIDTH, 512)),
+         whole((1, WIDTH))],
+        [pltpu.VMEM((WIDTH, QROWS), LOW), pltpu.VMEM((WIDTH, rows), LOW),
+         pltpu.VMEM((QROWS, WIDTH), F32), pltpu.VMEM((rows, WIDTH), F32)],
+        3 * 10**9,
+    )
+
+
+ORDERS = ("xzy", "yzx", "zyx", "xzy", "yzx", "zxy", "zxy")
+SMALL_ROWS = 16
+LANES = 128
+
+
+def small_rows(gains, table):
+    flat = jnp.pad(table.reshape(1, -1).astype(F32), ((0, 0), (0, LANES - table.size)))
+    rows = jnp.concatenate([g.reshape(1, LANES).astype(F32) for g in gains] + [flat], axis=0)
+    return jnp.pad(rows, ((0, SMALL_ROWS - 4), (0, 0)))
+
+
+def swap(value, axis, pairs):
+    return lax.ppermute(value, axis, pairs)
+
+
+def share_rows(grads, y, half):
+    n = grads.shape[1] // 2
+    away = lax.dynamic_slice_in_dim(grads, (1 - y) * n, n, 1)
+    got = swap(away, "ctx", [(0, 1), (1, 0)])
+    mine = lax.dynamic_slice_in_dim(grads, y * n, n, 1).astype(F32)
+    n = n // 2
+    away = (
+        lax.dynamic_slice_in_dim(mine, (1 - half) * n, n, 1)
+        + lax.dynamic_slice_in_dim(got, (1 - half) * n, n, 1).astype(F32)
+    ).astype(LOW)
+    second = swap(away, "tp", [(0, 1), (1, 0), (2, 3), (3, 2)])
+    total = (
+        lax.dynamic_slice_in_dim(mine, half * n, n, 1)
+        + lax.dynamic_slice_in_dim(got, half * n, n, 1).astype(F32)
+        + second.astype(F32)
+    )
+    return total.astype(LOW)
+
+
+def tokens_split(
+    inputs, encoder, lengths, cotangent,
+    norm_self, self_query, self_key_matrix, self_value_matrix, self_out, bias_table,
+    norm_cross, cross_query, cross_key_matrix, cross_value_matrix, cross_out,
+    norm_feed, feed_gate, feed_up, feed_out,
+):
+    y = lax.axis_index("ctx")
+    t = lax.axis_index("tp")
+    seq, half = lax.div(t, 2), lax.rem(t, 2)
+    first = y * (2 * QROWS) + half * QROWS
+    info = jnp.stack([first, lax.dynamic_index_in_dim(lengths, seq, 0, False)])
+    x_seq = lax.dynamic_index_in_dim(inputs, seq, 0, False)
+    enc_seq = lax.dynamic_index_in_dim(encoder, seq, 0, False)
+    x_own = lax.dynamic_slice_in_dim(x_seq, half * QROWS, QROWS, 0)
+    cot = lax.dynamic_slice(cotangent, (seq, half * QROWS, 0), (1, QROWS, WIDTH))[0]
+    packed = (
+        feed_gate, feed_up, feed_out,
+        jnp.concatenate([self_query, self_out], axis=1),
+        jnp.concatenate([cross_query, cross_out], axis=1),
+        jnp.concatenate(
+            [self_key_matrix, self_value_matrix, cross_key_matrix, cross_value_matrix], axis=1
+        ),
+        small_rows((norm_self, norm_cross, norm_feed), bias_table),
+        x_seq, enc_seq,
+    )
+    wg, wu, wo, w1, w2, w3, small, x_all, enc_all = gather(
+        packed, ORDERS + ("y", "y"), 1, "gather_weights"
+    )
+    small = small.reshape(4, 8, SMALL_ROWS, LANES)
+    gains = jnp.transpose(small[0, :, :3], (1, 0, 2)).reshape(3, 1, WIDTH)
+    table = jnp.transpose(
+        small[:, :, 3, :16].reshape(4, 8, 4, 4), (1, 2, 0, 3)
+    ).reshape(BUCKETS, 16)
+    x_all = x_all.reshape(KEYS, WIDTH)
+    enc_all = enc_all.reshape(ENC_ROWS, WIDTH)
+
+    distance = jnp.maximum(
+        first + jnp.arange(SPAN)[None, :] - (SPAN - 264) - jnp.arange(8)[:, None], 0
+    )
+    bucket = bucket_index(distance)
+    x2, h1, q1, kv1, p1, o1 = self_forward(info, x_all, gains[0], w1, w3, table, bucket)
+    x3, h2, q2, kv2, p2, o2 = cross_forward(x2, enc_all, gains[1], w2, w3)
+    out, g3, gg, gu, go, gn3 = feed(info, x3, cot, gains[2], wg, wu, wo)
+    g2, dkv2, gw2, gn2 = cross_backward(g3, x2, h2, gains[1], w2, q2, kv2, p2, o2)
+    dh, dkv1, gw1, near = self_backward(g2, h1, w1, q1, kv1, p1, o1)
+    dkvc = share_rows(dkv2, y, half)
+    dkv = share_rows(dkv1, y, half)
+    enc_own = lax.dynamic_slice_in_dim(enc_seq, half * (QROWS // 2), QROWS // 2, 0)
+    gx, genc, gw3, gn1 = last_grads(
+        dh, dkv, x_own, h1, gains[0], g2, w3, dkvc, enc_own
+    )
+    one_hot = (bucket[:, :, None] == jnp.arange(BUCKETS, dtype=jnp.int32)).astype(F32)
+    grad_table = jnp.einsum(
+        "hrm,rmb->bh", near.reshape(16, 8, SPAN), one_hot, precision=TOP_PRECISION
+    )
+    gain_grads = jnp.concatenate([gn1, gn2, gn3], axis=0).reshape(3, 8, LANES)
+    gain_grads = jnp.broadcast_to(jnp.transpose(gain_grads, (1, 0, 2))[None], (4, 8, 3, LANES))
+    table_grads = jnp.transpose(grad_table.reshape(8, 4, 4, 4), (2, 0, 1, 3)).reshape(4, 8, 1, 16)
+    table_grads = jnp.pad(table_grads, ((0, 0), (0, 0), (0, 0), (0, LANES - 16)))
+    small_grads = jnp.pad(
+        jnp.concatenate([gain_grads, table_grads], axis=2),
+        ((0, 0), (0, 0), (0, SMALL_ROWS - 4), (0, 0)),
+    ).reshape(4, 8 * SMALL_ROWS, LANES)
+    gg, gu, go, gw1, gw2, gw3, gs = scatter(
+        (gg, gu, go, gw1, gw2, gw3, small_grads), ORDERS, 2, "scatter_grads"
+    )
+    out, gx, genc = gather((out, gx, genc), ("z", "z", "z"), 3, "gather_rows")
+    return (
+        out.reshape(inputs.shape),
+        gx.reshape(inputs.shape).astype(F32),
+        genc.reshape(encoder.shape).astype(F32),
+        gs[0], gw1[:, :256], gw3[:, :128], gw3[:, 128:256], gw1[:, 256:],
+        gs[3, :16].reshape(4, 4),
+        gs[1], gw2[:, :256], gw3[:, 256:384], gw3[:, 384:], gw2[:, 256:],
+        gs[2], gg, gu, go,
+    )
+
+
 def solution(mesh):
+    sizes = (mesh.shape["fsdp"], mesh.shape["ctx"], mesh.shape["tp"])
     return jax.shard_map(
-        shards,
+        tokens_split if sizes == (4, 2, DEPTH) else shards,
         mesh=mesh,
         in_specs=(
             P("fsdp", "ctx", None),

time: 1440 us -> 585 us (0.41)
  waiting for transfers between devices: 800 us -> 35.4 us
  Pallas kernels: 0 us -> 474 us
  blocking collectives: 244 us -> 0 us
  matrix products: 196 us -> 5.33 us
  other arithmetic: 95.6 us -> 23.6 us
  local copies, waits for them, and re-layouts: 72.2 us -> 31.6 us
  between operations: 18 us -> 1.14 us
    psum x5 -> x0, waiting for transfers between devices: 491 us -> none  [reduce_rows(): return lax.psum(partial_sum, 'tp')]
    pallas_call x0 -> x9, Pallas kernels: none -> 474 us  [the longest x2 245 us: gather(): pl.pallas_call(functools.partial(gather_kernel, orders, rows, count), out...]
    all_gather x16 -> x0, blocking collectives: 221 us -> none  [the longest x1 19.8 us: shards(): lax.all_gather(cross_out, ('fsdp', 'ctx'), axis=0, tiled=True)]
    dot_general x47 -> x1, matrix products: 196 us -> 5.33 us  [tokens_split(): jnp.einsum('hrm,rmb->bh', near.reshape(16, 8, SPAN), one_hot, precision=T...]
    reduce_scatter x10 -> x0, waiting for transfers between devices: 169 us -> none  [the longest x1 35.7 us: shards(): lax.psum_scatter(grad_cross_query.astype(jnp.bfloat16), ('fsdp', 'ctx'),...]
    unnamed x28 -> x0, waiting for transfers between devices: 139 us -> none
    reduce_sum x9 -> x0, other arithmetic: 48.9 us -> none  [the longest x1 19.2 us: backward_block(): grad_bias = jnp.sum(grad_scores, axis=0)]
    ppermute x0 -> x4, waiting for transfers between devices: none -> 35.4 us  [swap(): return lax.ppermute(value, axis, pairs)]
  transfers between devices with their start and end apart: 23 -> 4, of which waited for: 13 -> 2; matrix products, arithmetic and copies ran while one was open for 15% -> 3% of each run, Pallas kernels for 0% -> 0%
where the time goes in v1:
time: 585 us; the launch traced here: 575 us
  Pallas kernels  474 us (81%)
  waiting for transfers between devices  35.4 us (6%)
  local copies, waits for them, and re-layouts  31.6 us (5%)
  other arithmetic  23.6 us (4%)
    pallas_call x2, Pallas kernels, gather(): pl.pallas_call(functools.partial(gather_kernel, orders, rows, count), out...  245 us
    pallas_call x1, Pallas kernels, scatter(): pl.pallas_call(functools.partial(scatter_kernel, orders, rows, count), ou...  127 us
    pallas_call x6, Pallas kernels, run_heads(): pl.pallas_call(kernel, grid=(steps,), in_specs=specs, out_specs=out_specs...  102 us
    ppermute x4, waiting for transfers between devices, swap(): return lax.ppermute(value, axis, pairs)  35.4 us
    unnamed x47, local copies, waits for them, and re-layouts  13.3 us
  transfers between devices with their start and end apart: 4, of which 2 were waited for; matrix products, arithmetic and copies ran while one was open for 3% of the time, Pallas kernels for 0%

profile of v1, /device:TPU:12, one launch (start us, length us, event | category | flops | bytes accessed | tf_op | source)
XLA Modules:
  0.0 575.4 jit_solution(2917268507930505913)
XLA Ops:
  0.7 1.8 copy.45.refs_0_
  2.5 1.7 copy.46.refs_1_
  4.2 1.7 copy.47.refs_2_
  8.1 2.4 dynamic-slice_bitcast_fusion.refs_7_
  10.5 2.1 dynamic-slice_bitcast_fusion.2
  14.0 153.3 %gather_weights.1 = (bf16[4,1024,704]{2,1,0:T(8,128)(2,1)}, bf16[4,1024,704]{2,1,0:T(8,128)(2,1)}, bf16[4,1024,704]{2,1,0:T(8,128)(2,1)}, bf16[4,1024,512]{2,1,0...) custom-call(bf16[128,704]{1,0:T(8,128)(2,1)} %copy.45.refs_0_, ...), custom_call_target="tpu_custom_call" | custom-call | tf_op jit(solution)/shard_map/gather_weights/pallas_call | solution.py:612
  173.0 21.2 %self_forward.1 = (f32[256,1024]{1,0:T(8,128)}, bf16[256,1024]{1,0:T(8,128)(2,1)}, bf16[4,256,256]{2,1,0:T(8,128)(2,1)}, bf16[4,1024,256]{2,1,0:T(8,128)(2,1)}, ...) custom-call(s32[2]{0:T(128)} %pad_add_fusion.info, f32[32,16]{1,0:T(8,128)} %reshape.196.table, ...), custom_call_target="tpu_custom_call" | custom-call | flops 5000000000 | bytes 23640072 | tf_op jit(solution)/shard_map/self_forward/pallas_call | solution.py:1120
  194.2 13.0 %cross_forward.1 = (f32[256,1024]{1,0:T(8,128)}, bf16[256,1024]{1,0:T(8,128)(2,1)}, bf16[4,256,256]{2,1,0:T(8,128)(2,1)}, bf16[4,512,256]{2,1,0:T(8,128)(2,1)}, ...) custom-call(f32[256,1024]{1,0:T(8,128)} %get-tuple-element.71.x2_ref, bf16[512,1024]{1,0:T(8,128)(2,1)} %bitcast.92, ...), custom_call_target="tpu_custom_call" | custom-call | flops 3000000000 | bytes 18354176 | tf_op jit(solution)/shard_map/cross_forward/pallas_call | solution.py:1120
  207.2 23.8 %feed.1 = (bf16[256,1024]{1,0:T(8,128)(2,1)}, f32[256,1024]{1,0:T(8,128)}, bf16[4,1024,704]{2,1,0:T(8,128)(2,1)}, bf16[4,1024,704]{2,1,0:T(8,128)(2,1)}, bf16[4,...) custom-call(s32[2]{0:T(128)} %pad_add_fusion.info, f32[256,1024]{1,0:T(8,128)} %get-tuple-element.74.x3_ref, ...), custom_call_target="tpu_custom_call" | custom-call | flops 12999999488 | bytes 37756936 | tf_op jit(solution)/shard_map/feed/pallas_call | solution.py:1120
  231.0 15.2 %cross_backward.1 = (f32[256,1024]{1,0:T(8,128)}, bf16[4,512,256]{2,1,0:T(8,128)(2,1)}, bf16[4,1024,512]{2,1,0:T(8,128)(2,1)}, f32[1,1024]{1,0:T(1,128)}) custom-call(f32[256,1024]{1,0:T(8,128)} %get-tuple-element.79.g3_ref, f32[256,1024]{1,0:T(8,128)} %get-tuple-element.71.x2_ref, bf16[256,1024]{1,0:T(8,128)(2,1)} %get-tuple-element.80.h_ref, ...), custom_call_target="tpu_custom_call" | custom-call | flops 5000000000 | bytes 19406848 | tf_op jit(solution)/shard_map/cross_backward/pallas_call | solution.py:1120
  246.2 20.0 %self_backward.1 = (f32[256,1024]{1,0:T(8,128)}, bf16[4,1024,256]{2,1,0:T(8,128)(2,1)}, bf16[4,1024,512]{2,1,0:T(8,128)(2,1)}, f32[4,4,8,1280]{3,2,1,0:T(8,128)}) custom-call(f32[256,1024]{1,0:T(8,128)} %get-tuple-element.85.g2_ref, bf16[256,1024]{1,0:T(8,128)(2,1)} %get-tuple-element.86.h_ref, bf16[4,1024,512]{2,1,0:T(8,128)(2,1)} %get-tuple-element.69.w_ref, ...), custom_call_target="tpu_custom_call" | custom-call | flops 6000000000 | bytes 25296896 | tf_op jit(solution)/shard_map/self_backward/pallas_call | solution.py:1120
  266.2 2.8 constant_dynamic-slice_fusion.1
  269.0 1.5 collective-permute-start
  270.5 2.1 constant_dynamic-slice_fusion
  273.2 31.9 %collective-permute-done.2 = bf16[4,256,256]{2,1,0:T(8,128)(2,1)} collective-permute-done((bf16[4,256,256]{2,1,0:T(8,128)(2,1)}, bf16[4,256,256]{2,1,0:T(8,128)(2,1)}, u32[]{:S(2)}, u32[]{:S(2)}) %collective-permute-start.2) | collective-permute-done | bytes 524320 | tf_op jit(solution)/shard_map/ppermute | solution.py:1260
  305.1 1.7 add_convert_fusion.3
  307.2 2.0 add_convert_fusion.1
  309.2 1.6 collective-permute-start.1
  310.8 5.3 fusion.3
  316.2 1.7 dynamic-slice_bitcast_fusion.4.enc_ref
  317.9 2.0 dynamic-slice_bitcast_fusion.1.x_ref
  319.9 1.7 add_convert_fusion.2.dkvc_ref
  321.6 3.5 collective-permute-done.1
  325.2 2.2 add_convert_fusion.dkv_ref
  327.3 8.4 %last_grads.1 = (bf16[256,1024]{1,0:T(8,128)(2,1)}, bf16[128,1024]{1,0:T(8,128)(2,1)}, bf16[4,1024,512]{2,1,0:T(8,128)(2,1)}, f32[1,1024]{1,0:T(1,128)}) custom-call(f32[256,1024]{1,0:T(8,128)} %get-tuple-element.91.dh_part_ref, bf16[4,256,256]{2,1,0:T(8,128)(2,1)} %add_convert_fusion.dkv_ref, bf16[256,1024]{1,0:T(8,128)(2,1)} %dynamic-slice_bitcast_fusion.1.x_ref, ...), custom_call_target="tpu_custom_call" | custom-call | flops 3000000000 | bytes 17571840 | tf_op jit(solution)/shard_map/last_grads/pallas_call | solution.py:1120
  337.3 127.4 %scatter_grads.1 = (f32[128,704]{1,0:T(8,128)}, f32[128,704]{1,0:T(8,128)}, f32[128,704]{1,0:T(8,128)}, f32[128,512]{1,0:T(8,128)}, f32[128,512]{1,0:T(8,128)}, /*index=5*/f32[128,512]{1,0:T(8,128)}, f32[16,128]{1,0:T(8,128)}) custom-call(bf16[4,1024,704]{2,1,0:T(8,128)(2,1)} %get-tuple-element.99.refs_0_, bf16[4,1024,704]{2,1,0:T(8,128)(2,1)} %get-tuple-element.100.refs_1_, ...), custom_call_target="tpu_custom_call" | custom-call | tf_op jit(solution)/shard_map/scatter_grads/pallas_call | solution.py:777
  466.8 1.9 copy.56
  468.7 1.9 copy.57
  470.6 1.9 copy.58
  475.3 92.1 %gather_rows.1 = (bf16[4,256,1024]{2,1,0:T(8,128)(2,1)}, bf16[4,256,1024]{2,1,0:T(8,128)(2,1)}, bf16[4,128,1024]{2,1,0:T(8,128)(2,1)}) custom-call(bf16[256,1024]{1,0:T(8,128)(2,1)} %get-tuple-element.78.refs_0_, bf16[256,1024]{1,0:T(8,128)(2,1)} %get-tuple-element.94.refs_1_, bf16[128,1024]{1,0:T(8,128)(2,1)} %get-tuple-element.95.refs_2_), custom_call_target="tpu_custom_call" | custom-call | tf_op jit(solution)/shard_map/gather_rows/pallas_call | solution.py:612
  567.4 4.2 bitcast_convert_fusion
  571.6 1.6 bitcast_convert_fusion.1
  (73 shorter events, 18.9 us)
Async XLA Ops:
  0.7 9.8 %copy-start.2 = (bf16[2,256,1024]{2,1,0:T(8,128)(2,1)S(1)}, bf16[2,256,1024]{2,1,0:T(8,128)(2,1)}, u32[]{:S(2)}) copy-start(bf16[2,256,1024]{2,1,0:T(8,128)(2,1)} %param.20) | copy-start | bytes 3145732
  8.0 4.5 copy-start.6
  8.0 4.5 copy-start.7
  8.0 4.5 copy-start.8
  8.0 4.5 copy-start.9
  8.1 5.3 copy-start.10
  8.1 5.2 copy-start.11
  8.1 5.2 copy-start.12
  8.1 5.2 copy-start.13
  12.6 158.0 %copy-start.16 = (s32[2]{0:T(128)S(1)}, s32[2]{0:T(128)}, u32[]{:S(2)}) copy-start(s32[2]{0:T(128)} %param.21) | copy-start | bytes 28
  269.0 38.3 %collective-permute-start = (bf16[4,512,256]{2,1,0:T(8,128)(2,1)}, bf16[4,512,256]{2,1,0:T(8,128)(2,1)}, u32[]{:S(2)}, u32[]{:S(2)}) collective-permute-start(bf16[4,512,256]{2,1,0:T(8,128)(2,1)} %get-tuple-element.152), channel_id=1, source_target_pairs={{0,4},{4,0},{1,5},{5,1},{2,6},{6,2},{3,7},{7,3},{8,12},{12,8},{9,1... | collective-permute-start | bytes 3145736 | tf_op jit(solution)/shard_map/ppermute | solution.py:1260
  272.6 32.5 %collective-permute-start.2 = (bf16[4,256,256]{2,1,0:T(8,128)(2,1)}, bf16[4,256,256]{2,1,0:T(8,128)(2,1)}, u32[]{:S(2)}, u32[]{:S(2)}) collective-permute-start(bf16[4,256,256]{2,1,0:T(8,128)(2,1)} %get-tuple-element.154), channel_id=1, source_target_pairs={{0,4},{4,0},{1,5},{5,1},{2,6},{6,2},{3,7},{7,3},{8,12},{12,8},{9,1... | collective-permute-start | bytes 1572872 | tf_op jit(solution)/shard_map/ppermute | solution.py:1260
  273.1 37.7 %copy-start.17 = (f32[4,4,8,1280]{3,2,1,0:T(8,128)S(1)}, f32[4,4,8,1280]{3,2,1,0:T(8,128)}, u32[]{:S(2)}) copy-start(f32[4,4,8,1280]{3,2,1,0:T(8,128)} %get-tuple-element.108) | copy-start | bytes 1966084
  306.8 13.1 %collective-permute-start.3 = (bf16[4,128,256]{2,1,0:T(8,128)(2,1)}, bf16[4,128,256]{2,1,0:T(8,128)(2,1)S(1)}, u32[]{:S(2)}, u32[]{:S(2)}) collective-permute-start(bf16[4,128,256]{2,1,0:T(8,128)(2,1)} %add_convert_fusion.3), channel_id=1, source_target_pairs={{0,1},{1,0},{2,3},{3,2},{4,5},{5,4},{6,7},{7,6},{8,9},{9,8},{10,11... | collective-permute-start | bytes 786440 | tf_op jit(solution)/shard_map/ppermute | solution.py:1260
  309.2 16.0 %collective-permute-start.1 = (bf16[4,256,256]{2,1,0:T(8,128)(2,1)}, bf16[4,256,256]{2,1,0:T(8,128)(2,1)}, u32[]{:S(2)}, u32[]{:S(2)}) collective-permute-start(bf16[4,256,256]{2,1,0:T(8,128)(2,1)} %add_convert_fusion.1), channel_id=1, source_target_pairs={{0,1},{1,0},{2,3},{3,2},{4,5},{5,4},{6,7},{7,6},{8,9},{9,8},{10,11... | collective-permute-start | bytes 1572872 | tf_op jit(solution)/shard_map/ppermute | solution.py:1260
  327.3 8.4 %copy-start.14 = (f32[1,1024]{1,0:T(1,128)S(1)}, f32[1,1024]{1,0:T(1,128)}, u32[]{:S(2)}) copy-start(f32[1,1024]{1,0:T(1,128)} %get-tuple-element.107) | copy-start | bytes 12292
  327.3 8.4 %copy-start.15 = (f32[1,1024]{1,0:T(1,128)S(1)}, f32[1,1024]{1,0:T(1,128)}, u32[]{:S(2)}) copy-start(f32[1,1024]{1,0:T(1,128)} %get-tuple-element.106) | copy-start | bytes 12292
  464.7 7.8 %copy-start.5 = (f32[128,512]{1,0:T(8,128)S(1)}, f32[128,512]{1,0:T(8,128)}, u32[]{:S(2)}) copy-start(f32[128,512]{1,0:T(8,128)} %get-tuple-element.110) | copy-start | bytes 786436
  464.7 8.5 %copy-start.4 = (f32[128,512]{1,0:T(8,128)S(1)}, f32[128,512]{1,0:T(8,128)}, u32[]{:S(2)}) copy-start(f32[128,512]{1,0:T(8,128)} %get-tuple-element.111) | copy-start | bytes 786436
  464.7 9.2 %copy-start.3 = (f32[128,512]{1,0:T(8,128)S(1)}, f32[128,512]{1,0:T(8,128)}, u32[]{:S(2)}) copy-start(f32[128,512]{1,0:T(8,128)} %get-tuple-element.112) | copy-start | bytes 786436
  567.4 4.2 copy-start.1
  571.6 2.3 copy-start

commit v2 on v1

--- a/solution.py
+++ b/solution.py
@@ -520,107 +520,104 @@
     )
 
 
-def gather_kernel(orders, rows, count, *refs):
-    ins, outs = refs[:count], refs[count : 2 * count]
-    send, recv, core_recv, local_sem = refs[2 * count :]
-    place = Place()
-    greet(place)
-    me = (place.x, place.y, place.z)
-
-    def slot(j, xyz, c):
+class Gather:
+    def __init__(self, place, orders, rows, ins, outs, sems):
+        self.place, self.orders, self.rows, self.ins, self.outs = place, orders, rows, ins, outs
+        self.send, self.recv, self.core_recv, self.local_sem = sems
+        self.me = (place.x, place.y, place.z)
+        self.arrivals = [
+            (k, hops, j, src, d)
+            for j in range(len(orders))
+            for k, hops, src, d in arrivals(orders[j])
+        ]
+        self.arrivals.sort(key=lambda e: (e[0], e[1]))
+
+    @staticmethod
+    def scratch(count):
+        dma = pltpu.SemaphoreType.DMA
+        return [
+            dma((count, 4 * DEPTH, 5)), dma((count, 4 * DEPTH)), dma((count, 4 * DEPTH)),
+            dma((count,)),
+        ]
+
+    def slot(self, j, xyz, c):
         x, y, z = xyz
-        if len(orders[j]) == 1:
-            return outs[j].at[y if orders[j] == "y" else z]
-        at = ((x * 2 + c) * 2 + y) * rows[j]
-        return outs[j].at[z, pl.ds(pl.multiple_of(at, rows[j]), rows[j]), :]
-
-    def copy(j, xyz, link, own):
-        here = slot(j, xyz, place.c)
-        arrived = core_recv if link[0] == "c" else recv
+        if len(self.orders[j]) == 1:
+            return self.outs[j].at[y if self.orders[j] == "y" else z]
+        at = ((x * 2 + c) * 2 + y) * self.rows[j]
+        return self.outs[j].at[z, pl.ds(pl.multiple_of(at, self.rows[j]), self.rows[j]), :]
+
+    def copy(self, j, xyz, link, own):
+        here = self.slot(j, xyz, self.place.c)
+        arrived = self.core_recv if link[0] == "c" else self.recv
         i = number(*xyz)
         return remote(
-            ins[j] if own else here, here, send.at[j, i, LINKS[link]], arrived.at[j, i],
-            place.link(*link),
+            self.ins[j] if own else here, here, self.send.at[j, i, LINKS[link]],
+            arrived.at[j, i], self.place.link(*link),
         )
 
-    def routes(j, k, d):
-        links = onward(orders[j], k, d)
-        return links + [("c", 0)] if len(orders[j]) == 3 else links
-
-    for stage in range(2):
+    def routes(self, j, k, d):
+        links = onward(self.orders[j], k, d)
+        return links + [("c", 0)] if len(self.orders[j]) == 3 else links
+
+    def local(self, j):
+        return pltpu.make_async_copy(
+            self.ins[j], self.slot(j, self.me, self.place.c), self.local_sem.at[j]
+        )
+
+    def start(self, first=()):
+        count = len(self.orders)
+        turn = list(first) + [j for j in range(count) if j not in first]
+        for stage in range(2):
+            for j in turn:
+                for link in self.routes(j, -1, 0):
+                    if (link[0] == "c") == (stage == 1):
+                        when(self.place.has(link), self.copy(j, self.me, link, True).start)
         for j in range(count):
-            for link in routes(j, -1, 0):
-                if (link[0] == "c") == (stage == 1):
-                    when(place.has(link), copy(j, me, link, True).start)
-    local = []
-    for j in range(count):
-        local.append(pltpu.make_async_copy(ins[j], slot(j, me, place.c), local_sem.at[j]))
-        local[-1].start()
-    events = [
-        (k, hops, j, src, d)
-        for j in range(count)
-        for k, hops, src, d in arrivals(orders[j])
-    ]
-    events.sort(key=lambda e: (e[0], e[1]))
-    for k, hops, j, src, d in events:
-        xyz = place.source(src)
-
-        def step():
-            copy(j, xyz, ("x", 0), True).wait_recv()
-            for link in routes(j, k, d):
-                when(place.has(link), copy(j, xyz, link, False).start)
-
-        when(place.exists(src), step)
-    for c in local:
-        c.wait()
-    for j in range(count):
-        for link in routes(j, -1, 0):
-            when(place.has(link), copy(j, me, link, True).wait_send)
-    for k, hops, j, src, d in events:
-        xyz = place.source(src)
-
-        def finish():
-            for link in routes(j, k, d):
-                when(place.has(link), copy(j, xyz, link, False).wait_send)
-
-        when(place.exists(src), finish)
-    for j in range(count):
-        if len(orders[j]) == 3:
-
-            def from_core(i, carry):
-                xyz = (lax.div(i, 2 * DEPTH), lax.rem(lax.div(i, DEPTH), 2), lax.rem(i, DEPTH))
-                there = slot(j, xyz, 1 - place.c)
-                remote(
-                    ins[j], there, send.at[j, i, 4], core_recv.at[j, i], place.link("c", 0)
-                ).wait_recv()
-                return carry
-
-            lax.fori_loop(0, 4 * DEPTH, from_core, 0)
-
-
-def gather(arrays, orders, number_id, name):
-    count = len(arrays)
-    rows = [a.shape[0] for a in arrays]
-    outs = [
-        jax.ShapeDtypeStruct(
-            (SIZES[o],) + a.shape if len(o) == 1 else (DEPTH, 8 * a.shape[0], a.shape[1]),
-            a.dtype,
-        )
-        for a, o in zip(arrays, orders)
-    ]
-    dma = pltpu.SemaphoreType.DMA
-    return pl.pallas_call(
-        functools.partial(gather_kernel, orders, rows, count),
-        out_shape=outs,
-        in_specs=[pl.BlockSpec(memory_space=pltpu.VMEM)] * count,
-        out_specs=[pl.BlockSpec(memory_space=pl.ANY)] * count,
-        scratch_shapes=[
-            dma((count, 4 * DEPTH, 5)), dma((count, 4 * DEPTH)), dma((count, 4 * DEPTH)),
-            dma((count,)),
-        ],
-        compiler_params=pltpu.CompilerParams(collective_id=number_id, has_side_effects=True),
-        name=name,
-    )(*arrays)
+            self.local(j).start()
+
+    def steps(self):
+        for e, (k, hops, j, src, d) in enumerate(self.arrivals):
+            xyz = self.place.source(src)
+
+            def step(k=k, j=j, d=d, xyz=xyz, src=src):
+                def run():
+                    self.copy(j, xyz, ("x", 0), True).wait_recv()
+                    for link in self.routes(j, k, d):
+                        when(self.place.has(link), self.copy(j, xyz, link, False).start)
+
+                when(self.place.exists(src), run)
+
+            yield (e + 1) / len(self.arrivals), step
+
+    def finish(self):
+        count = len(self.orders)
+        for j in range(count):
+            self.local(j).wait()
+            for link in self.routes(j, -1, 0):
+                when(self.place.has(link), self.copy(j, self.me, link, True).wait_send)
+        for k, hops, j, src, d in self.arrivals:
+            xyz = self.place.source(src)
+
+            def run():
+                for link in self.routes(j, k, d):
+                    when(self.place.has(link), self.copy(j, xyz, link, False).wait_send)
+
+            when(self.place.exists(src), run)
+        for j in range(count):
+            if len(self.orders[j]) == 3:
+
+                def from_core(i, carry):
+                    xyz = (
+                        lax.div(i, 2 * DEPTH), lax.rem(lax.div(i, DEPTH), 2), lax.rem(i, DEPTH)
+                    )
+                    remote(
+                        self.ins[j], self.slot(j, xyz, 1 - self.place.c), self.send.at[j, i, 4],
+                        self.core_recv.at[j, i], self.place.link("c", 0),
+                    ).wait_recv()
+                    return carry
+
+                lax.fori_loop(0, 4 * DEPTH, from_core, 0)
 
 
 def child_slots(order):
@@ -641,72 +638,95 @@
     return starts[m] + at
 
 
-def scatter_kernel(orders, rows, count, *refs):
-    ins, outs = refs[:count], refs[count : 2 * count]
-    sums, gifts, kids = (refs[i * count : (i + 1) * count] for i in (2, 3, 4))
-    load_sem, give_sem, gift_sem, up_sem, kid_sem = refs[5 * count :]
-    place = Place()
-    greet(place)
-    me = (place.x, place.y, place.z)
-    plans = [child_slots(o) for o in orders]
-    partner = place.link("c", 0)
-
-    def slot(j, xyz, c):
+def add_rows(out, terms, rows):
+    step = min(rows, 16)
+
+    def body(q, carry):
+        at = pl.ds(pl.multiple_of(q * step, step), step)
+        value = terms[0][at, :].astype(jnp.float32)
+        for term in terms[1:]:
+            value = value + term[at, :].astype(jnp.float32)
+        out[at, :] = value.astype(out.dtype)
+        return carry
+
+    lax.fori_loop(0, rows // step, body, 0)
+
+
+class Scatter:
+    def __init__(self, place, orders, rows, ins, outs, scratch):
+        self.place, self.orders, self.rows, self.ins, self.outs = place, orders, rows, ins, outs
+        n = len(orders)
+        self.sums, self.gifts, self.kids = (scratch[i * n : (i + 1) * n] for i in range(3))
+        self.load_sem, self.give_sem, self.gift_sem, self.up_sem, self.kid_sem = scratch[3 * n :]
+        self.me = (place.x, place.y, place.z)
+        self.plans = [child_slots(o) for o in orders]
+        self.partner = place.link("c", 0)
+        self.events = [
+            (k, hops, j, src, d)
+            for j in range(n)
+            for k, hops, src, d in arrivals(orders[j])
+        ]
+        self.events.sort(key=lambda e: (-e[0], -e[1]))
+
+    @staticmethod
+    def scratch(arrays, rows, orders):
+        plans = [child_slots(o)[1] for o in orders]
+        count = len(arrays)
+        dma = pltpu.SemaphoreType.DMA
+
+        def room(slots):
+            return [
+                pltpu.VMEM((n, r, a.shape[2]), a.dtype) for n, r, a in zip(slots, rows, arrays)
+            ]
+
+        full = [4 * DEPTH] * count
+        return (
+            room(full) + room(full) + room(plans)
+            + [dma((count, 4 * DEPTH))] * 4 + [dma((count, max(plans)))]
+        )
+
+    def slot(self, j, xyz, c):
         x, y, z = xyz
-        at = ((x * 2 + c) * 2 + y) * rows[j]
-        return ins[j].at[z, pl.ds(pl.multiple_of(at, rows[j]), rows[j]), :]
-
-    def load(j, xyz):
+        at = ((x * 2 + c) * 2 + y) * self.rows[j]
+        return self.ins[j].at[z, pl.ds(pl.multiple_of(at, self.rows[j]), self.rows[j]), :]
+
+    def load(self, j, xyz):
         i = number(*xyz)
-        return pltpu.make_async_copy(slot(j, xyz, place.c), sums[j].at[i], load_sem.at[j, i])
-
-    def give(j, xyz):
+        return pltpu.make_async_copy(
+            self.slot(j, xyz, self.place.c), self.sums[j].at[i], self.load_sem.at[j, i]
+        )
+
+    def give(self, j, xyz):
         i = number(*xyz)
         return remote(
-            slot(j, xyz, 1 - place.c), gifts[j].at[i], give_sem.at[j, i], gift_sem.at[j, i],
-            partner,
+            self.slot(j, xyz, 1 - self.place.c), self.gifts[j].at[i], self.give_sem.at[j, i],
+            self.gift_sem.at[j, i], self.partner,
         )
 
-    def up(j, xyz, k, d):
-        axis = orders[j][k]
+    def up(self, j, xyz, k, d):
+        axis = self.orders[j][k]
         tail = xyz[2]
         if axis == "z" and d < 0:
-            tail = jnp.where(xyz[2] == place.z - d, DEPTH, xyz[2])
-        at = child_slot(orders[j], plans[j][0], k, xyz, tail)
+            tail = jnp.where(xyz[2] == self.place.z - d, DEPTH, xyz[2])
+        at = child_slot(self.orders[j], self.plans[j][0], k, xyz, tail)
         i = number(*xyz)
         return remote(
-            sums[j].at[i], kids[j].at[at], up_sem.at[j, i], kid_sem.at[j, at],
-            place.link(axis, -d),
+            self.sums[j].at[i], self.kids[j].at[at], self.up_sem.at[j, i],
+            self.kid_sem.at[j, at], self.place.link(axis, -d),
         )
 
-    def kid(j, m, xyz, tail):
-        at = child_slot(orders[j], plans[j][0], m, xyz, tail)
-        ref = kids[j].at[at]
-        remote(ref, ref, up_sem.at[j, 0], kid_sem.at[j, at], partner).wait_recv()
+    def kid(self, j, m, xyz, tail):
+        at = child_slot(self.orders[j], self.plans[j][0], m, xyz, tail)
+        ref = self.kids[j].at[at]
+        remote(ref, ref, self.up_sem.at[j, 0], self.kid_sem.at[j, at], self.partner).wait_recv()
         return ref
 
-    def add(j, i, terms, out=None):
-        total = sums[j].at[i]
-        step = min(rows[j], 16)
-
-        def body(q, carry):
-            at = pl.ds(pl.multiple_of(q * step, step), step)
-            value = total[at, :].astype(jnp.float32)
-            for term in terms:
-                value = value + term[at, :].astype(jnp.float32)
-            if out is None:
-                total[at, :] = value.astype(total.dtype)
-            else:
-                out[at, :] = value.astype(out.dtype)
-            return carry
-
-        lax.fori_loop(0, rows[j] // step, body, 0)
-
-    def collect(j, xyz, k, d, out=None):
+    def collect(self, j, xyz, k, d, out=None):
         i = number(*xyz)
-        order = orders[j]
-        load(j, xyz).wait()
-        give(j, xyz).wait_recv()
+        order = self.orders[j]
+        total = self.sums[j].at[i]
+        self.load(j, xyz).wait()
+        self.give(j, xyz).wait_recv()
         always, sometimes = [], []
         if k >= 0 and order[k] == "z":
             sometimes.append((k, ("z", d), xyz[2]))
@@ -718,76 +738,252 @@
         for m, link, tail in sometimes:
 
             def more():
-                add(j, i, [kid(j, m, xyz, tail)])
-
-            when(place.has(link), more)
-        add(j, i, [gifts[j].at[i]] + [kid(j, m, xyz, 0) for m in always], out)
-
-    events = [
-        (k, hops, j, src, d)
-        for j in range(count)
-        for k, hops, src, d in arrivals(orders[j])
-    ]
-    events.sort(key=lambda e: (-e[0], -e[1]))
-    for k, hops, j, src, d in events:
-        xyz = place.source(src)
-
-        def begin():
-            give(j, xyz).start()
-            load(j, xyz).start()
-
-        when(place.exists(src), begin)
-    for j in range(count):
-        give(j, me).start()
-        load(j, me).start()
-    for k, hops, j, src, d in events:
-        xyz = place.source(src)
-
-        def step():
-            collect(j, xyz, k, d)
-            up(j, xyz, k, d).start()
-
-        when(place.exists(src), step)
-    for j in range(count):
-        collect(j, me, -1, 0, outs[j])
-    for k, hops, j, src, d in events:
-        xyz = place.source(src)
-
-        def finish():
-            up(j, xyz, k, d).wait_send()
-            give(j, xyz).wait_send()
-
-        when(place.exists(src), finish)
-    for j in range(count):
-        give(j, me).wait_send()
-
-
-def scatter(arrays, orders, number_id, name):
-    count = len(arrays)
-    rows = [a.shape[1] // 8 for a in arrays]
-    plans = [child_slots(o)[1] for o in orders]
-    dma = pltpu.SemaphoreType.DMA
-
-    def room(slots):
-        return [
-            pltpu.VMEM((n, r, a.shape[2]), a.dtype) for n, r, a in zip(slots, rows, arrays)
-        ]
-
-    full = [4 * DEPTH] * count
+                add_rows(total, [total, self.kid(j, m, xyz, tail)], self.rows[j])
+
+            when(self.place.has(link), more)
+        terms = [total, self.gifts[j].at[i]] + [self.kid(j, m, xyz, 0) for m in always]
+        add_rows(total if out is None else out, terms, self.rows[j])
+
+    def start(self):
+        for k, hops, j, src, d in self.events:
+            xyz = self.place.source(src)
+
+            def begin():
+                self.give(j, xyz).start()
+                self.load(j, xyz).start()
+
+            when(self.place.exists(src), begin)
+        for j in range(len(self.orders)):
+            self.give(j, self.me).start()
+            self.load(j, self.me).start()
+
+    def steps(self):
+        count = len(self.events)
+        for e, (k, hops, j, src, d) in enumerate(self.events):
+            xyz = self.place.source(src)
+
+            def step(k=k, j=j, d=d, xyz=xyz, src=src):
+                def run():
+                    self.collect(j, xyz, k, d)
+                    self.up(j, xyz, k, d).start()
+
+                when(self.place.exists(src), run)
+
+            yield (e + 1) / (count + 1), step
+        for j in range(len(self.orders)):
+
+            def last(j=j):
+                self.collect(j, self.me, -1, 0, self.outs[j])
+
+            yield 1.0, last
+
+    def finish(self):
+        for k, hops, j, src, d in self.events:
+            xyz = self.place.source(src)
+
+            def run():
+                self.up(j, xyz, k, d).wait_send()
+                self.give(j, xyz).wait_send()
+
+            when(self.place.exists(src), run)
+        for j in range(len(self.orders)):
+            self.give(j, self.me).wait_send()
+
+
+class Share:
+    def __init__(self, place, rows, ins, outs, scratch):
+        self.place, self.rows, self.ins, self.outs = place, rows, ins, outs
+        n = len(rows)
+        self.first, self.second, self.sums = (scratch[i * n : (i + 1) * n] for i in range(3))
+        self.send, self.recv = scratch[3 * n :]
+        self.half = lax.rem(place.z, 2)
+        self.over_y = place.link("y", 0)
+        self.over_z = place.link("z", 1 - 2 * self.half)
+
+    @staticmethod
+    def scratch(rows):
+        dma = pltpu.SemaphoreType.DMA
+        out = []
+        for slots in (8, 4, 4):
+            out += [pltpu.VMEM((slots, n, 256), jnp.bfloat16) for n in rows]
+        return out + [dma((len(rows), 12)), dma((len(rows), 12))]
+
+    def block(self, j, t, y, half):
+        n = self.rows[j]
+        return self.ins[j].at[t, pl.ds(pl.multiple_of((y * 2 + half) * n, n), n), :]
+
+    def early(self, j, t, s):
+        if t < 2:
+            src, device = self.block(j, t, 1 - self.place.y, s), self.over_y
+        else:
+            src, device = self.block(j, t, s, 1 - self.half), self.over_z
+        i = t * 2 + s
+        return remote(src, self.first[j].at[i], self.send.at[j, i], self.recv.at[j, i], device)
+
+    def late(self, j, t):
+        return remote(
+            self.sums[j].at[t], self.second[j].at[t], self.send.at[j, 8 + t],
+            self.recv.at[j, 8 + t], self.over_z if t < 2 else self.over_y,
+        )
+
+    def start(self):
+        for j in range(len(self.rows)):
+            for s in range(2):
+                for t in range(4):
+                    self.early(j, t, s).start()
+
+    def steps(self):
+        for j in range(len(self.rows)):
+            for t in range(4):
+
+                def pass_on(j=j, t=t):
+                    for s in range(2):
+                        self.early(j, t, s).wait_recv()
+                    if t < 2:
+                        away = 1 - self.half
+                        mine = self.block(j, t, self.place.y, away)
+                    else:
+                        away = 1 - self.place.y
+                        mine = self.block(j, t, away, self.half)
+                    add_rows(
+                        self.sums[j].at[t], [mine, self.first[j].at[t * 2 + away]], self.rows[j]
+                    )
+                    self.late(j, t).start()
+
+                yield 0.25, pass_on
+        for j in range(len(self.rows)):
+            for t in range(4):
+
+                def total(j=j, t=t):
+                    self.late(j, t).wait_recv()
+                    kept = self.half if t < 2 else self.place.y
+                    mine = self.block(j, t, self.place.y, self.half)
+                    add_rows(
+                        self.outs[j].at[t],
+                        [mine, self.first[j].at[t * 2 + kept], self.second[j].at[t]],
+                        self.rows[j],
+                    )
+
+                yield 0.5, total
+
+    def finish(self):
+        for j in range(len(self.rows)):
+            for t in range(4):
+                for s in range(2):
+                    self.early(j, t, s).wait_send()
+                self.late(j, t).wait_send()
+
+
+def run_steps(parts):
+    steps = []
+    for plan, begin, length in parts:
+        steps += [(begin + length * at, step) for at, step in plan.steps()]
+    steps.sort(key=lambda s: s[0])
+    for _, step in steps:
+        step()
+
+
+HBM = pl.BlockSpec(memory_space=pl.ANY)
+INSIDE = pl.BlockSpec(memory_space=pltpu.VMEM)
+
+
+def comm_call(kernel, name, number_id, ins, in_specs, outs, out_specs, scratch):
     return pl.pallas_call(
-        functools.partial(scatter_kernel, orders, rows, count),
-        out_shape=[
-            jax.ShapeDtypeStruct((r, a.shape[2]), jnp.float32) for r, a in zip(rows, arrays)
-        ],
-        in_specs=[pl.BlockSpec(memory_space=pl.ANY)] * count,
-        out_specs=[pl.BlockSpec(memory_space=pltpu.VMEM)] * count,
-        scratch_shapes=room(full) + room(full) + room(plans)
-        + [dma((count, 4 * DEPTH))] * 4 + [dma((count, max(plans)))],
+        kernel,
+        out_shape=outs,
+        in_specs=in_specs,
+        out_specs=out_specs,
+        scratch_shapes=scratch,
         compiler_params=pltpu.CompilerParams(
             collective_id=number_id, has_side_effects=True, vmem_limit_bytes=67043328
         ),
         name=name,
-    )(*arrays)
+    )(*ins)
+
+
+def gathered(a, order):
+    if len(order) == 1:
+        return jax.ShapeDtypeStruct((SIZES[order],) + a.shape, a.dtype)
+    return jax.ShapeDtypeStruct((DEPTH, 8 * a.shape[0], a.shape[1]), a.dtype)
+
+
+def gather(arrays, orders, name):
+    count = len(arrays)
+    rows = [a.shape[0] for a in arrays]
+
+    def kernel(*refs):
+        place = Place()
+        ins, outs, sems = refs[:count], refs[count : 2 * count], refs[2 * count :]
+        plan = Gather(place, orders, rows, ins, outs, sems)
+        greet(place)
+        plan.start()
+        run_steps([(plan, 0.0, 1.0)])
+        plan.finish()
+
+    return comm_call(
+        kernel, name, 1, arrays, [INSIDE] * count,
+        [gathered(a, o) for a, o in zip(arrays, orders)], [HBM] * count,
+        Gather.scratch(count),
+    )
+
+
+def scattered(arrays):
+    return [
+        jax.ShapeDtypeStruct((a.shape[1] // 8, a.shape[2]), jnp.float32) for a in arrays
+    ]
+
+
+def scatter_and_share(arrays, orders, shared, name):
+    n, m = len(arrays), len(shared)
+    rows = [a.shape[1] // 8 for a in arrays]
+    own = [a.shape[1] // 4 for a in shared]
+    room = Scatter.scratch(arrays, rows, orders)
+
+    def kernel(*refs):
+        place = Place()
+        ins, outs, scratch = refs[: n + m], refs[n + m : 2 * (n + m)], refs[2 * (n + m) :]
+        plan = Scatter(place, orders, rows, ins[:n], outs[:n], scratch[: len(room)])
+        share = Share(place, own, ins[n:], outs[n:], scratch[len(room) :])
+        greet(place)
+        share.start()
+        plan.start()
+        run_steps([(plan, 0.0, 80.0), (share, 0.0, 80.0)])
+        share.finish()
+        plan.finish()
+
+    return comm_call(
+        kernel, name, 2, arrays + shared, [HBM] * n + [INSIDE] * m,
+        scattered(arrays)
+        + [jax.ShapeDtypeStruct((4, r, 256), jnp.bfloat16) for r in own],
+        [INSIDE] * (n + m), room + Share.scratch(own),
+    )
+
+
+def scatter_and_rows(arrays, orders, rows_in, name):
+    n, m = len(arrays), len(rows_in)
+    rows = [a.shape[1] // 8 for a in arrays]
+    room = Scatter.scratch(arrays, rows, orders)
+
+    def kernel(*refs):
+        place = Place()
+        ins, outs, scratch = refs[: n + m], refs[n + m : 2 * (n + m)], refs[2 * (n + m) :]
+        plan = Scatter(place, orders, rows, ins[:n], outs[:n], scratch[: len(room)])
+        lines = Gather(
+            place, ["z"] * m, [a.shape[0] for a in rows_in], ins[n:], outs[n:],
+            scratch[len(room) :],
+        )
+        greet(place)
+        lines.start()
+        plan.start()
+        run_steps([(plan, 0.0, 70.0), (lines, 0.0, 60.0)])
+        lines.finish()
+        plan.finish()
+
+    return comm_call(
+        kernel, name, 3, arrays + rows_in, [HBM] * n + [INSIDE] * m,
+        scattered(arrays) + [gathered(a, "z") for a in rows_in],
+        [INSIDE] * n + [HBM] * m, room + Gather.scratch(m),
+    )
 
 
 WIDTH = 1024
@@ -1245,7 +1441,9 @@
     )
 
 
-ORDERS = ("xzy", "yzx", "zyx", "xzy", "yzx", "zxy", "zxy")
+GATHER_ORDERS = ("yzx", "yzx", "zxy", "yxz", "zxy", "zxy", "zxy")
+FEED_ORDERS = ("xzy", "zyx", "yzx")
+HEAD_ORDERS = ("zyx", "zxy", "zyx", "zxy")
 SMALL_ROWS = 16
 LANES = 128
 
@@ -1256,27 +1454,14 @@
     return jnp.pad(rows, ((0, SMALL_ROWS - 4), (0, 0)))
 
 
-def swap(value, axis, pairs):
-    return lax.ppermute(value, axis, pairs)
-
-
-def share_rows(grads, y, half):
-    n = grads.shape[1] // 2
-    away = lax.dynamic_slice_in_dim(grads, (1 - y) * n, n, 1)
-    got = swap(away, "ctx", [(0, 1), (1, 0)])
-    mine = lax.dynamic_slice_in_dim(grads, y * n, n, 1).astype(F32)
-    n = n // 2
-    away = (
-        lax.dynamic_slice_in_dim(mine, (1 - half) * n, n, 1)
-        + lax.dynamic_slice_in_dim(got, (1 - half) * n, n, 1).astype(F32)
-    ).astype(LOW)
-    second = swap(away, "tp", [(0, 1), (1, 0), (2, 3), (3, 2)])
-    total = (
-        lax.dynamic_slice_in_dim(mine, half * n, n, 1)
-        + lax.dynamic_slice_in_dim(got, half * n, n, 1).astype(F32)
-        + second.astype(F32)
-    )
-    return total.astype(LOW)
+def rows_along_tp(own, t):
+    found = [own]
+    for k in range(1, DEPTH):
+        found.append(lax.ppermute(own, "tp", [(i, (i + k) % DEPTH) for i in range(DEPTH)]))
+    found = jnp.stack(found)
+    return jnp.stack(
+        [lax.dynamic_index_in_dim(found, (t - i + DEPTH) % DEPTH, 0, False) for i in range(DEPTH)]
+    )
 
 
 def tokens_split(
@@ -1305,7 +1490,7 @@
         x_seq, enc_seq,
     )
     wg, wu, wo, w1, w2, w3, small, x_all, enc_all = gather(
-        packed, ORDERS + ("y", "y"), 1, "gather_weights"
+        packed, GATHER_ORDERS + ("y", "y"), "gather_weights"
     )
     small = small.reshape(4, 8, SMALL_ROWS, LANES)
     gains = jnp.transpose(small[0, :, :3], (1, 0, 2)).reshape(3, 1, WIDTH)
@@ -1322,10 +1507,12 @@
     x2, h1, q1, kv1, p1, o1 = self_forward(info, x_all, gains[0], w1, w3, table, bucket)
     x3, h2, q2, kv2, p2, o2 = cross_forward(x2, enc_all, gains[1], w2, w3)
     out, g3, gg, gu, go, gn3 = feed(info, x3, cot, gains[2], wg, wu, wo)
+    out = rows_along_tp(out, t)
     g2, dkv2, gw2, gn2 = cross_backward(g3, x2, h2, gains[1], w2, q2, kv2, p2, o2)
     dh, dkv1, gw1, near = self_backward(g2, h1, w1, q1, kv1, p1, o1)
-    dkvc = share_rows(dkv2, y, half)
-    dkv = share_rows(dkv1, y, half)
+    gg, gu, go, dkv, dkvc = scatter_and_share(
+        (gg, gu, go), FEED_ORDERS, (dkv1, dkv2), "scatter_feed"
+    )
     enc_own = lax.dynamic_slice_in_dim(enc_seq, half * (QROWS // 2), QROWS // 2, 0)
     gx, genc, gw3, gn1 = last_grads(
         dh, dkv, x_own, h1, gains[0], g2, w3, dkvc, enc_own
@@ -1342,10 +1529,9 @@
         jnp.concatenate([gain_grads, table_grads], axis=2),
         ((0, 0), (0, 0), (0, SMALL_ROWS - 4), (0, 0)),
     ).reshape(4, 8 * SMALL_ROWS, LANES)
-    gg, gu, go, gw1, gw2, gw3, gs = scatter(
-        (gg, gu, go, gw1, gw2, gw3, small_grads), ORDERS, 2, "scatter_grads"
-    )
-    out, gx, genc = gather((out, gx, genc), ("z", "z", "z"), 3, "gather_rows")
+    gw1, gw2, gw3, gs, gx, genc = scatter_and_rows(
+        (gw1, gw2, gw3, small_grads), HEAD_ORDERS, (gx, genc), "scatter_heads"
+    )
     return (
         out.reshape(inputs.shape),
         gx.reshape(inputs.shape).astype(F32),

time: 585 us -> 512 us (0.88)
  waiting for transfers between devices: 35.4 us -> 0.01 us
  Pallas kernels: 474 us -> 449 us
  other arithmetic: 23.6 us -> 15.2 us
    ppermute x4 -> x3, waiting for transfers between devices: 35.4 us -> 0.01 us  [rows_along_tp(): lax.ppermute(own, 'tp', [(i, (i + k) % DEPTH) for i in range(DEPTH)])]
    pallas_call x3, Pallas kernels: 373 us -> 348 us  [comm_call(): pl.pallas_call(kernel, out_shape=outs, in_specs=in_specs, out_specs=out_s...]
    convert_element_type x4 -> x0, other arithmetic: 7.56 us -> none  [the longest x2 3.89 us: share_rows(): return total.astype(LOW)]
    unnamed x47 -> x54, local copies, waits for them, and re-layouts: 13.3 us -> 8.26 us
  transfers between devices with their start and end apart: 4 -> 3, of which waited for: 2 -> 0; matrix products, arithmetic and copies ran while one was open for 3% -> 5% of each run, Pallas kernels for 0% -> 49%
where the time goes in v2:
time: 512 us; the launch traced here: 506 us
  Pallas kernels  449 us (88%)
  local copies, waits for them, and re-layouts  27.3 us (5%)
  other arithmetic  15.2 us (3%)
  starting transfers between devices  7.67 us (1%)
  matrix products  5.34 us (1%)
    pallas_call x3, Pallas kernels, comm_call(): pl.pallas_call(kernel, out_shape=outs, in_specs=in_specs, out_specs=out_s...  348 us
    pallas_call x6, Pallas kernels, run_heads(): pl.pallas_call(kernel, grid=(steps,), in_specs=specs, out_specs=out_specs...  101 us
  transfers between devices with their start and end apart: 3, of which 0 were waited for; matrix products, arithmetic and copies ran while one was open for 5% of the time, Pallas kernels for 49%

profile of v2, /device:TPU:12, one launch (start us, length us, event | category | flops | bytes accessed | tf_op | source)
XLA Modules:
  0.0 505.5 jit_solution(15887230489390263553)
XLA Ops:
  0.7 1.8 copy.45.refs_0_
  2.5 1.7 copy.46.refs_1_
  4.2 1.7 copy.47.refs_2_
  6.0 0.8 convert_element_type.198
  8.1 2.4 dynamic-slice_bitcast_fusion.refs_7_
  10.5 2.1 dynamic-slice_bitcast_fusion.2
  14.0 140.8 %gather_weights.1 = (bf16[4,1024,704]{2,1,0:T(8,128)(2,1)}, bf16[4,1024,704]{2,1,0:T(8,128)(2,1)}, bf16[4,1024,704]{2,1,0:T(8,128)(2,1)}, bf16[4,1024,512]{2,1,0...) custom-call(bf16[128,704]{1,0:T(8,128)(2,1)} %copy.45.refs_0_, ...), custom_call_target="tpu_custom_call" | custom-call | tf_op jit(solution)/shard_map/gather_weights/pallas_call | solution.py:891
  154.8 0.9 slice.73
  155.8 0.8 slice.74
  158.1 1.2 dynamic_slice.38
  160.0 1.2 pad_add_fusion.info
  161.2 21.2 %self_forward.1 = (f32[256,1024]{1,0:T(8,128)}, bf16[256,1024]{1,0:T(8,128)(2,1)}, bf16[4,256,256]{2,1,0:T(8,128)(2,1)}, bf16[4,1024,256]{2,1,0:T(8,128)(2,1)}, ...) custom-call(s32[2]{0:T(128)} %pad_add_fusion.info, f32[32,16]{1,0:T(8,128)} %reshape.196.table, ...), custom_call_target="tpu_custom_call" | custom-call | flops 5000000000 | bytes 23640072 | tf_op jit(solution)/shard_map/self_forward/pallas_call | solution.py:1316
  182.4 13.0 %cross_forward.1 = (f32[256,1024]{1,0:T(8,128)}, bf16[256,1024]{1,0:T(8,128)(2,1)}, bf16[4,256,256]{2,1,0:T(8,128)(2,1)}, bf16[4,512,256]{2,1,0:T(8,128)(2,1)}, ...) custom-call(f32[256,1024]{1,0:T(8,128)} %get-tuple-element.72.x2_ref, bf16[512,1024]{1,0:T(8,128)(2,1)} %bitcast.97, ...), custom_call_target="tpu_custom_call" | custom-call | flops 3000000000 | bytes 18354176 | tf_op jit(solution)/shard_map/cross_forward/pallas_call | solution.py:1316
  195.4 23.8 %feed.1 = (bf16[256,1024]{1,0:T(8,128)(2,1)}, f32[256,1024]{1,0:T(8,128)}, bf16[4,1024,704]{2,1,0:T(8,128)(2,1)}, bf16[4,1024,704]{2,1,0:T(8,128)(2,1)}, bf16[4,...) custom-call(s32[2]{0:T(128)} %pad_add_fusion.info, f32[256,1024]{1,0:T(8,128)} %get-tuple-element.75.x3_ref, ...), custom_call_target="tpu_custom_call" | custom-call | flops 12999999488 | bytes 37756936 | tf_op jit(solution)/shard_map/feed/pallas_call | solution.py:1316
  219.2 1.6 collective-permute-start
  220.9 5.4 %collective-permute-start.1 = (bf16[256,1024]{1,0:T(8,128)(2,1)}, bf16[256,1024]{1,0:T(8,128)(2,1)}, u32[]{:S(2)}, u32[]{:S(2)}) collective-permute-start(bf16[256,1024]{1,0:T(8,128)(2,1)} %get-tuple-element.79), channel_id=1, source_target_pairs={{0,2},{1,3},{2,0},{3,1},{4,6},{5,7},{6,4},{7,5},{8,10},{9,11},{10,... | collective-permute-start | bytes 1572872 | tf_op jit(solution)/shard_map/ppermute | solution.py:1460
  228.2 2.0 dynamic-slice_bitcast_fusion.1.x_ref
  230.1 1.7 dynamic-slice_bitcast_fusion.4.enc_ref
  231.9 15.1 %cross_backward.1 = (f32[256,1024]{1,0:T(8,128)}, bf16[4,512,256]{2,1,0:T(8,128)(2,1)}, bf16[4,1024,512]{2,1,0:T(8,128)(2,1)}, f32[1,1024]{1,0:T(1,128)}) custom-call(f32[256,1024]{1,0:T(8,128)} %get-tuple-element.80.g3_ref, f32[256,1024]{1,0:T(8,128)} %get-tuple-element.72.x2_ref, bf16[256,1024]{1,0:T(8,128)(2,1)} %get-tuple-element.81.h_ref, ...), custom_call_target="tpu_custom_call" | custom-call | flops 5000000000 | bytes 19406848 | tf_op jit(solution)/shard_map/cross_backward/pallas_call | solution.py:1316
  247.0 19.6 %self_backward.1 = (f32[256,1024]{1,0:T(8,128)}, bf16[4,1024,256]{2,1,0:T(8,128)(2,1)}, bf16[4,1024,512]{2,1,0:T(8,128)(2,1)}, f32[4,4,8,1280]{3,2,1,0:T(8,128)}) custom-call(f32[256,1024]{1,0:T(8,128)} %get-tuple-element.86.g2_ref, bf16[256,1024]{1,0:T(8,128)(2,1)} %get-tuple-element.87.h_ref, bf16[4,1024,512]{2,1,0:T(8,128)(2,1)} %get-tuple-element.70.w_ref, ...), custom_call_target="tpu_custom_call" | custom-call | flops 6000000000 | bytes 25296896 | tf_op jit(solution)/shard_map/self_backward/pallas_call | solution.py:1316
  266.6 119.6 %scatter_feed.1 = (f32[128,704]{1,0:T(8,128)}, f32[128,704]{1,0:T(8,128)}, f32[128,704]{1,0:T(8,128)}, bf16[4,256,256]{2,1,0:T(8,128)(2,1)}, bf16[4,128,256]{2,1,0:T(8,128)(2,1)}) custom-call(bf16[4,1024,704]{2,1,0:T(8,128)(2,1)} %get-tuple-element.95.refs_0_, bf16[4,1024,704]{2,1,0:T(8,128)(2,1)} %get-tuple-element.96.refs_1_, ...), custom_call_target="tpu_custom_call" | custom-call | tf_op jit(solution)/shard_map/scatter_feed/pallas_call | solution.py:891
  386.3 8.5 %last_grads.1 = (bf16[256,1024]{1,0:T(8,128)(2,1)}, bf16[128,1024]{1,0:T(8,128)(2,1)}, bf16[4,1024,512]{2,1,0:T(8,128)(2,1)}, f32[1,1024]{1,0:T(1,128)}) custom-call(f32[256,1024]{1,0:T(8,128)} %get-tuple-element.94.dh_part_ref, bf16[4,256,256]{2,1,0:T(8,128)(2,1)} %get-tuple-element.100.dkv_ref, bf16[256,1024]{1,0:T(8,128)(2,1)} %dynamic-slice_bitcast_fusion.1.x_ref, ...), custom_call_target="tpu_custom_call" | custom-call | flops 3000000000 | bytes 17571840 | tf_op jit(solution)/shard_map/last_grads/pallas_call | solution.py:1316
  395.5 5.3 %fusion.3 = f32[4,8,4,4]{1,3,0,2:T(4,128)S(1)} fusion(f32[4,4,1280,8]{2,3,1,0:T(8,128)S(1)} %bitcast.98, s32[8,4]{0,1:T(4,128)S(1)} %copy-done.20, s32[1280,8]{0,1:T(8,128)S(1)} %copy-done.13), kind=kOutput, calls=%fused_computation.6 | convolution fusion | flops 63242240 | bytes 698496 | tf_op jit(solution)/shard_map/hrm,rmb->bh/dot_general | solution.py:1521
  401.7 87.2 %scatter_heads.1 = (f32[128,512]{1,0:T(8,128)}, f32[128,512]{1,0:T(8,128)}, f32[128,512]{1,0:T(8,128)}, f32[16,128]{1,0:T(8,128)}, bf16[4,256,1024]{2,1,0:T(8,128)(2,1)}, /*index=5*/bf16[4,128,1024]{2,1,0:T(8,128)(2,1)}) custom-call(bf16[4,1024,512]{2,1,0:T(8,128)(2,1)} %get-tuple-element.92.refs_0_, bf16[4,1024,512]{2,1,0:T(8,128)(2,1)} %get-tuple-element.93.refs_1_, ...), custom_call_target="tpu_custom_call" | custom-call | tf_op jit(solution)/shard_map/scatter_heads/pallas_call | solution.py:891
  489.0 2.9 bitcast_convert_fusion.1
  495.4 0.9 copy.56
  496.3 0.9 copy.57
  497.2 0.9 copy.58
  498.2 1.3 slice_bitcast_fusion
  499.5 2.5 bitcast_convert_fusion
  502.0 1.6 pad_maximum_fusion
  503.8 1.6 pad_maximum_fusion.1
  (75 shorter events, 12.3 us)
Async XLA Ops:
  0.7 9.8 %copy-start.1 = (bf16[2,256,1024]{2,1,0:T(8,128)(2,1)S(1)}, bf16[2,256,1024]{2,1,0:T(8,128)(2,1)}, u32[]{:S(2)}) copy-start(bf16[2,256,1024]{2,1,0:T(8,128)(2,1)} %param.20) | copy-start | bytes 3145732
  8.0 4.5 copy-start.9
  8.0 4.5 copy-start.10
  8.0 4.5 copy-start.11
  8.0 4.5 copy-start.12
  8.1 5.2 %copy-start.14 = (bf16[128,128]{1,0:T(8,128)(2,1)S(1)}, bf16[128,128]{1,0:T(8,128)(2,1)}, u32[]{:S(2)}) copy-start(bf16[128,128]{1,0:T(8,128)(2,1)} %param.32) | copy-start | bytes 98308
  8.1 5.2 %copy-start.15 = (bf16[128,128]{1,0:T(8,128)(2,1)S(1)}, bf16[128,128]{1,0:T(8,128)(2,1)}, u32[]{:S(2)}) copy-start(bf16[128,128]{1,0:T(8,128)(2,1)} %param.31) | copy-start | bytes 98308
  8.1 5.2 %copy-start.16 = (bf16[128,128]{1,0:T(8,128)(2,1)S(1)}, bf16[128,128]{1,0:T(8,128)(2,1)}, u32[]{:S(2)}) copy-start(bf16[128,128]{1,0:T(8,128)(2,1)} %param.26) | copy-start | bytes 98308
  8.1 5.2 %copy-start.17 = (bf16[128,128]{1,0:T(8,128)(2,1)S(1)}, bf16[128,128]{1,0:T(8,128)(2,1)}, u32[]{:S(2)}) copy-start(bf16[128,128]{1,0:T(8,128)(2,1)} %param.25) | copy-start | bytes 98308
  219.2 282.7 %collective-permute-start = (bf16[256,1024]{1,0:T(8,128)(2,1)}, bf16[256,1024]{1,0:T(8,128)(2,1)}, u32[]{:S(2)}, u32[]{:S(2)}) collective-permute-start(bf16[256,1024]{1,0:T(8,128)(2,1)} %get-tuple-element.79), channel_id=1, source_target_pairs={{0,1},{1,2},{2,3},{3,0},{4,5},{5,6},{6,7},{7,4},{8,9},{9,10},{10,1... | collective-permute-start | bytes 1572872 | tf_op jit(solution)/shard_map/ppermute | solution.py:1460
  220.9 281.1 %collective-permute-start.1 = (bf16[256,1024]{1,0:T(8,128)(2,1)}, bf16[256,1024]{1,0:T(8,128)(2,1)}, u32[]{:S(2)}, u32[]{:S(2)}) collective-permute-start(bf16[256,1024]{1,0:T(8,128)(2,1)} %get-tuple-element.79), channel_id=1, source_target_pairs={{0,2},{1,3},{2,0},{3,1},{4,6},{5,7},{6,4},{7,5},{8,10},{9,11},{10,... | collective-permute-start | bytes 1572872 | tf_op jit(solution)/shard_map/ppermute | solution.py:1460
  226.2 275.7 %collective-permute-start.2 = (bf16[256,1024]{1,0:T(8,128)(2,1)}, bf16[256,1024]{1,0:T(8,128)(2,1)}, u32[]{:S(2)}, u32[]{:S(2)}) collective-permute-start(bf16[256,1024]{1,0:T(8,128)(2,1)} %get-tuple-element.79), channel_id=1, source_target_pairs={{0,3},{1,0},{2,1},{3,2},{4,7},{5,4},{6,5},{7,6},{8,11},{9,8},{10,9... | collective-permute-start | bytes 1572872 | tf_op jit(solution)/shard_map/ppermute | solution.py:1460
  386.2 8.5 %copy-start.18 = (f32[1,1024]{1,0:T(1,128)S(1)}, f32[1,1024]{1,0:T(1,128)}, u32[]{:S(2)}) copy-start(f32[1,1024]{1,0:T(1,128)} %get-tuple-element.105) | copy-start | bytes 12292
  386.2 8.5 %copy-start.19 = (f32[1,1024]{1,0:T(1,128)S(1)}, f32[1,1024]{1,0:T(1,128)}, u32[]{:S(2)}) copy-start(f32[1,1024]{1,0:T(1,128)} %get-tuple-element.104) | copy-start | bytes 12292
  386.3 9.2 %copy-start.13 = (s32[1280,8]{0,1:T(8,128)S(1)}, s32[1280,8]{0,1:T(8,128)}, u32[]{:S(2)}) copy-start(s32[1280,8]{0,1:T(8,128)} %compare_select_fusion) | copy-start | bytes 122884
  386.3 9.2 %copy-start.20 = (s32[8,4]{0,1:T(4,128)S(1)}, s32[8,4]{0,1:T(4,128)}, u32[]{:S(2)}) copy-start(s32[8,4]{0,1:T(4,128)} %multiply_add_fusion) | copy-start | bytes 388
  386.3 9.2 %copy-start.21 = (f32[4,4,8,1280]{3,2,1,0:T(8,128)S(1)}, f32[4,4,8,1280]{3,2,1,0:T(8,128)}, u32[]{:S(2)}) copy-start(f32[4,4,8,1280]{3,2,1,0:T(8,128)} %get-tuple-element.106) | copy-start | bytes 1966084
  489.0 3.0 copy-start.8
  489.0 3.7 copy-start.7
  489.0 4.4 copy-start.6
  489.0 6.4 %copy-start.5 = (f32[128,704]{1,0:T(8,128)S(1)}, f32[128,704]{1,0:T(8,128)}, u32[]{:S(2)}) copy-start(f32[128,704]{1,0:T(8,128)} %get-tuple-element.151) | copy-start | bytes 1081348
  489.0 7.3 %copy-start.4 = (f32[128,704]{1,0:T(8,128)S(1)}, f32[128,704]{1,0:T(8,128)}, u32[]{:S(2)}) copy-start(f32[128,704]{1,0:T(8,128)} %get-tuple-element.152) | copy-start | bytes 1081348
  491.9 5.3 %copy-start.3 = (f32[128,704]{1,0:T(8,128)S(1)}, f32[128,704]{1,0:T(8,128)}, u32[]{:S(2)}) copy-start(f32[128,704]{1,0:T(8,128)} %get-tuple-element.153) | copy-start | bytes 1081348
  491.9 7.5 %copy-start = (bf16[4,256,1024]{2,1,0:T(8,128)(2,1)S(1)}, bf16[4,256,1024]{2,1,0:T(8,128)(2,1)}, u32[]{:S(2)}) copy-start(bf16[4,256,1024]{2,1,0:T(8,128)(2,1)} %get-tuple-element.109) | copy-start | bytes 6291460
  499.5 2.5 copy-start.2

commit v3 on v2

--- a/solution.py
+++ b/solution.py
@@ -565,20 +565,21 @@
             self.ins[j], self.slot(j, self.me, self.place.c), self.local_sem.at[j]
         )
 
-    def start(self, first=()):
-        count = len(self.orders)
-        turn = list(first) + [j for j in range(count) if j not in first]
+    def start(self, which=None):
+        which = range(len(self.orders)) if which is None else which
         for stage in range(2):
-            for j in turn:
+            for j in which:
                 for link in self.routes(j, -1, 0):
                     if (link[0] == "c") == (stage == 1):
                         when(self.place.has(link), self.copy(j, self.me, link, True).start)
-        for j in range(count):
+        for j in which:
             self.local(j).start()
 
-    def steps(self):
+    def steps(self, wanted=None):
         for e, (k, hops, j, src, d) in enumerate(self.arrivals):
             xyz = self.place.source(src)
+            if wanted is not None and not wanted(j, k):
+                continue
 
             def step(k=k, j=j, d=d, xyz=xyz, src=src):
                 def run():
@@ -590,21 +591,9 @@
 
             yield (e + 1) / len(self.arrivals), step
 
-    def finish(self):
-        count = len(self.orders)
-        for j in range(count):
+    def settle(self, which):
+        for j in which:
             self.local(j).wait()
-            for link in self.routes(j, -1, 0):
-                when(self.place.has(link), self.copy(j, self.me, link, True).wait_send)
-        for k, hops, j, src, d in self.arrivals:
-            xyz = self.place.source(src)
-
-            def run():
-                for link in self.routes(j, k, d):
-                    when(self.place.has(link), self.copy(j, xyz, link, False).wait_send)
-
-            when(self.place.exists(src), run)
-        for j in range(count):
             if len(self.orders[j]) == 3:
 
                 def from_core(i, carry):
@@ -618,6 +607,23 @@
                     return carry
 
                 lax.fori_loop(0, 4 * DEPTH, from_core, 0)
+
+    def sent(self):
+        for j in range(len(self.orders)):
+            for link in self.routes(j, -1, 0):
+                when(self.place.has(link), self.copy(j, self.me, link, True).wait_send)
+        for k, hops, j, src, d in self.arrivals:
+            xyz = self.place.source(src)
+
+            def run():
+                for link in self.routes(j, k, d):
+                    when(self.place.has(link), self.copy(j, xyz, link, False).wait_send)
+
+            when(self.place.exists(src), run)
+
+    def finish(self):
+        self.settle(range(len(self.orders)))
+        self.sent()
 
 
 def child_slots(order):
@@ -905,26 +911,6 @@
     if len(order) == 1:
         return jax.ShapeDtypeStruct((SIZES[order],) + a.shape, a.dtype)
     return jax.ShapeDtypeStruct((DEPTH, 8 * a.shape[0], a.shape[1]), a.dtype)
-
-
-def gather(arrays, orders, name):
-    count = len(arrays)
-    rows = [a.shape[0] for a in arrays]
-
-    def kernel(*refs):
-        place = Place()
-        ins, outs, sems = refs[:count], refs[count : 2 * count], refs[2 * count :]
-        plan = Gather(place, orders, rows, ins, outs, sems)
-        greet(place)
-        plan.start()
-        run_steps([(plan, 0.0, 1.0)])
-        plan.finish()
-
-    return comm_call(
-        kernel, name, 1, arrays, [INSIDE] * count,
-        [gathered(a, o) for a, o in zip(arrays, orders)], [HBM] * count,
-        Gather.scratch(count),
-    )
 
 
 def scattered(arrays):
@@ -1082,24 +1068,8 @@
     return jnp.transpose(qt_ref[...]).astype(jnp.bfloat16)
 
 
-def self_forward_kernel(
-    info, table, x_ref, gain_ref, w_ref, wkv_ref, bucket_ref,
-    x2_ref, h_ref, q_ref, kv_ref, p_ref, o_ref,
-    h1_ref, s_ref, strip_ref, ot_ref,
-):
-    first = pl.multiple_of(info[0], QROWS)
-    length = info[1]
-
-    @pl.when(pl.program_id(0) == 0)
-    def _():
-        for c in range(KEYS // QROWS):
-            rows = pl.ds(c * QROWS, QROWS)
-            h1_ref[rows, :] = norm_rows(
-                x_ref[rows, :].astype(jnp.float32), gain_ref[...]
-            ).astype(jnp.bfloat16)
-        x2_ref[...] = x_ref[pl.ds(first, QROWS), :].astype(jnp.float32)
-        h_ref[...] = h1_ref[pl.ds(first, QROWS), :]
-
+def self_step(first, length, h1_ref, w_ref, wkv_ref, near_of, q_ref, kv_ref, p_ref, o_ref, work):
+    s_ref, strip_ref, ot_ref = work
     kv = mm(h1_ref[...], wkv_ref[0]).astype(jnp.bfloat16)
     kv_ref[0] = kv
     q = mm(h1_ref[pl.ds(first, QROWS), :], w_ref[0, :, :QROWS]).astype(jnp.bfloat16)
@@ -1111,11 +1081,7 @@
     def add_bias(a, c, s):
         if c is None:
             for b in range(2):
-                head = pl.program_id(0) * 4 + 2 * a + b
-                bucket = bucket_ref[...]
-                near = jnp.full((8, SPAN), table[BUCKETS - 1, head], jnp.float32)
-                for i in range(BUCKETS - 1):
-                    near = jnp.where(bucket == i, table[i, head], near)
+                near = near_of(2 * a + b)
                 for g in range(16):
                     shift = (SPAN - (120 - 8 * g)) % SPAN
                     strip_ref[b, 8 * g : 8 * g + 8, :] = (
@@ -1129,26 +1095,18 @@
 
     o = attend(q, kv, p_ref, s_ref, ot_ref, KEYS, add_bias)
     o_ref[0] = o
-    x2_ref[...] += mm(o, w_ref[0, :, QROWS:], LAST)
-
-
-def cross_forward_kernel(
-    x2_ref, enc_ref, gain_ref, w_ref, wkv_ref,
-    x3_ref, h_ref, q_ref, kv_ref, p_ref, o_ref,
-    s_ref, ot_ref,
-):
-    @pl.when(pl.program_id(0) == 0)
-    def _():
-        x3_ref[...] = x2_ref[...]
-        h_ref[...] = norm_rows(x2_ref[...], gain_ref[...]).astype(jnp.bfloat16)
-
-    kv = mm(enc_ref[...], wkv_ref[0]).astype(jnp.bfloat16)
+    return mm(o, w_ref[0, :, QROWS:], LAST)
+
+
+def cross_step(h_ref, enc, w_ref, wkv_ref, q_ref, kv_ref, p_ref, o_ref, work):
+    s_ref, ot_ref = work
+    kv = mm(enc, wkv_ref[0]).astype(jnp.bfloat16)
     kv_ref[0] = kv
     q = mm(h_ref[...], w_ref[0, :, :QROWS]).astype(jnp.bfloat16)
     q_ref[0] = q
     o = attend(q, kv, p_ref, s_ref, ot_ref, ENC_ROWS, None)
     o_ref[0] = o
-    x3_ref[...] += mm(o, w_ref[0, :, QROWS:], LAST)
+    return mm(o, w_ref[0, :, QROWS:], LAST)
 
 
 def feed_kernel(
@@ -1332,39 +1290,6 @@
     return jax.ShapeDtypeStruct(shape, dtype)
 
 
-def self_forward(info, x, gain, w1, w3, table, bucket):
-    return run_heads(
-        self_forward_kernel, "self_forward",
-        (info, table, x, gain, w1, w3, bucket),
-        [SCALARS, SCALARS, whole((KEYS, WIDTH)), whole((1, WIDTH)), part((1, WIDTH, 512)),
-         part((1, WIDTH, 256)), whole((8, SPAN))],
-        [shape_of((QROWS, WIDTH), F32), shape_of((QROWS, WIDTH), LOW),
-         shape_of((4, QROWS, 256), LOW), shape_of((4, KEYS, 256), LOW),
-         shape_of((4, 2, KEYS, 512), LOW), shape_of((4, QROWS, 256), LOW)],
-        [whole((QROWS, WIDTH)), whole((QROWS, WIDTH)), part((1, QROWS, 256)),
-         part((1, KEYS, 256)), part((1, 2, KEYS, 512)), part((1, QROWS, 256))],
-        [pltpu.VMEM((KEYS, WIDTH), LOW), pltpu.VMEM((KEYS, 512), F32),
-         pltpu.VMEM((2, CHUNK, SPAN), F32), pltpu.VMEM((256, QROWS), F32)],
-        5 * 10**9,
-    )
-
-
-def cross_forward(x2, enc, gain, w2, w3):
-    return run_heads(
-        cross_forward_kernel, "cross_forward",
-        (x2, enc, gain, w2, w3),
-        [whole((QROWS, WIDTH)), whole((ENC_ROWS, WIDTH)), whole((1, WIDTH)),
-         part((1, WIDTH, 512)), part((1, WIDTH, 256), 1)],
-        [shape_of((QROWS, WIDTH), F32), shape_of((QROWS, WIDTH), LOW),
-         shape_of((4, QROWS, 256), LOW), shape_of((4, ENC_ROWS, 256), LOW),
-         shape_of((4, 2, ENC_ROWS, 512), LOW), shape_of((4, QROWS, 256), LOW)],
-        [whole((QROWS, WIDTH)), whole((QROWS, WIDTH)), part((1, QROWS, 256)),
-         part((1, ENC_ROWS, 256)), part((1, 2, ENC_ROWS, 512)), part((1, QROWS, 256))],
-        [pltpu.VMEM((ENC_ROWS, 512), F32), pltpu.VMEM((256, QROWS), F32)],
-        3 * 10**9,
-    )
-
-
 def feed(info, x3, cot, gain, wg, wu, wo):
     units = wg.shape[2]
     wide = part((1, WIDTH, units))
@@ -1441,11 +1366,144 @@
     )
 
 
-GATHER_ORDERS = ("yzx", "yzx", "zxy", "yxz", "zxy", "zxy", "zxy")
+GATHER_ORDERS = ("zyx", "zyx", "xzy", "yzx", "zxy", "yzx", "zxy", "y", "y")
+SMALL_ROWS = 16
+LANES = 128
+
+
+def split_steps(steps, parts, low, high):
+    ends = [int(len(steps) * (low + (high - low) * (i + 1) / parts)) for i in range(parts)]
+    return [steps[a:b] for a, b in zip([0] + ends, ends)], steps[ends[-1] :]
+
+
+def at_step(t, chunks):
+    for i, chunk in enumerate(chunks):
+
+        def run():
+            for step in chunk:
+                step()
+
+        if chunk:
+            pl.when(t == i)(run)
+
+
+def forward_kernel(rows, *refs):
+    lengths, ins = refs[0], refs[1:10]
+    weights, refs = refs[10:16], refs[16:]
+    gains_ref, x2_ref, x3_ref, h1_out, h2_ref = refs[:5]
+    q1_out, kv1_out, p1_out, o1_out, q2_out, kv2_out, p2_out, o2_out = refs[5:13]
+    small, x_all, enc_all, bucket_ref, h1_ref, s_ref, strip_ref, ot_ref = refs[13:21]
+    place = Place()
+    plan = Gather(place, GATHER_ORDERS, rows, ins, weights + (small, x_all, enc_all), refs[21:])
+    greet(place)
+    half = lax.rem(place.z, 2)
+    first = pl.multiple_of(place.y * (2 * QROWS) + half * QROWS, QROWS)
+    length = lengths[lax.div(place.z, 2)]
+    plan.start(range(3, 9))
+    row = lax.broadcasted_iota(jnp.int32, (8, SPAN), 0)
+    col = lax.broadcasted_iota(jnp.int32, (8, SPAN), 1)
+    bucket_ref[...] = bucket_index(jnp.maximum(first + col - (SPAN - 264) - row, 0))
+    for _, step in plan.steps(lambda j, k: 3 <= j < 7 and k < 2):
+        step()
+    plan.start(range(3))
+    for _, step in plan.steps(lambda j, k: j >= 7 or (j >= 3 and k == 2)):
+        step()
+    plan.settle(range(3, 9))
+    feed_steps = [step for _, step in plan.steps(lambda j, k: j < 3)]
+    chunks, rest = split_steps(feed_steps, 8, 0.0, 0.7)
+
+    for k in range(3):
+        gains_ref[pl.ds(k, 1), :] = jnp.concatenate(
+            [small[0, pl.ds(r * SMALL_ROWS + k, 1), :] for r in range(8)], axis=1
+        )
+    gain = gains_ref[pl.ds(0, 1), :]
+    for y in range(2):
+        for c in range(2):
+            at = pl.ds(c * QROWS, QROWS)
+            h1_ref[pl.ds(y * 512 + c * QROWS, QROWS), :] = norm_rows(
+                x_all[y, at, :].astype(jnp.float32), gain
+            ).astype(jnp.bfloat16)
+    x2_ref[...] = ins[7][pl.ds(half * QROWS, QROWS), :].astype(jnp.float32)
+    h1_out[...] = h1_ref[pl.ds(first, QROWS), :]
+
+    def self_body(w_ref, wkv_ref, q_ref, kv_ref, p_ref, o_ref):
+        t = pl.program_id(0)
+
+        def near_of(head):
+            rows_of = [small[t, pl.ds(r * SMALL_ROWS + 3, 1), :] for r in range(8)]
+            bucket = bucket_ref[...]
+            near = jnp.zeros((8, SPAN), jnp.float32)
+            for i in range(BUCKETS):
+                lane = (i % 4) * 4 + head
+                value = rows_of[i // 4][:, lane : lane + 1]
+                near = jnp.where(bucket == i, value, near)
+            return near
+
+        x2_ref[...] += self_step(
+            first, length, h1_ref, w_ref, wkv_ref, near_of, q_ref, kv_ref, p_ref, o_ref,
+            (s_ref, strip_ref, ot_ref),
+        )
+        at_step(t, chunks[:4])
+
+    pltpu.emit_pipeline(
+        self_body,
+        grid=(4,),
+        in_specs=[part((1, WIDTH, 512)), part((1, WIDTH, 256))],
+        out_specs=[
+            part((1, QROWS, 256)), part((1, KEYS, 256)), part((1, 2, KEYS, 512)),
+            part((1, QROWS, 256)),
+        ],
+    )(weights[3], weights[5], q1_out, kv1_out, p1_out, o1_out)
+    x3_ref[...] = x2_ref[...]
+    h2_ref[...] = norm_rows(x2_ref[...], gains_ref[pl.ds(1, 1), :]).astype(jnp.bfloat16)
+
+    def cross_body(w_ref, wkv_ref, q_ref, kv_ref, p_ref, o_ref):
+        enc = jnp.concatenate([enc_all[0], enc_all[1]], axis=0)
+        x3_ref[...] += cross_step(
+            h2_ref, enc, w_ref, wkv_ref, q_ref, kv_ref, p_ref, o_ref, (s_ref, ot_ref)
+        )
+        at_step(pl.program_id(0), chunks[4:])
+
+    pltpu.emit_pipeline(
+        cross_body,
+        grid=(4,),
+        in_specs=[part((1, WIDTH, 512)), part((1, WIDTH, 256), 1)],
+        out_specs=[
+            part((1, QROWS, 256)), part((1, ENC_ROWS, 256)), part((1, 2, ENC_ROWS, 512)),
+            part((1, QROWS, 256)),
+        ],
+    )(weights[4], weights[5], q2_out, kv2_out, p2_out, o2_out)
+    for step in rest:
+        step()
+    plan.settle(range(3))
+    plan.sent()
+
+
+def forward(lengths, arrays):
+    rows = [a.shape[0] for a in arrays]
+    wide = [gathered(a, o) for a, o in zip(arrays, GATHER_ORDERS)]
+    vm = pltpu.VMEM
+    return comm_call(
+        functools.partial(forward_kernel, rows), "forward", 1,
+        (lengths,) + tuple(arrays), [SCALARS] + [INSIDE] * 9,
+        wide[:6]
+        + [shape_of((8, WIDTH), F32), shape_of((QROWS, WIDTH), F32),
+           shape_of((QROWS, WIDTH), F32), shape_of((QROWS, WIDTH), LOW),
+           shape_of((QROWS, WIDTH), LOW),
+           shape_of((4, QROWS, 256), LOW), shape_of((4, KEYS, 256), LOW),
+           shape_of((4, 2, KEYS, 512), LOW), shape_of((4, QROWS, 256), LOW),
+           shape_of((4, QROWS, 256), LOW), shape_of((4, ENC_ROWS, 256), LOW),
+           shape_of((4, 2, ENC_ROWS, 512), LOW), shape_of((4, QROWS, 256), LOW)],
+        [HBM] * 6 + [INSIDE] * 5 + [HBM] * 8,
+        [vm(w.shape, w.dtype) for w in wide[6:]]
+        + [vm((8, SPAN), jnp.int32), vm((KEYS, WIDTH), LOW), vm((KEYS, 512), F32),
+           vm((2, CHUNK, SPAN), F32), vm((256, QROWS), F32)]
+        + Gather.scratch(9),
+    )
+
+
 FEED_ORDERS = ("xzy", "zyx", "yzx")
 HEAD_ORDERS = ("zyx", "zxy", "zyx", "zxy")
-SMALL_ROWS = 16
-LANES = 128
 
 
 def small_rows(gains, table):
@@ -1489,23 +1547,14 @@
         small_rows((norm_self, norm_cross, norm_feed), bias_table),
         x_seq, enc_seq,
     )
-    wg, wu, wo, w1, w2, w3, small, x_all, enc_all = gather(
-        packed, GATHER_ORDERS + ("y", "y"), "gather_weights"
-    )
-    small = small.reshape(4, 8, SMALL_ROWS, LANES)
-    gains = jnp.transpose(small[0, :, :3], (1, 0, 2)).reshape(3, 1, WIDTH)
-    table = jnp.transpose(
-        small[:, :, 3, :16].reshape(4, 8, 4, 4), (1, 2, 0, 3)
-    ).reshape(BUCKETS, 16)
-    x_all = x_all.reshape(KEYS, WIDTH)
-    enc_all = enc_all.reshape(ENC_ROWS, WIDTH)
-
+    (
+        wg, wu, wo, w1, w2, w3, gains, x2, x3, h1, h2, q1, kv1, p1, o1, q2, kv2, p2, o2,
+    ) = forward(lengths, packed)
+    gains = gains[:3].reshape(3, 1, WIDTH)
     distance = jnp.maximum(
         first + jnp.arange(SPAN)[None, :] - (SPAN - 264) - jnp.arange(8)[:, None], 0
     )
     bucket = bucket_index(distance)
-    x2, h1, q1, kv1, p1, o1 = self_forward(info, x_all, gains[0], w1, w3, table, bucket)
-    x3, h2, q2, kv2, p2, o2 = cross_forward(x2, enc_all, gains[1], w2, w3)
     out, g3, gg, gu, go, gn3 = feed(info, x3, cot, gains[2], wg, wu, wo)
     out = rows_along_tp(out, t)
     g2, dkv2, gw2, gn2 = cross_backward(g3, x2, h2, gains[1], w2, q2, kv2, p2, o2)

time: 512 us -> 488 us (0.953)
  Pallas kernels: 449 us -> 424 us
    pallas_call x6 -> x4, Pallas kernels: 101 us -> 67.1 us  [run_heads(): pl.pallas_call(kernel, grid=(steps,), in_specs=specs, out_specs=out_specs...]
    pallas_call x3, Pallas kernels: 348 us -> 357 us  [comm_call(): pl.pallas_call(kernel, out_shape=outs, in_specs=in_specs, out_specs=out_s...]
  transfers between devices with their start and end apart: 3 -> 3, of which waited for: 0 -> 0; matrix products, arithmetic and copies ran while one was open for 5% -> 5% of each run, Pallas kernels for 49% -> 52%
where the time goes in v3:
time: 488 us; the launch traced here: 478 us
  Pallas kernels  424 us (87%)
  local copies, waits for them, and re-layouts  24.9 us (5%)
  other arithmetic  14.5 us (3%)
  starting transfers between devices  7.76 us (2%)
  matrix products  5.33 us (1%)
    pallas_call x3, Pallas kernels, comm_call(): pl.pallas_call(kernel, out_shape=outs, in_specs=in_specs, out_specs=out_s...  357 us
    pallas_call x4, Pallas kernels, run_heads(): pl.pallas_call(kernel, grid=(steps,), in_specs=specs, out_specs=out_specs...  67.1 us
  transfers between devices with their start and end apart: 3, of which 0 were waited for; matrix products, arithmetic and copies ran while one was open for 5% of the time, Pallas kernels for 52%

profile of v3, /device:TPU:12, one launch (start us, length us, event | category | flops | bytes accessed | tf_op | source)
XLA Modules:
  0.0 478.4 jit_solution(15847085730389651668)
XLA Ops:
  0.7 1.8 copy.44.refs_1_
  2.5 1.7 copy.45.refs_2_
  4.3 1.7 copy.46.refs_3_
  6.0 0.8 convert_element_type.168
  8.1 2.4 dynamic-slice_bitcast_fusion.refs_8_
  11.1 2.1 dynamic-slice_bitcast_fusion.2
  13.2 0.7 pad_maximum_fusion.2
  14.6 151.2 %forward.1 = (bf16[4,1024,704]{2,1,0:T(8,128)(2,1)}, bf16[4,1024,704]{2,1,0:T(8,128)(2,1)}, bf16[4,1024,704]{2,1,0:T(8,128)(2,1)}, bf16[4,1024,512]{2,1,0:T(8,12...) custom-call(s32[2]{0:T(128)} %refs_0_.1, ...), custom_call_target="tpu_custom_call" | custom-call | tf_op jit(solution)/shard_map/forward/pallas_call | solution.py:897
  165.8 1.5 fusion.30
  167.2 1.2 pad_add_fusion.info
  168.5 23.6 %feed.1 = (bf16[256,1024]{1,0:T(8,128)(2,1)}, f32[256,1024]{1,0:T(8,128)}, bf16[4,1024,704]{2,1,0:T(8,128)(2,1)}, bf16[4,1024,704]{2,1,0:T(8,128)(2,1)}, bf16[4,...) custom-call(s32[2]{0:T(128)} %pad_add_fusion.info, f32[256,1024]{1,0:T(8,128)} %get-tuple-element.66.x3_ref, ...), custom_call_target="tpu_custom_call" | custom-call | flops 12999999488 | bytes 37756936 | tf_op jit(solution)/shard_map/feed/pallas_call | solution.py:1274
  192.1 3.0 collective-permute-start.2
  195.1 4.8 collective-permute-start.1
  201.0 2.0 dynamic-slice_bitcast_fusion.1.x_ref
  203.0 1.7 dynamic-slice_bitcast_fusion.4.enc_ref
  204.7 15.4 %cross_backward.1 = (f32[256,1024]{1,0:T(8,128)}, bf16[4,512,256]{2,1,0:T(8,128)(2,1)}, bf16[4,1024,512]{2,1,0:T(8,128)(2,1)}, f32[1,1024]{1,0:T(1,128)}) custom-call(f32[256,1024]{1,0:T(8,128)} %get-tuple-element.72.g3_ref, f32[256,1024]{1,0:T(8,128)} %get-tuple-element.73.x2_ref, bf16[256,1024]{1,0:T(8,128)(2,1)} %get-tuple-element.74.h_ref, ...), custom_call_target="tpu_custom_call" | custom-call | flops 5000000000 | bytes 19406848 | tf_op jit(solution)/shard_map/cross_backward/pallas_call | solution.py:1274
  220.1 19.6 %self_backward.1 = (f32[256,1024]{1,0:T(8,128)}, bf16[4,1024,256]{2,1,0:T(8,128)(2,1)}, bf16[4,1024,512]{2,1,0:T(8,128)(2,1)}, f32[4,4,8,1280]{3,2,1,0:T(8,128)}) custom-call(f32[256,1024]{1,0:T(8,128)} %get-tuple-element.80.g2_ref, bf16[256,1024]{1,0:T(8,128)(2,1)} %get-tuple-element.81.h_ref, bf16[4,1024,512]{2,1,0:T(8,128)(2,1)} %get-tuple-element.82.w_ref, ...), custom_call_target="tpu_custom_call" | custom-call | flops 6000000000 | bytes 25296896 | tf_op jit(solution)/shard_map/self_backward/pallas_call | solution.py:1274
  239.7 119.2 %scatter_feed.1 = (f32[128,704]{1,0:T(8,128)}, f32[128,704]{1,0:T(8,128)}, f32[128,704]{1,0:T(8,128)}, bf16[4,256,256]{2,1,0:T(8,128)(2,1)}, bf16[4,128,256]{2,1,0:T(8,128)(2,1)}) custom-call(bf16[4,1024,704]{2,1,0:T(8,128)(2,1)} %get-tuple-element.90.refs_0_, bf16[4,1024,704]{2,1,0:T(8,128)(2,1)} %get-tuple-element.91.refs_1_, ...), custom_call_target="tpu_custom_call" | custom-call | tf_op jit(solution)/shard_map/scatter_feed/pallas_call | solution.py:897
  358.9 8.4 %last_grads.1 = (bf16[256,1024]{1,0:T(8,128)(2,1)}, bf16[128,1024]{1,0:T(8,128)(2,1)}, bf16[4,1024,512]{2,1,0:T(8,128)(2,1)}, f32[1,1024]{1,0:T(1,128)}) custom-call(f32[256,1024]{1,0:T(8,128)} %get-tuple-element.89.dh_part_ref, bf16[4,256,256]{2,1,0:T(8,128)(2,1)} %get-tuple-element.95.dkv_ref, bf16[256,1024]{1,0:T(8,128)(2,1)} %dynamic-slice_bitcast_fusion.1.x_ref, ...), custom_call_target="tpu_custom_call" | custom-call | flops 3000000000 | bytes 17571840 | tf_op jit(solution)/shard_map/last_grads/pallas_call | solution.py:1274
  368.3 5.3 %fusion.3 = f32[4,8,4,4]{1,3,0,2:T(4,128)S(1)} fusion(f32[4,4,1280,8]{2,3,1,0:T(8,128)S(1)} %bitcast.73, s32[8,4]{0,1:T(4,128)S(1)} %copy-done.20, s32[1280,8]{0,1:T(8,128)S(1)} %compare_select_fusion), kind=kOutput, calls=%fused_computation.6 | convolution fusion | flops 63242240 | bytes 698496 | tf_op jit(solution)/shard_map/hrm,rmb->bh/dot_general | solution.py:1570
  373.7 0.7 pad.23
  374.5 87.1 %scatter_heads.1 = (f32[128,512]{1,0:T(8,128)}, f32[128,512]{1,0:T(8,128)}, f32[128,512]{1,0:T(8,128)}, f32[16,128]{1,0:T(8,128)}, bf16[4,256,1024]{2,1,0:T(8,128)(2,1)}, /*index=5*/bf16[4,128,1024]{2,1,0:T(8,128)(2,1)}) custom-call(bf16[4,1024,512]{2,1,0:T(8,128)(2,1)} %get-tuple-element.87.refs_0_, bf16[4,1024,512]{2,1,0:T(8,128)(2,1)} %get-tuple-element.88.refs_1_, ...), custom_call_target="tpu_custom_call" | custom-call | tf_op jit(solution)/shard_map/scatter_heads/pallas_call | solution.py:897
  461.6 2.9 bitcast_convert_fusion.1
  464.5 0.7 fusion.27
  465.9 0.7 fusion.29
  468.0 0.9 copy.51
  468.9 0.9 copy.52
  469.8 0.9 copy.53
  470.7 1.3 slice_bitcast_fusion
  472.0 2.5 bitcast_convert_fusion
  474.5 1.6 pad_maximum_fusion
  476.4 1.6 pad_maximum_fusion.1
  (68 shorter events, 7.0 us)
Async XLA Ops:
  0.7 9.8 %copy-start.21 = (s32[2]{0:T(128)S(1)}, s32[2]{0:T(128)}, u32[]{:S(2)}) copy-start(s32[2]{0:T(128)} %refs_0_.1) | copy-start | bytes 28
  0.7 10.4 %copy-start.1 = (bf16[2,256,1024]{2,1,0:T(8,128)(2,1)S(1)}, bf16[2,256,1024]{2,1,0:T(8,128)(2,1)}, u32[]{:S(2)}) copy-start(bf16[2,256,1024]{2,1,0:T(8,128)(2,1)} %param.20) | copy-start | bytes 3145732
  8.1 5.1 %copy-start.9 = (bf16[128,256]{1,0:T(8,128)(2,1)S(1)}, bf16[128,256]{1,0:T(8,128)(2,1)}, u32[]{:S(2)}) copy-start(bf16[128,256]{1,0:T(8,128)(2,1)} %param.27) | copy-start | bytes 196612
  8.1 5.1 %copy-start.10 = (bf16[128,256]{1,0:T(8,128)(2,1)S(1)}, bf16[128,256]{1,0:T(8,128)(2,1)}, u32[]{:S(2)}) copy-start(bf16[128,256]{1,0:T(8,128)(2,1)} %param.24) | copy-start | bytes 196612
  8.1 5.1 %copy-start.11 = (bf16[128,256]{1,0:T(8,128)(2,1)S(1)}, bf16[128,256]{1,0:T(8,128)(2,1)}, u32[]{:S(2)}) copy-start(bf16[128,256]{1,0:T(8,128)(2,1)} %param.33) | copy-start | bytes 196612
  8.1 5.1 %copy-start.12 = (bf16[128,256]{1,0:T(8,128)(2,1)S(1)}, bf16[128,256]{1,0:T(8,128)(2,1)}, u32[]{:S(2)}) copy-start(bf16[128,256]{1,0:T(8,128)(2,1)} %param.30) | copy-start | bytes 196612
  8.1 5.8 %copy-start.14 = (bf16[128,128]{1,0:T(8,128)(2,1)S(1)}, bf16[128,128]{1,0:T(8,128)(2,1)}, u32[]{:S(2)}) copy-start(bf16[128,128]{1,0:T(8,128)(2,1)} %param.32) | copy-start | bytes 98308
  8.1 5.8 %copy-start.15 = (bf16[128,128]{1,0:T(8,128)(2,1)S(1)}, bf16[128,128]{1,0:T(8,128)(2,1)}, u32[]{:S(2)}) copy-start(bf16[128,128]{1,0:T(8,128)(2,1)} %param.31) | copy-start | bytes 98308
  8.1 5.8 %copy-start.16 = (bf16[128,128]{1,0:T(8,128)(2,1)S(1)}, bf16[128,128]{1,0:T(8,128)(2,1)}, u32[]{:S(2)}) copy-start(bf16[128,128]{1,0:T(8,128)(2,1)} %param.26) | copy-start | bytes 98308
  8.1 5.8 %copy-start.17 = (bf16[128,128]{1,0:T(8,128)(2,1)S(1)}, bf16[128,128]{1,0:T(8,128)(2,1)}, u32[]{:S(2)}) copy-start(bf16[128,128]{1,0:T(8,128)(2,1)} %param.25) | copy-start | bytes 98308
  192.1 282.4 %collective-permute-start.2 = (bf16[256,1024]{1,0:T(8,128)(2,1)}, bf16[256,1024]{1,0:T(8,128)(2,1)}, u32[]{:S(2)}, u32[]{:S(2)}) collective-permute-start(bf16[256,1024]{1,0:T(8,128)(2,1)} %get-tuple-element.71), channel_id=1, source_target_pairs={{0,3},{1,0},{2,1},{3,2},{4,7},{5,4},{6,5},{7,6},{8,11},{9,8},{10,9... | collective-permute-start | bytes 1572872 | tf_op jit(solution)/shard_map/ppermute | solution.py:1518
  195.1 279.4 %collective-permute-start = (bf16[256,1024]{1,0:T(8,128)(2,1)}, bf16[256,1024]{1,0:T(8,128)(2,1)}, u32[]{:S(2)}, u32[]{:S(2)}) collective-permute-start(bf16[256,1024]{1,0:T(8,128)(2,1)} %get-tuple-element.71), channel_id=1, source_target_pairs={{0,1},{1,2},{2,3},{3,0},{4,5},{5,6},{6,7},{7,4},{8,9},{9,10},{10,1... | collective-permute-start | bytes 1572872 | tf_op jit(solution)/shard_map/ppermute | solution.py:1518
  195.1 279.4 %collective-permute-start.1 = (bf16[256,1024]{1,0:T(8,128)(2,1)}, bf16[256,1024]{1,0:T(8,128)(2,1)}, u32[]{:S(2)}, u32[]{:S(2)}) collective-permute-start(bf16[256,1024]{1,0:T(8,128)(2,1)} %get-tuple-element.71), channel_id=1, source_target_pairs={{0,2},{1,3},{2,0},{3,1},{4,6},{5,7},{6,4},{7,5},{8,10},{9,11},{10,... | collective-permute-start | bytes 1572872 | tf_op jit(solution)/shard_map/ppermute | solution.py:1518
  358.9 8.5 %copy-start.18 = (f32[1,1024]{1,0:T(1,128)S(1)}, f32[1,1024]{1,0:T(1,128)}, u32[]{:S(2)}) copy-start(f32[1,1024]{1,0:T(1,128)} %get-tuple-element.101) | copy-start | bytes 12292
  358.9 8.5 %copy-start.19 = (f32[1,1024]{1,0:T(1,128)S(1)}, f32[1,1024]{1,0:T(1,128)}, u32[]{:S(2)}) copy-start(f32[1,1024]{1,0:T(1,128)} %get-tuple-element.100) | copy-start | bytes 12292
  358.9 9.2 %copy-start.13 = (s32[1280]{0:T(1024)S(1)}, s32[1280]{0:T(1024)}, u32[]{:S(2)}) copy-start(s32[1280]{0:T(1024)} %add_add_fusion) | copy-start | bytes 15364
  358.9 9.3 %copy-start.20 = (s32[8,4]{0,1:T(4,128)S(1)}, s32[8,4]{0,1:T(4,128)}, u32[]{:S(2)}) copy-start(s32[8,4]{0,1:T(4,128)} %multiply_add_fusion) | copy-start | bytes 388
  358.9 9.3 %copy-start.22 = (f32[4,4,8,1280]{3,2,1,0:T(8,128)S(1)}, f32[4,4,8,1280]{3,2,1,0:T(8,128)}, u32[]{:S(2)}) copy-start(f32[4,4,8,1280]{3,2,1,0:T(8,128)} %get-tuple-element.102) | copy-start | bytes 1966084
  461.6 3.0 copy-start.8
  461.6 3.7 copy-start.7
  461.6 4.4 copy-start.6
  461.6 6.4 %copy-start.5 = (f32[128,704]{1,0:T(8,128)S(1)}, f32[128,704]{1,0:T(8,128)}, u32[]{:S(2)}) copy-start(f32[128,704]{1,0:T(8,128)} %get-tuple-element.147) | copy-start | bytes 1081348
  461.6 7.3 %copy-start.4 = (f32[128,704]{1,0:T(8,128)S(1)}, f32[128,704]{1,0:T(8,128)}, u32[]{:S(2)}) copy-start(f32[128,704]{1,0:T(8,128)} %get-tuple-element.148) | copy-start | bytes 1081348
  464.5 5.3 %copy-start.3 = (f32[128,704]{1,0:T(8,128)S(1)}, f32[128,704]{1,0:T(8,128)}, u32[]{:S(2)}) copy-start(f32[128,704]{1,0:T(8,128)} %get-tuple-element.149) | copy-start | bytes 1081348
  464.5 7.5 %copy-start = (bf16[4,256,1024]{2,1,0:T(8,128)(2,1)S(1)}, bf16[4,256,1024]{2,1,0:T(8,128)(2,1)}, u32[]{:S(2)}) copy-start(bf16[4,256,1024]{2,1,0:T(8,128)(2,1)} %get-tuple-element.105) | copy-start | bytes 6291460
  472.0 2.5 copy-start.2

commit v4 on v3

--- a/solution.py
+++ b/solution.py
@@ -917,32 +917,6 @@
     return [
         jax.ShapeDtypeStruct((a.shape[1] // 8, a.shape[2]), jnp.float32) for a in arrays
     ]
-
-
-def scatter_and_share(arrays, orders, shared, name):
-    n, m = len(arrays), len(shared)
-    rows = [a.shape[1] // 8 for a in arrays]
-    own = [a.shape[1] // 4 for a in shared]
-    room = Scatter.scratch(arrays, rows, orders)
-
-    def kernel(*refs):
-        place = Place()
-        ins, outs, scratch = refs[: n + m], refs[n + m : 2 * (n + m)], refs[2 * (n + m) :]
-        plan = Scatter(place, orders, rows, ins[:n], outs[:n], scratch[: len(room)])
-        share = Share(place, own, ins[n:], outs[n:], scratch[len(room) :])
-        greet(place)
-        share.start()
-        plan.start()
-        run_steps([(plan, 0.0, 80.0), (share, 0.0, 80.0)])
-        share.finish()
-        plan.finish()
-
-    return comm_call(
-        kernel, name, 2, arrays + shared, [HBM] * n + [INSIDE] * m,
-        scattered(arrays)
-        + [jax.ShapeDtypeStruct((4, r, 256), jnp.bfloat16) for r in own],
-        [INSIDE] * (n + m), room + Share.scratch(own),
-    )
 
 
 def scatter_and_rows(arrays, orders, rows_in, name):
@@ -1060,9 +1034,9 @@
             ds_ref[rows, :] = ds.astype(jnp.bfloat16)
         if take_bias is not None:
             take_bias(a, None, None)
-        dkv_ref[0, :, a * 64 : a * 64 + 64] = mm(ds_ref[...], q2).astype(jnp.bfloat16)
+        dkv_ref[0, :, a * 64 : a * 64 + 64] = mm(ds_ref[pl.ds(0, keys), :], q2).astype(jnp.bfloat16)
         dkv_ref[0, :, 128 + a * 64 : 192 + a * 64] = mm(p_ref[0, a], do2).astype(jnp.bfloat16)
-        qt = mm(k, ds_ref[...], ROWS_OF)
+        qt = mm(k, ds_ref[pl.ds(0, keys), :], ROWS_OF)
         qt_ref[a * 128 : a * 128 + 64, :] = qt[:, :QROWS]
         qt_ref[a * 128 + 64 : a * 128 + 128, :] = qt[:, QROWS:]
     return jnp.transpose(qt_ref[...]).astype(jnp.bfloat16)
@@ -1118,7 +1092,7 @@
 
     @pl.when(step == 0)
     def _():
-        h = norm_rows(x3_ref[...], gain_ref[...]).astype(jnp.bfloat16)
+        h = norm_rows(x3_ref[...], gain_ref[pl.ds(2, 1), :]).astype(jnp.bfloat16)
         h_ref[...] = h
         ht_ref[...] = jnp.transpose(h)
         row = lax.broadcasted_iota(jnp.int32, (QROWS, 1), 0) + info[0]
@@ -1150,77 +1124,9 @@
     @pl.when(step == pl.num_programs(0) - 1)
     def _():
         out_ref[...] = y_ref[...].astype(jnp.bfloat16)
-        back, gain_grad = norm_back(x3_ref[...], gain_ref[...], dh_ref[...])
+        back, gain_grad = norm_back(x3_ref[...], gain_ref[pl.ds(2, 1), :], dh_ref[...])
         g3_ref[...] = g_ref[...].astype(jnp.float32) + back
         gn_ref[...] = gain_grad
-
-
-def cross_backward_kernel(
-    g3_ref, x2_ref, h_ref, gain_ref, w_ref, q_ref, kv_ref, p_ref, o_ref,
-    g2_ref, dkv_ref, gw_ref, gn_ref,
-    g_ref, gt_ref, ht_ref, dh_ref, d_ref, ds_ref, qt_ref,
-):
-    step = pl.program_id(0)
-
-    @pl.when(step == 0)
-    def _():
-        g = g3_ref[...].astype(jnp.bfloat16)
-        g_ref[...] = g
-        gt_ref[...] = jnp.transpose(g)
-        ht_ref[...] = jnp.transpose(h_ref[...])
-        dh_ref[...] = jnp.zeros_like(dh_ref)
-
-    do = mm(g_ref[...], w_ref[0, :, QROWS:]).astype(jnp.bfloat16)
-    gw_ref[0, :, QROWS:] = mm(gt_ref[...], o_ref[0]).astype(jnp.bfloat16)
-    dq = attend_back(
-        q_ref[0], kv_ref[0], p_ref, do, dkv_ref, d_ref, ds_ref, qt_ref, ENC_ROWS, None
-    )
-    gw_ref[0, :, :QROWS] = mm(ht_ref[...], dq).astype(jnp.bfloat16)
-    dh_ref[...] += mm(dq, w_ref[0, :, :QROWS], LAST)
-
-    @pl.when(step == pl.num_programs(0) - 1)
-    def _():
-        back, gain_grad = norm_back(x2_ref[...], gain_ref[...], dh_ref[...])
-        g2_ref[...] = g3_ref[...] + back
-        gn_ref[...] = gain_grad
-
-
-def self_backward_kernel(
-    g2_ref, h_ref, w_ref, q_ref, kv_ref, p_ref, o_ref,
-    dh_ref, dkv_ref, gw_ref, near_ref,
-    g_ref, gt_ref, ht_ref, d_ref, ds_ref, qt_ref, strip_ref,
-):
-    @pl.when(pl.program_id(0) == 0)
-    def _():
-        g = g2_ref[...].astype(jnp.bfloat16)
-        g_ref[...] = g
-        gt_ref[...] = jnp.transpose(g)
-        ht_ref[...] = jnp.transpose(h_ref[...])
-        dh_ref[...] = jnp.zeros_like(dh_ref)
-
-    def take_bias(a, c, ds):
-        if c is None:
-            for b in range(2):
-                total = jnp.zeros((8, SPAN), jnp.float32)
-                for g in range(16):
-                    part = strip_ref[b, 8 * g : 8 * g + 8, :]
-                    shift = 120 - 8 * g
-                    total = total + (pltpu.roll(part, shift, 1) if shift else part)
-                near_ref[0, 2 * a + b] = total
-            return
-        if c == 0:
-            strip_ref[...] = jnp.zeros_like(strip_ref)
-        cols = pl.ds(CHUNK * (7 - c), QROWS)
-        strip_ref[0, :, cols] += ds[:, :QROWS]
-        strip_ref[1, :, cols] += ds[:, QROWS:]
-
-    do = mm(g_ref[...], w_ref[0, :, QROWS:]).astype(jnp.bfloat16)
-    gw_ref[0, :, QROWS:] = mm(gt_ref[...], o_ref[0]).astype(jnp.bfloat16)
-    dq = attend_back(
-        q_ref[0], kv_ref[0], p_ref, do, dkv_ref, d_ref, ds_ref, qt_ref, KEYS, take_bias
-    )
-    gw_ref[0, :, :QROWS] = mm(ht_ref[...], dq).astype(jnp.bfloat16)
-    dh_ref[...] += mm(dq, w_ref[0, :, :QROWS], LAST)
 
 
 def last_kernel(
@@ -1247,9 +1153,9 @@
     @pl.when(step == pl.num_programs(0) - 1)
     def _():
         back, gain_grad = norm_back(
-            x_ref[...].astype(jnp.float32), gain_ref[...], dh_ref[...]
+            x_ref[...].astype(jnp.float32), gain_ref[pl.ds(0, 1), :], dh_ref[...]
         )
-        gx_ref[...] = (g2_ref[...] + back).astype(jnp.bfloat16)
+        gx_ref[...] = (g2_ref[pl.ds(0, QROWS), :] + back).astype(jnp.bfloat16)
         genc_ref[...] = de_ref[...].astype(jnp.bfloat16)
         gn_ref[...] = gain_grad
 
@@ -1296,7 +1202,7 @@
     return run_heads(
         feed_kernel, "feed",
         (info, x3, cot, gain, wg, wu, wo),
-        [SCALARS, whole((QROWS, WIDTH)), whole((QROWS, WIDTH)), whole((1, WIDTH)),
+        [SCALARS, whole((QROWS, WIDTH)), whole((QROWS, WIDTH)), whole((8, WIDTH)),
          wide, wide, wide],
         [shape_of((QROWS, WIDTH), LOW), shape_of((QROWS, WIDTH), F32)]
         + [shape_of((4, WIDTH, units), LOW)] * 3
@@ -1309,51 +1215,13 @@
     )
 
 
-def cross_backward(g3, x2, h, gain, w2, q, kv, p, o):
-    return run_heads(
-        cross_backward_kernel, "cross_backward",
-        (g3, x2, h, gain, w2, q, kv, p, o),
-        [whole((QROWS, WIDTH)), whole((QROWS, WIDTH)), whole((QROWS, WIDTH)),
-         whole((1, WIDTH)), part((1, WIDTH, 512)), part((1, QROWS, 256)),
-         part((1, ENC_ROWS, 256)), part((1, 2, ENC_ROWS, 512)), part((1, QROWS, 256))],
-        [shape_of((QROWS, WIDTH), F32), shape_of((4, ENC_ROWS, 256), LOW),
-         shape_of((4, WIDTH, 512), LOW), shape_of((1, WIDTH), F32)],
-        [whole((QROWS, WIDTH)), part((1, ENC_ROWS, 256)), part((1, WIDTH, 512)),
-         whole((1, WIDTH))],
-        [pltpu.VMEM((QROWS, WIDTH), LOW), pltpu.VMEM((WIDTH, QROWS), LOW),
-         pltpu.VMEM((WIDTH, QROWS), LOW), pltpu.VMEM((QROWS, WIDTH), F32),
-         pltpu.VMEM((ENC_ROWS, 512), F32), pltpu.VMEM((ENC_ROWS, 512), LOW),
-         pltpu.VMEM((256, QROWS), F32)],
-        5 * 10**9,
-    )
-
-
-def self_backward(g2, h, w1, q, kv, p, o):
-    return run_heads(
-        self_backward_kernel, "self_backward",
-        (g2, h, w1, q, kv, p, o),
-        [whole((QROWS, WIDTH)), whole((QROWS, WIDTH)), part((1, WIDTH, 512)),
-         part((1, QROWS, 256)), part((1, KEYS, 256)), part((1, 2, KEYS, 512)),
-         part((1, QROWS, 256))],
-        [shape_of((QROWS, WIDTH), F32), shape_of((4, KEYS, 256), LOW),
-         shape_of((4, WIDTH, 512), LOW), shape_of((4, 4, 8, SPAN), F32)],
-        [whole((QROWS, WIDTH)), part((1, KEYS, 256)), part((1, WIDTH, 512)),
-         part((1, 4, 8, SPAN))],
-        [pltpu.VMEM((QROWS, WIDTH), LOW), pltpu.VMEM((WIDTH, QROWS), LOW),
-         pltpu.VMEM((WIDTH, QROWS), LOW), pltpu.VMEM((KEYS, 512), F32),
-         pltpu.VMEM((KEYS, 512), LOW), pltpu.VMEM((256, QROWS), F32),
-         pltpu.VMEM((2, CHUNK, SPAN), F32)],
-        6 * 10**9,
-    )
-
-
 def last_grads(dh, dkv, x, h, gain, g2, w3, dkvc, enc):
     rows = enc.shape[0]
     return run_heads(
         last_kernel, "last_grads",
         (dh, dkv, x, h, gain, g2, w3, w3, dkvc, enc),
         [whole((QROWS, WIDTH)), part((1, QROWS, 256)), whole((QROWS, WIDTH)),
-         whole((QROWS, WIDTH)), whole((1, WIDTH)), whole((QROWS, WIDTH)),
+         whole((QROWS, WIDTH)), whole((8, WIDTH)), whole((QROWS + 8, WIDTH)),
          part((1, WIDTH, 256)), part((1, WIDTH, 256), 1), part((1, rows, 256)),
          whole((rows, WIDTH))],
         [shape_of((QROWS, WIDTH), LOW), shape_of((rows, WIDTH), LOW),
@@ -1502,7 +1370,129 @@
     )
 
 
-FEED_ORDERS = ("xzy", "zyx", "yzx")
+FEED_ORDERS = ("zxy", "zyx", "zyx")
+
+
+def backward_kernel(rows, own, room, *refs):
+    grads, refs = refs[:3], refs[3:]
+    out_ref, g3_ref, x2_ref, h2_ref, h1_ref, gains_ref = refs[:6]
+    w1, w2, q1, kv1, p1, o1, q2, kv2, p2, o2 = refs[6:16]
+    shards, refs = refs[16:19], refs[19:]
+    dkv1_out, dkv2_out, rows_out, g2_ref, dh_ref, near_ref, gw1, gw2 = refs[:8]
+    dkv1, dkv2, g_ref, gt_ref, ht_ref, dc_ref, d_ref, ds_ref, qt_ref, strip_ref = refs[8:18]
+    scratch = refs[18:]
+    place = Place()
+    plan = Scatter(place, FEED_ORDERS, rows, grads, shards, scratch[: len(room)])
+    scratch = scratch[len(room) :]
+    share = Share(place, own, (dkv1, dkv2), (dkv1_out, dkv2_out), scratch[:8])
+    lines = Gather(place, ("z",), (QROWS,), (out_ref,), (rows_out,), scratch[8:])
+    greet(place)
+    lines.start()
+    plan.start()
+    steps = [step for _, step in plan.steps()]
+    begin = len(steps) // 10
+    for step in steps[:begin]:
+        step()
+    chunks, rest = split_steps(steps[begin:], 8, 0.0, 0.6)
+
+    def load_grad(ref, h_ref):
+        g = ref[...].astype(jnp.bfloat16)
+        g_ref[...] = g
+        gt_ref[...] = jnp.transpose(g)
+        ht_ref[...] = jnp.transpose(h_ref[...])
+
+    def heads(t, w_ref, q_ref, kv_ref, p_ref, o_ref, gw_ref, dkv, d_sum, keys, take_bias):
+        do = mm(g_ref[...], w_ref[0, :, QROWS:]).astype(jnp.bfloat16)
+        gw_ref[0, :, QROWS:] = mm(gt_ref[...], o_ref[0]).astype(jnp.bfloat16)
+        dq = attend_back(
+            q_ref[0], kv_ref[0], p_ref, do, dkv.at[pl.ds(t, 1)], d_ref, ds_ref, qt_ref, keys,
+            take_bias,
+        )
+        gw_ref[0, :, :QROWS] = mm(ht_ref[...], dq).astype(jnp.bfloat16)
+        d_sum[...] += mm(dq, w_ref[0, :, :QROWS], LAST)
+
+    def specs(keys):
+        return [
+            part((1, WIDTH, 512)), part((1, QROWS, 256)), part((1, keys, 256)),
+            part((1, 2, keys, 512)), part((1, QROWS, 256)),
+        ]
+
+    load_grad(g3_ref, h2_ref)
+    dc_ref[...] = jnp.zeros_like(dc_ref)
+
+    def cross_body(w_ref, q_ref, kv_ref, p_ref, o_ref, gw_ref):
+        t = pl.program_id(0)
+        heads(t, w_ref, q_ref, kv_ref, p_ref, o_ref, gw_ref, dkv2, dc_ref, ENC_ROWS, None)
+        at_step(t, chunks[:4])
+
+    pltpu.emit_pipeline(
+        cross_body, grid=(4,), in_specs=specs(ENC_ROWS), out_specs=[part((1, WIDTH, 512))]
+    )(w2, q2, kv2, p2, o2, gw2)
+    back, gain_grad = norm_back(x2_ref[...], gains_ref[pl.ds(1, 1), :], dc_ref[...])
+    g2_ref[pl.ds(0, QROWS), :] = g3_ref[...] + back
+    g2_ref[pl.ds(QROWS, 1), :] = gain_grad
+    load_grad(g2_ref.at[pl.ds(0, QROWS)], h1_ref)
+    dh_ref[...] = jnp.zeros_like(dh_ref)
+
+    def self_body(w_ref, q_ref, kv_ref, p_ref, o_ref, gw_ref):
+        t = pl.program_id(0)
+
+        def take_bias(a, c, ds):
+            if c is None:
+                for b in range(2):
+                    total = jnp.zeros((8, SPAN), jnp.float32)
+                    for g in range(16):
+                        piece = strip_ref[b, 8 * g : 8 * g + 8, :]
+                        shift = 120 - 8 * g
+                        total = total + (pltpu.roll(piece, shift, 1) if shift else piece)
+                    near_ref[t, 2 * a + b] = total
+                return
+            if c == 0:
+                strip_ref[...] = jnp.zeros_like(strip_ref)
+            cols = pl.ds(CHUNK * (7 - c), QROWS)
+            strip_ref[0, :, cols] += ds[:, :QROWS]
+            strip_ref[1, :, cols] += ds[:, QROWS:]
+
+        heads(t, w_ref, q_ref, kv_ref, p_ref, o_ref, gw_ref, dkv1, dh_ref, KEYS, take_bias)
+        at_step(t, chunks[4:])
+
+    pltpu.emit_pipeline(
+        self_body, grid=(4,), in_specs=specs(KEYS), out_specs=[part((1, WIDTH, 512))]
+    )(w1, q1, kv1, p1, o1, gw1)
+    share.start()
+    ordered = [(i / max(len(rest), 1), step) for i, step in enumerate(rest)]
+    ordered += [(0.05 + 0.9 * at, step) for at, step in share.steps()]
+    ordered += [(0.1 * at, step) for at, step in lines.steps()]
+    ordered.sort(key=lambda s: s[0])
+    for _, step in ordered:
+        step()
+    lines.finish()
+    share.finish()
+    plan.finish()
+
+
+def backward(grads, out, g3, x2, h2, h1, gains, w1, w2, saved1, saved2):
+    rows = [a.shape[1] // 8 for a in grads]
+    own = [KEYS // 4, ENC_ROWS // 4]
+    room = Scatter.scratch(grads, rows, FEED_ORDERS)
+    vm = pltpu.VMEM
+    return comm_call(
+        functools.partial(backward_kernel, rows, own, room), "backward", 2,
+        tuple(grads) + (out, g3, x2, h2, h1, gains, w1, w2) + tuple(saved1) + tuple(saved2),
+        [HBM] * 3 + [INSIDE] * 6 + [HBM] * 10,
+        scattered(grads)
+        + [shape_of((4, r, 256), LOW) for r in own]
+        + [gathered(out, "z"), shape_of((QROWS + 8, WIDTH), F32), shape_of((QROWS, WIDTH), F32),
+           shape_of((4, 4, 8, SPAN), F32), shape_of(w1.shape, LOW), shape_of(w2.shape, LOW)],
+        [INSIDE] * 5 + [HBM] + [INSIDE] * 3 + [HBM] * 2,
+        [vm((4, KEYS, 256), LOW), vm((4, ENC_ROWS, 256), LOW), vm((QROWS, WIDTH), LOW),
+         vm((WIDTH, QROWS), LOW), vm((WIDTH, QROWS), LOW), vm((QROWS, WIDTH), F32),
+         vm((KEYS, 512), F32), vm((KEYS, 512), LOW), vm((256, QROWS), F32),
+         vm((2, CHUNK, SPAN), F32)]
+        + room + Share.scratch(own) + Gather.scratch(1),
+    )
+
+
 HEAD_ORDERS = ("zyx", "zxy", "zyx", "zxy")
 
 
@@ -1510,16 +1500,6 @@
     flat = jnp.pad(table.reshape(1, -1).astype(F32), ((0, 0), (0, LANES - table.size)))
     rows = jnp.concatenate([g.reshape(1, LANES).astype(F32) for g in gains] + [flat], axis=0)
     return jnp.pad(rows, ((0, SMALL_ROWS - 4), (0, 0)))
-
-
-def rows_along_tp(own, t):
-    found = [own]
-    for k in range(1, DEPTH):
-        found.append(lax.ppermute(own, "tp", [(i, (i + k) % DEPTH) for i in range(DEPTH)]))
-    found = jnp.stack(found)
-    return jnp.stack(
-        [lax.dynamic_index_in_dim(found, (t - i + DEPTH) % DEPTH, 0, False) for i in range(DEPTH)]
-    )
 
 
 def tokens_split(
@@ -1550,21 +1530,18 @@
     (
         wg, wu, wo, w1, w2, w3, gains, x2, x3, h1, h2, q1, kv1, p1, o1, q2, kv2, p2, o2,
     ) = forward(lengths, packed)
-    gains = gains[:3].reshape(3, 1, WIDTH)
     distance = jnp.maximum(
         first + jnp.arange(SPAN)[None, :] - (SPAN - 264) - jnp.arange(8)[:, None], 0
     )
     bucket = bucket_index(distance)
-    out, g3, gg, gu, go, gn3 = feed(info, x3, cot, gains[2], wg, wu, wo)
-    out = rows_along_tp(out, t)
-    g2, dkv2, gw2, gn2 = cross_backward(g3, x2, h2, gains[1], w2, q2, kv2, p2, o2)
-    dh, dkv1, gw1, near = self_backward(g2, h1, w1, q1, kv1, p1, o1)
-    gg, gu, go, dkv, dkvc = scatter_and_share(
-        (gg, gu, go), FEED_ORDERS, (dkv1, dkv2), "scatter_feed"
-    )
+    out, g3, gg, gu, go, gn3 = feed(info, x3, cot, gains, wg, wu, wo)
+    gg, gu, go, dkv, dkvc, out, g2, dh, near, gw1, gw2 = backward(
+        (gg, gu, go), out, g3, x2, h2, h1, gains, w1, w2, (q1, kv1, p1, o1), (q2, kv2, p2, o2)
+    )
+    gn2 = g2[QROWS : QROWS + 1]
     enc_own = lax.dynamic_slice_in_dim(enc_seq, half * (QROWS // 2), QROWS // 2, 0)
     gx, genc, gw3, gn1 = last_grads(
-        dh, dkv, x_own, h1, gains[0], g2, w3, dkvc, enc_own
+        dh, dkv, x_own, h1, gains, g2, w3, dkvc, enc_own
     )
     one_hot = (bucket[:, :, None] == jnp.arange(BUCKETS, dtype=jnp.int32)).astype(F32)
     grad_table = jnp.einsum(

time: 488 us -> 458 us (0.939)
  the two profiles are of different devices: /device:TPU:12 before, /device:TPU:10 now
where the time goes in v4:
time: 458 us; the launch traced here: 449 us
  Pallas kernels  409 us (89%)
  local copies, waits for them, and re-layouts  22.7 us (5%)
  other arithmetic  9.85 us (2%)
  matrix products  5.33 us (1%)
    pallas_call x3, Pallas kernels, comm_call(): pl.pallas_call(kernel, out_shape=outs, in_specs=in_specs, out_specs=out_s...  377 us
    pallas_call x2, Pallas kernels, run_heads(): pl.pallas_call(kernel, grid=(steps,), in_specs=specs, out_specs=out_specs...  32.1 us

profile of v4, /device:TPU:10, one launch (start us, length us, event | category | flops | bytes accessed | tf_op | source)
XLA Modules:
  0.0 448.7 jit_solution(11374533586405633681)
XLA Ops:
  0.8 2.4 dynamic-slice_bitcast_fusion.2
  3.3 2.3 dynamic-slice_bitcast_fusion.refs_8_
  5.6 0.7 pad_maximum_fusion
  6.3 0.8 copy.44.refs_1_
  7.1 0.8 copy.45.refs_2_
  7.9 0.8 copy.46.refs_3_
  8.8 0.7 pad_maximum_fusion.2.refs_6_
  10.2 151.2 %forward.1 = (bf16[4,1024,704]{2,1,0:T(8,128)(2,1)}, bf16[4,1024,704]{2,1,0:T(8,128)(2,1)}, bf16[4,1024,704]{2,1,0:T(8,128)(2,1)}, bf16[4,1024,512]{2,1,0:T(8,12...) custom-call(s32[2]{0:T(128)} %refs_0_.1, ...), custom_call_target="tpu_custom_call" | custom-call | tf_op jit(solution)/shard_map/forward/pallas_call | solution.py:897
  161.4 1.2 dynamic_slice.25
  162.6 1.2 pad_add_fusion.info
  163.9 23.6 %feed.1 = (bf16[256,1024]{1,0:T(8,128)(2,1)}, f32[256,1024]{1,0:T(8,128)}, bf16[4,1024,704]{2,1,0:T(8,128)(2,1)}, bf16[4,1024,704]{2,1,0:T(8,128)(2,1)}, bf16[4,...) custom-call(s32[2]{0:T(128)} %pad_add_fusion.info, f32[256,1024]{1,0:T(8,128)} %get-tuple-element.64.x3_ref, ...), custom_call_target="tpu_custom_call" | custom-call | flops 12999999488 | bytes 37785608 | tf_op jit(solution)/shard_map/feed/pallas_call | solution.py:1180
  187.5 138.0 %backward.1 = (f32[128,704]{1,0:T(8,128)}, f32[128,704]{1,0:T(8,128)}, f32[128,704]{1,0:T(8,128)}, bf16[4,256,256]{2,1,0:T(8,128)(2,1)}, bf16[4,128,256]{2,1,0:T...) custom-call(bf16[4,1024,704]{2,1,0:T(8,128)(2,1)} %get-tuple-element, ...), custom_call_target="tpu_custom_call" | custom-call | tf_op jit(solution)/shard_map/backward/pallas_call | solution.py:897
  325.5 2.0 dynamic-slice_bitcast_fusion.1.x_ref
  327.5 1.7 dynamic-slice_bitcast_fusion.4.enc_ref
  329.2 8.5 %last_grads.1 = (bf16[256,1024]{1,0:T(8,128)(2,1)}, bf16[128,1024]{1,0:T(8,128)(2,1)}, bf16[4,1024,512]{2,1,0:T(8,128)(2,1)}, f32[1,1024]{1,0:T(1,128)}) custom-call(f32[256,1024]{1,0:T(8,128)} %get-tuple-element.90.dh_part_ref, bf16[4,256,256]{2,1,0:T(8,128)(2,1)} %get-tuple-element.91.dkv_ref, bf16[256,1024]{1,0:T(8,128)(2,1)} %dynamic-slice_bitcast_fusion.1.x_ref, ...), custom_call_target="tpu_custom_call" | custom-call | flops 3000000000 | bytes 17633280 | tf_op jit(solution)/shard_map/last_grads/pallas_call | solution.py:1180
  337.7 0.8 slice.39
  338.4 0.7 maximum_bitcast_fusion
  339.3 5.3 %fusion.3 = f32[4,8,4,4]{1,3,0,2:T(4,128)S(1)} fusion(f32[4,4,1280,8]{2,3,1,0:T(8,128)S(1)} %bitcast.68, s32[8,4]{0,1:T(4,128)S(1)} %multiply_add_fusion, s32[1280,8]{0,1:T(8,128)S(1)} %compare_select_fusion), kind=kOutput, calls=%fused_computation.4 | convolution fusion | flops 63242240 | bytes 698496 | tf_op jit(solution)/shard_map/hrm,rmb->bh/dot_general | solution.py:1547
  344.8 0.7 pad.23
  345.5 88.0 %scatter_heads.1 = (f32[128,512]{1,0:T(8,128)}, f32[128,512]{1,0:T(8,128)}, f32[128,512]{1,0:T(8,128)}, f32[16,128]{1,0:T(8,128)}, bf16[4,256,1024]{2,1,0:T(8,128)(2,1)}, /*index=5*/bf16[4,128,1024]{2,1,0:T(8,128)(2,1)}) custom-call(bf16[4,1024,512]{2,1,0:T(8,128)(2,1)} %get-tuple-element.88.refs_0_, bf16[4,1024,512]{2,1,0:T(8,128)(2,1)} %get-tuple-element.89.refs_1_, ...), custom_call_target="tpu_custom_call" | custom-call | tf_op jit(solution)/shard_map/scatter_heads/pallas_call | solution.py:897
  433.5 4.2 bitcast_convert_fusion
  437.8 1.6 bitcast_convert_fusion.1
  439.3 0.7 fusion.29
  440.0 0.7 fusion.28
  440.8 0.7 fusion.27
  441.5 0.7 slice_reduce_fusion
  442.2 0.7 reshape_squeeze.3
  442.8 1.3 slice_bitcast_fusion
  444.2 0.9 copy.51
  445.1 0.9 copy.52
  446.0 0.9 copy.53
  446.9 1.3 copy.65
  (62 shorter events, 1.0 us)
Async XLA Ops:
  0.7 4.9 %copy-start.12 = (bf16[128,256]{1,0:T(8,128)(2,1)S(1)}, bf16[128,256]{1,0:T(8,128)(2,1)}, u32[]{:S(2)}) copy-start(bf16[128,256]{1,0:T(8,128)(2,1)} %param.24) | copy-start | bytes 196612
  0.7 4.9 %copy-start.11 = (bf16[128,256]{1,0:T(8,128)(2,1)S(1)}, bf16[128,256]{1,0:T(8,128)(2,1)}, u32[]{:S(2)}) copy-start(bf16[128,256]{1,0:T(8,128)(2,1)} %param.27) | copy-start | bytes 196612
  0.7 4.9 %copy-start.14 = (bf16[128,256]{1,0:T(8,128)(2,1)S(1)}, bf16[128,256]{1,0:T(8,128)(2,1)}, u32[]{:S(2)}) copy-start(bf16[128,256]{1,0:T(8,128)(2,1)} %param.30) | copy-start | bytes 196612
  0.7 4.9 %copy-start.13 = (bf16[128,256]{1,0:T(8,128)(2,1)S(1)}, bf16[128,256]{1,0:T(8,128)(2,1)}, u32[]{:S(2)}) copy-start(bf16[128,256]{1,0:T(8,128)(2,1)} %param.33) | copy-start | bytes 196612
  0.7 5.6 %copy-start.8 = (bf16[128,704]{0,1:T(8,128)(2,1)S(1)}, bf16[128,704]{0,1:T(8,128)(2,1)}, u32[]{:S(2)}) copy-start(bf16[128,704]{0,1:T(8,128)(2,1)} %param.35) | copy-start | bytes 540676
  0.7 6.4 %copy-start.9 = (bf16[128,704]{0,1:T(8,128)(2,1)S(1)}, bf16[128,704]{0,1:T(8,128)(2,1)}, u32[]{:S(2)}) copy-start(bf16[128,704]{0,1:T(8,128)(2,1)} %param.36) | copy-start | bytes 540676
  0.7 7.2 %copy-start.10 = (bf16[128,704]{0,1:T(8,128)(2,1)S(1)}, bf16[128,704]{0,1:T(8,128)(2,1)}, u32[]{:S(2)}) copy-start(bf16[128,704]{0,1:T(8,128)(2,1)} %param.37) | copy-start | bytes 540676
  0.7 8.0 %copy-start.18 = (bf16[128,128]{1,0:T(8,128)(2,1)S(1)}, bf16[128,128]{1,0:T(8,128)(2,1)}, u32[]{:S(2)}) copy-start(bf16[128,128]{1,0:T(8,128)(2,1)} %param.25) | copy-start | bytes 98308
  0.7 8.0 %copy-start.17 = (bf16[128,128]{1,0:T(8,128)(2,1)S(1)}, bf16[128,128]{1,0:T(8,128)(2,1)}, u32[]{:S(2)}) copy-start(bf16[128,128]{1,0:T(8,128)(2,1)} %param.26) | copy-start | bytes 98308
  0.8 8.0 %copy-start.16 = (bf16[128,128]{1,0:T(8,128)(2,1)S(1)}, bf16[128,128]{1,0:T(8,128)(2,1)}, u32[]{:S(2)}) copy-start(bf16[128,128]{1,0:T(8,128)(2,1)} %param.31) | copy-start | bytes 98308
  0.8 8.0 %copy-start.15 = (bf16[128,128]{1,0:T(8,128)(2,1)S(1)}, bf16[128,128]{1,0:T(8,128)(2,1)}, u32[]{:S(2)}) copy-start(bf16[128,128]{1,0:T(8,128)(2,1)} %param.32) | copy-start | bytes 98308
  0.8 8.7 %copy-start.24 = (bf16[4,4]{1,0:T(4,128)(2,1)S(1)}, bf16[4,4]{1,0:T(4,128)(2,1)}, u32[]{:S(2)}) copy-start(bf16[4,4]{1,0:T(4,128)(2,1)} %param.28) | copy-start | bytes 100
  0.8 8.8 %copy-start.22 = (bf16[128]{0:T(256)(128)(2,1)S(1)}, bf16[128]{0:T(256)(128)(2,1)}, u32[]{:S(2)}) copy-start(bf16[128]{0:T(256)(128)(2,1)} %param.23) | copy-start | bytes 772
  0.8 8.8 %copy-start.21 = (bf16[128]{0:T(256)(128)(2,1)S(1)}, bf16[128]{0:T(256)(128)(2,1)}, u32[]{:S(2)}) copy-start(bf16[128]{0:T(256)(128)(2,1)} %param.29) | copy-start | bytes 772
  0.8 8.7 %copy-start.20 = (bf16[128]{0:T(256)(128)(2,1)S(1)}, bf16[128]{0:T(256)(128)(2,1)}, u32[]{:S(2)}) copy-start(bf16[128]{0:T(256)(128)(2,1)} %param.34) | copy-start | bytes 772
  329.2 9.2 %copy-start.19 = (f32[1,1024]{1,0:T(1,128)S(1)}, f32[1,1024]{1,0:T(1,128)}, u32[]{:S(2)}) copy-start(f32[1,1024]{1,0:T(1,128)} %get-tuple-element.97) | copy-start | bytes 12292
  329.2 10.1 %copy-start.23 = (f32[4,4,8,1280]{3,2,1,0:T(8,128)S(1)}, f32[4,4,8,1280]{3,2,1,0:T(8,128)}, u32[]{:S(2)}) copy-start(f32[4,4,8,1280]{3,2,1,0:T(8,128)} %get-tuple-element.98) | copy-start | bytes 1966084
  433.5 4.3 copy-start.1
  433.5 5.8 %copy-start.7 = (f32[128,512]{1,0:T(8,128)S(1)}, f32[128,512]{1,0:T(8,128)}, u32[]{:S(2)}) copy-start(f32[128,512]{1,0:T(8,128)} %get-tuple-element.104) | copy-start | bytes 786436
  433.5 6.5 %copy-start.6 = (f32[128,512]{1,0:T(8,128)S(1)}, f32[128,512]{1,0:T(8,128)}, u32[]{:S(2)}) copy-start(f32[128,512]{1,0:T(8,128)} %get-tuple-element.105) | copy-start | bytes 786436
  433.5 7.2 %copy-start.5 = (f32[128,512]{1,0:T(8,128)S(1)}, f32[128,512]{1,0:T(8,128)}, u32[]{:S(2)}) copy-start(f32[128,512]{1,0:T(8,128)} %get-tuple-element.106) | copy-start | bytes 786436
  433.5 10.6 %copy-start.4 = (f32[128,704]{1,0:T(8,128)S(1)}, f32[128,704]{1,0:T(8,128)}, u32[]{:S(2)}) copy-start(f32[128,704]{1,0:T(8,128)} %get-tuple-element.143) | copy-start | bytes 1081348
  437.7 7.3 %copy-start.3 = (f32[128,704]{1,0:T(8,128)S(1)}, f32[128,704]{1,0:T(8,128)}, u32[]{:S(2)}) copy-start(f32[128,704]{1,0:T(8,128)} %get-tuple-element.144) | copy-start | bytes 1081348
  437.8 8.2 %copy-start.2 = (f32[128,704]{1,0:T(8,128)S(1)}, f32[128,704]{1,0:T(8,128)}, u32[]{:S(2)}) copy-start(f32[128,704]{1,0:T(8,128)} %get-tuple-element.145) | copy-start | bytes 1081348
  437.8 9.1 %copy-start = (bf16[4,256,1024]{2,1,0:T(8,128)(2,1)S(1)}, bf16[4,256,1024]{2,1,0:T(8,128)(2,1)}, u32[]{:S(2)}) copy-start(bf16[4,256,1024]{2,1,0:T(8,128)(2,1)} %get-tuple-element.87) | copy-start | bytes 6291460

commit v5 on v4

--- a/solution.py
+++ b/solution.py
@@ -420,6 +420,7 @@
 
 
 MESH = pl.DeviceIdType.MESH
+LANES = 128
 DEPTH = 4
 LINKS = {("x", 0): 0, ("y", 0): 1, ("z", 1): 2, ("z", -1): 3, ("c", 0): 4}
 SIZES = {"x": 2, "y": 2, "z": DEPTH}
@@ -520,6 +521,12 @@
     )
 
 
+def shard(ref, z, r, rows):
+    if ref.shape[1] == rows:
+        return ref.at[z, :, pl.ds(pl.multiple_of(r * LANES, LANES), LANES)]
+    return ref.at[z, pl.ds(pl.multiple_of(r * rows, rows), rows), :]
+
+
 class Gather:
     def __init__(self, place, orders, rows, ins, outs, sems):
         self.place, self.orders, self.rows, self.ins, self.outs = place, orders, rows, ins, outs
@@ -544,8 +551,7 @@
         x, y, z = xyz
         if len(self.orders[j]) == 1:
             return self.outs[j].at[y if self.orders[j] == "y" else z]
-        at = ((x * 2 + c) * 2 + y) * self.rows[j]
-        return self.outs[j].at[z, pl.ds(pl.multiple_of(at, self.rows[j]), self.rows[j]), :]
+        return shard(self.outs[j], z, (x * 2 + c) * 2 + y, self.rows[j])
 
     def copy(self, j, xyz, link, own):
         here = self.slot(j, xyz, self.place.c)
@@ -609,17 +615,40 @@
                 lax.fori_loop(0, 4 * DEPTH, from_core, 0)
 
     def sent(self):
-        for j in range(len(self.orders)):
-            for link in self.routes(j, -1, 0):
-                when(self.place.has(link), self.copy(j, self.me, link, True).wait_send)
-        for k, hops, j, src, d in self.arrivals:
-            xyz = self.place.source(src)
-
-            def run():
-                for link in self.routes(j, k, d):
-                    when(self.place.has(link), self.copy(j, xyz, link, False).wait_send)
-
-            when(self.place.exists(src), run)
+        place = self.place
+        for j, order in enumerate(self.orders):
+
+            def wait(i, carry):
+                xyz = (lax.div(i, 2 * DEPTH), lax.rem(lax.div(i, DEPTH), 2), lax.rem(i, DEPTH))
+                same = {a: xyz["xyz".index(a)] == self.me["xyz".index(a)] for a in "xyz"}
+                if len(order) == 3:
+                    for m, a in enumerate(order):
+                        after = True
+                        for b in order[m + 1 :]:
+                            after = same[b] & after
+                        for link in ((a, 0),) if a != "z" else (("z", 1), ("z", -1)):
+                            if a == "z":
+                                d = link[1]
+                                near = (xyz[2] - place.z) * d <= 0
+                                cond = near & after & place.has(link)
+                            else:
+                                cond = same[a] & after
+                            pl.when(cond)(self.copy(j, xyz, link, False).wait_send)
+                    self.copy(j, xyz, ("c", 0), False).wait_send()
+                elif order == "z":
+                    column = same["x"] & same["y"]
+                    for link in (("z", 1), ("z", -1)):
+                        near = (xyz[2] - place.z) * link[1] <= 0
+                        pl.when(column & near & place.has(link))(
+                            self.copy(j, xyz, link, False).wait_send
+                        )
+                else:
+                    pl.when(same["x"] & same["y"] & same["z"])(
+                        self.copy(j, xyz, (order, 0), False).wait_send
+                    )
+                return carry
+
+            lax.fori_loop(0, 4 * DEPTH, wait, 0)
 
     def finish(self):
         self.settle(range(len(self.orders)))
@@ -645,7 +674,7 @@
 
 
 def add_rows(out, terms, rows):
-    step = min(rows, 16)
+    step = min(rows, 64 if out.shape[-1] <= LANES else 32)
 
     def body(q, carry):
         at = pl.ds(pl.multiple_of(q * step, step), step)
@@ -675,15 +704,13 @@
         self.events.sort(key=lambda e: (-e[0], -e[1]))
 
     @staticmethod
-    def scratch(arrays, rows, orders):
+    def scratch(arrays, orders):
         plans = [child_slots(o)[1] for o in orders]
         count = len(arrays)
         dma = pltpu.SemaphoreType.DMA
 
         def room(slots):
-            return [
-                pltpu.VMEM((n, r, a.shape[2]), a.dtype) for n, r, a in zip(slots, rows, arrays)
-            ]
+            return [pltpu.VMEM((n,) + shard_shape(a), a.dtype) for n, a in zip(slots, arrays)]
 
         full = [4 * DEPTH] * count
         return (
@@ -693,8 +720,7 @@
 
     def slot(self, j, xyz, c):
         x, y, z = xyz
-        at = ((x * 2 + c) * 2 + y) * self.rows[j]
-        return self.ins[j].at[z, pl.ds(pl.multiple_of(at, self.rows[j]), self.rows[j]), :]
+        return shard(self.ins[j], z, (x * 2 + c) * 2 + y, self.rows[j])
 
     def load(self, j, xyz):
         i = number(*xyz)
@@ -750,23 +776,31 @@
         terms = [total, self.gifts[j].at[i]] + [self.kid(j, m, xyz, 0) for m in always]
         add_rows(total if out is None else out, terms, self.rows[j])
 
-    def start(self):
-        for k, hops, j, src, d in self.events:
-            xyz = self.place.source(src)
-
-            def begin():
+    def start(self, which=None):
+        for j in range(len(self.orders)) if which is None else which:
+            order = self.orders[j]
+
+            def begin(e, carry):
+                left = 4 * DEPTH - 1 - e
+                at = {}
+                for a in order:
+                    at[a] = lax.rem(left, SIZES[a])
+                    left = lax.div(left, SIZES[a])
+                xyz = tuple(
+                    lax.rem(self.me["xyz".index(a)] + at[a], SIZES[a]) for a in "xyz"
+                )
                 self.give(j, xyz).start()
                 self.load(j, xyz).start()
-
-            when(self.place.exists(src), begin)
-        for j in range(len(self.orders)):
-            self.give(j, self.me).start()
-            self.load(j, self.me).start()
-
-    def steps(self):
+                return carry
+
+            lax.fori_loop(0, 4 * DEPTH, begin, 0)
+
+    def steps(self, wanted=None):
         count = len(self.events)
         for e, (k, hops, j, src, d) in enumerate(self.events):
             xyz = self.place.source(src)
+            if wanted is not None and not wanted(j):
+                continue
 
             def step(k=k, j=j, d=d, xyz=xyz, src=src):
                 def run():
@@ -777,6 +811,8 @@
 
             yield (e + 1) / (count + 1), step
         for j in range(len(self.orders)):
+            if wanted is not None and not wanted(j):
+                continue
 
             def last(j=j):
                 self.collect(j, self.me, -1, 0, self.outs[j])
@@ -784,16 +820,23 @@
             yield 1.0, last
 
     def finish(self):
-        for k, hops, j, src, d in self.events:
-            xyz = self.place.source(src)
-
-            def run():
-                self.up(j, xyz, k, d).wait_send()
+        me = number(*self.me)
+        for j in range(len(self.orders)):
+
+            def wait(i, carry):
+                xyz = (lax.div(i, 2 * DEPTH), lax.rem(lax.div(i, DEPTH), 2), lax.rem(i, DEPTH))
                 self.give(j, xyz).wait_send()
 
-            when(self.place.exists(src), run)
-        for j in range(len(self.orders)):
-            self.give(j, self.me).wait_send()
+                def sent():
+                    mine = self.sums[j].at[i]
+                    remote(
+                        mine, mine, self.up_sem.at[j, i], self.kid_sem.at[j, 0], self.partner
+                    ).wait_send()
+
+                pl.when(i != me)(sent)
+                return carry
+
+            lax.fori_loop(0, 4 * DEPTH, wait, 0)
 
 
 class Share:
@@ -880,15 +923,6 @@
                 self.late(j, t).wait_send()
 
 
-def run_steps(parts):
-    steps = []
-    for plan, begin, length in parts:
-        steps += [(begin + length * at, step) for at, step in plan.steps()]
-    steps.sort(key=lambda s: s[0])
-    for _, step in steps:
-        step()
-
-
 HBM = pl.BlockSpec(memory_space=pl.ANY)
 INSIDE = pl.BlockSpec(memory_space=pltpu.VMEM)
 
@@ -910,40 +944,19 @@
 def gathered(a, order):
     if len(order) == 1:
         return jax.ShapeDtypeStruct((SIZES[order],) + a.shape, a.dtype)
+    if a.shape[0] > a.shape[1] == LANES:
+        return jax.ShapeDtypeStruct((DEPTH, a.shape[0], 8 * LANES), a.dtype)
     return jax.ShapeDtypeStruct((DEPTH, 8 * a.shape[0], a.shape[1]), a.dtype)
 
 
+def shard_shape(a):
+    if a.shape[2] == 8 * LANES:
+        return (a.shape[1], LANES)
+    return (a.shape[1] // 8, a.shape[2])
+
+
 def scattered(arrays):
-    return [
-        jax.ShapeDtypeStruct((a.shape[1] // 8, a.shape[2]), jnp.float32) for a in arrays
-    ]
-
-
-def scatter_and_rows(arrays, orders, rows_in, name):
-    n, m = len(arrays), len(rows_in)
-    rows = [a.shape[1] // 8 for a in arrays]
-    room = Scatter.scratch(arrays, rows, orders)
-
-    def kernel(*refs):
-        place = Place()
-        ins, outs, scratch = refs[: n + m], refs[n + m : 2 * (n + m)], refs[2 * (n + m) :]
-        plan = Scatter(place, orders, rows, ins[:n], outs[:n], scratch[: len(room)])
-        lines = Gather(
-            place, ["z"] * m, [a.shape[0] for a in rows_in], ins[n:], outs[n:],
-            scratch[len(room) :],
-        )
-        greet(place)
-        lines.start()
-        plan.start()
-        run_steps([(plan, 0.0, 70.0), (lines, 0.0, 60.0)])
-        lines.finish()
-        plan.finish()
-
-    return comm_call(
-        kernel, name, 3, arrays + rows_in, [HBM] * n + [INSIDE] * m,
-        scattered(arrays) + [gathered(a, "z") for a in rows_in],
-        [INSIDE] * n + [HBM] * m, room + Gather.scratch(m),
-    )
+    return [jax.ShapeDtypeStruct(shard_shape(a), jnp.float32) for a in arrays]
 
 
 WIDTH = 1024
@@ -1083,28 +1096,30 @@
     return mm(o, w_ref[0, :, QROWS:], LAST)
 
 
+def here():
+    z = lax.axis_index("tp")
+    half = lax.rem(z, 2)
+    return lax.div(z, 2), half, lax.axis_index("ctx") * (2 * QROWS) + half * QROWS
+
+
 def feed_kernel(
-    info, x3_ref, cot_ref, gain_ref, wg_ref, wu_ref, wo_ref,
+    at, lengths, x3_ref, cot_ref, gain_ref, wg_ref, wu_ref, wo_ref,
     out_ref, g3_ref, gg_ref, gu_ref, go_ref, gn_ref,
-    h_ref, ht_ref, g_ref, gt_ref, y_ref, dh_ref,
+    h_ref, g_ref, y_ref, dh_ref,
 ):
     step = pl.program_id(0)
 
     @pl.when(step == 0)
     def _():
-        h = norm_rows(x3_ref[...], gain_ref[pl.ds(2, 1), :]).astype(jnp.bfloat16)
-        h_ref[...] = h
-        ht_ref[...] = jnp.transpose(h)
-        row = lax.broadcasted_iota(jnp.int32, (QROWS, 1), 0) + info[0]
-        g4 = jnp.where(row < info[1], cot_ref[...].astype(jnp.float32), 0.0)
-        g = g4.astype(jnp.bfloat16)
-        g_ref[...] = g
-        gt_ref[...] = jnp.transpose(g)
+        h_ref[...] = norm_rows(x3_ref[...], gain_ref[pl.ds(2, 1), :]).astype(jnp.bfloat16)
+        row = lax.broadcasted_iota(jnp.int32, (QROWS, 1), 0) + at[2]
+        g4 = jnp.where(row < lengths[at[0]], cot_ref[0].astype(jnp.float32), 0.0)
+        g_ref[...] = g4.astype(jnp.bfloat16)
         y_ref[...] = x3_ref[...]
         dh_ref[...] = jnp.zeros_like(dh_ref)
 
-    gate = mm(h_ref[...], wg_ref[0])
-    up = mm(h_ref[...], wu_ref[0])
+    gate = mm(h_ref[...], wg_ref[0], LAST)
+    up = mm(h_ref[...], wu_ref[0], LAST)
     root = math.sqrt(2.0 / math.pi)
     square = gate * gate
     th = jnp.tanh(root * (gate + 0.044715 * gate * square))
@@ -1112,14 +1127,14 @@
     gelu = gate * half
     slope = half + 0.5 * gate * (1.0 - th * th) * (root * (1.0 + 3 * 0.044715 * square))
     hidden = (gelu * up).astype(jnp.bfloat16)
-    y_ref[...] += mm(hidden, wo_ref[0], LAST)
-    go_ref[0] = mm(gt_ref[...], hidden).astype(jnp.bfloat16)
-    dhid = mm(g_ref[...], wo_ref[0])
+    y_ref[...] += mm(hidden, wo_ref[0])
+    go_ref[0] = mm(hidden, g_ref[...], ROWS_OF).astype(jnp.bfloat16)
+    dhid = mm(g_ref[...], wo_ref[0], LAST)
     dup = (dhid * gelu).astype(jnp.bfloat16)
     dgate = (dhid * up * slope).astype(jnp.bfloat16)
-    gg_ref[0] = mm(ht_ref[...], dgate).astype(jnp.bfloat16)
-    gu_ref[0] = mm(ht_ref[...], dup).astype(jnp.bfloat16)
-    dh_ref[...] += mm(dgate, wg_ref[0], LAST) + mm(dup, wu_ref[0], LAST)
+    gg_ref[0] = mm(dgate, h_ref[...], ROWS_OF).astype(jnp.bfloat16)
+    gu_ref[0] = mm(dup, h_ref[...], ROWS_OF).astype(jnp.bfloat16)
+    dh_ref[...] += mm(dgate, wg_ref[0]) + mm(dup, wu_ref[0])
 
     @pl.when(step == pl.num_programs(0) - 1)
     def _():
@@ -1129,37 +1144,6 @@
         gn_ref[...] = gain_grad
 
 
-def last_kernel(
-    dh_part_ref, dkv_ref, x_ref, h_ref, gain_ref, g2_ref, ws_ref, wc_ref, dkvc_ref, enc_ref,
-    gx_ref, genc_ref, gw_ref, gn_ref,
-    ht_ref, et_ref, dh_ref, de_ref,
-):
-    step = pl.program_id(0)
-
-    @pl.when(step == 0)
-    def _():
-        ht_ref[...] = jnp.transpose(h_ref[...])
-        et_ref[...] = jnp.transpose(enc_ref[...])
-        dh_ref[...] = dh_part_ref[...]
-        de_ref[...] = jnp.zeros_like(de_ref)
-
-    dkv = dkv_ref[0]
-    dkvc = dkvc_ref[0]
-    gw_ref[0, :, :QROWS] = mm(ht_ref[...], dkv).astype(jnp.bfloat16)
-    gw_ref[0, :, QROWS:] = mm(et_ref[...], dkvc).astype(jnp.bfloat16)
-    dh_ref[...] += mm(dkv, ws_ref[0], LAST)
-    de_ref[...] += mm(dkvc, wc_ref[0], LAST)
-
-    @pl.when(step == pl.num_programs(0) - 1)
-    def _():
-        back, gain_grad = norm_back(
-            x_ref[...].astype(jnp.float32), gain_ref[pl.ds(0, 1), :], dh_ref[...]
-        )
-        gx_ref[...] = (g2_ref[pl.ds(0, QROWS), :] + back).astype(jnp.bfloat16)
-        genc_ref[...] = de_ref[...].astype(jnp.bfloat16)
-        gn_ref[...] = gain_grad
-
-
 def whole(shape):
     zeros = (0,) * len(shape)
     return pl.BlockSpec(shape, lambda t: zeros)
@@ -1175,68 +1159,55 @@
 LOW = jnp.bfloat16
 
 
-def run_heads(kernel, name, ins, specs, outs, out_specs, scratch, flops, steps=4):
-    moved = sum(math.prod(a.shape) * a.dtype.itemsize for a in list(ins) + list(outs))
+def shape_of(shape, dtype):
+    return jax.ShapeDtypeStruct(shape, dtype)
+
+
+def feed(at, lengths, x3, cot, gains, wg, wu, wo):
+    units = wg.shape[1]
+
+    def fixed(shape):
+        return pl.BlockSpec(shape, lambda t, at: (0,) * len(shape))
+
+    wide = pl.BlockSpec((1, units, WIDTH), lambda t, at: (t, 0, 0))
+    outs = (
+        [shape_of((QROWS, WIDTH), LOW), shape_of((QROWS, WIDTH), F32)]
+        + [shape_of((4, units, WIDTH), LOW)] * 3
+        + [shape_of((1, WIDTH), F32)]
+    )
     return pl.pallas_call(
-        kernel,
-        grid=(steps,),
-        in_specs=specs,
-        out_specs=out_specs,
+        feed_kernel,
+        grid_spec=pltpu.PrefetchScalarGridSpec(
+            num_scalar_prefetch=1,
+            grid=(4,),
+            in_specs=[
+                SCALARS, fixed((QROWS, WIDTH)),
+                pl.BlockSpec((1, QROWS, WIDTH), lambda t, at: (at[0], at[1], 0)),
+                fixed((8, WIDTH)), wide, wide, wide,
+            ],
+            out_specs=[fixed((QROWS, WIDTH)), fixed((QROWS, WIDTH)), wide, wide, wide,
+                       fixed((1, WIDTH))],
+            scratch_shapes=[
+                pltpu.VMEM((QROWS, WIDTH), LOW), pltpu.VMEM((QROWS, WIDTH), LOW),
+                pltpu.VMEM((QROWS, WIDTH), F32), pltpu.VMEM((QROWS, WIDTH), F32),
+            ],
+        ),
         out_shape=outs,
-        scratch_shapes=scratch,
         compiler_params=pltpu.CompilerParams(
             dimension_semantics=("arbitrary",), vmem_limit_bytes=VMEM_MOST
         ),
-        cost_estimate=pl.CostEstimate(flops=flops, bytes_accessed=moved, transcendentals=0),
-        name=name,
-    )(*ins)
-
-
-def shape_of(shape, dtype):
-    return jax.ShapeDtypeStruct(shape, dtype)
-
-
-def feed(info, x3, cot, gain, wg, wu, wo):
-    units = wg.shape[2]
-    wide = part((1, WIDTH, units))
-    return run_heads(
-        feed_kernel, "feed",
-        (info, x3, cot, gain, wg, wu, wo),
-        [SCALARS, whole((QROWS, WIDTH)), whole((QROWS, WIDTH)), whole((8, WIDTH)),
-         wide, wide, wide],
-        [shape_of((QROWS, WIDTH), LOW), shape_of((QROWS, WIDTH), F32)]
-        + [shape_of((4, WIDTH, units), LOW)] * 3
-        + [shape_of((1, WIDTH), F32)],
-        [whole((QROWS, WIDTH)), whole((QROWS, WIDTH)), wide, wide, wide, whole((1, WIDTH))],
-        [pltpu.VMEM((QROWS, WIDTH), LOW), pltpu.VMEM((WIDTH, QROWS), LOW),
-         pltpu.VMEM((QROWS, WIDTH), LOW), pltpu.VMEM((WIDTH, QROWS), LOW),
-         pltpu.VMEM((QROWS, WIDTH), F32), pltpu.VMEM((QROWS, WIDTH), F32)],
-        13 * 10**9,
-    )
-
-
-def last_grads(dh, dkv, x, h, gain, g2, w3, dkvc, enc):
-    rows = enc.shape[0]
-    return run_heads(
-        last_kernel, "last_grads",
-        (dh, dkv, x, h, gain, g2, w3, w3, dkvc, enc),
-        [whole((QROWS, WIDTH)), part((1, QROWS, 256)), whole((QROWS, WIDTH)),
-         whole((QROWS, WIDTH)), whole((8, WIDTH)), whole((QROWS + 8, WIDTH)),
-         part((1, WIDTH, 256)), part((1, WIDTH, 256), 1), part((1, rows, 256)),
-         whole((rows, WIDTH))],
-        [shape_of((QROWS, WIDTH), LOW), shape_of((rows, WIDTH), LOW),
-         shape_of((4, WIDTH, 512), LOW), shape_of((1, WIDTH), F32)],
-        [whole((QROWS, WIDTH)), whole((rows, WIDTH)), part((1, WIDTH, 512)),
-         whole((1, WIDTH))],
-        [pltpu.VMEM((WIDTH, QROWS), LOW), pltpu.VMEM((WIDTH, rows), LOW),
-         pltpu.VMEM((QROWS, WIDTH), F32), pltpu.VMEM((rows, WIDTH), F32)],
-        3 * 10**9,
-    )
-
-
+        cost_estimate=pl.CostEstimate(
+            flops=13 * 10**9, bytes_accessed=4 * 10**7, transcendentals=0
+        ),
+        name="feed",
+    )(at, lengths, x3, cot, gains, wg, wu, wo)
+
+
+FORWARD_SPLIT = (0.0, 0.7)
+BACKWARD_SPLIT = (0.1, 0.0, 0.6)
+FINISH_SPLIT = (0.0, 0.0)
 GATHER_ORDERS = ("zyx", "zyx", "xzy", "yzx", "zxy", "yzx", "zxy", "y", "y")
 SMALL_ROWS = 16
-LANES = 128
 
 
 def split_steps(steps, parts, low, high):
@@ -1256,17 +1227,30 @@
 
 
 def forward_kernel(rows, *refs):
-    lengths, ins = refs[0], refs[1:10]
+    lengths, feeds, packs, inputs, encoder = refs[0], refs[1:4], refs[4:8], refs[8], refs[9]
     weights, refs = refs[10:16], refs[16:]
-    gains_ref, x2_ref, x3_ref, h1_out, h2_ref = refs[:5]
-    q1_out, kv1_out, p1_out, o1_out, q2_out, kv2_out, p2_out, o2_out = refs[5:13]
-    small, x_all, enc_all, bucket_ref, h1_ref, s_ref, strip_ref, ot_ref = refs[13:21]
+    gains_ref, x2_ref, x3_ref, h1_out, h2_ref, x_out, enc_out = refs[:7]
+    q1_out, kv1_out, p1_out, o1_out, q2_out, kv2_out, p2_out, o2_out = refs[7:15]
+    small, x_all, enc_all, bucket_ref, h1_ref, s_ref, strip_ref, ot_ref = refs[15:23]
+    own_feeds, own_x, own_enc, own_sem = refs[23:26], refs[26], refs[27], refs[28]
     place = Place()
-    plan = Gather(place, GATHER_ORDERS, rows, ins, weights + (small, x_all, enc_all), refs[21:])
+    half = lax.rem(place.z, 2)
+    seq = lax.div(place.z, 2)
+    ins = own_feeds + packs + (own_x, own_enc)
+    loads = [
+        pltpu.make_async_copy(src, dst, own_sem.at[i])
+        for i, (src, dst) in enumerate(
+            [(inputs.at[seq], own_x), (encoder.at[seq], own_enc)] + list(zip(feeds, own_feeds))
+        )
+    ]
+    for load in loads:
+        load.start()
+    plan = Gather(place, GATHER_ORDERS, rows, ins, weights + (small, x_all, enc_all), refs[29:])
     greet(place)
-    half = lax.rem(place.z, 2)
     first = pl.multiple_of(place.y * (2 * QROWS) + half * QROWS, QROWS)
-    length = lengths[lax.div(place.z, 2)]
+    length = lengths[seq]
+    for load in loads:
+        load.wait()
     plan.start(range(3, 9))
     row = lax.broadcasted_iota(jnp.int32, (8, SPAN), 0)
     col = lax.broadcasted_iota(jnp.int32, (8, SPAN), 1)
@@ -1278,7 +1262,7 @@
         step()
     plan.settle(range(3, 9))
     feed_steps = [step for _, step in plan.steps(lambda j, k: j < 3)]
-    chunks, rest = split_steps(feed_steps, 8, 0.0, 0.7)
+    chunks, rest = split_steps(feed_steps, 8, *FORWARD_SPLIT)
 
     for k in range(3):
         gains_ref[pl.ds(k, 1), :] = jnp.concatenate(
@@ -1291,7 +1275,11 @@
             h1_ref[pl.ds(y * 512 + c * QROWS, QROWS), :] = norm_rows(
                 x_all[y, at, :].astype(jnp.float32), gain
             ).astype(jnp.bfloat16)
-    x2_ref[...] = ins[7][pl.ds(half * QROWS, QROWS), :].astype(jnp.float32)
+    own = own_x[pl.ds(pl.multiple_of(half * QROWS, QROWS), QROWS), :]
+    x_out[...] = own
+    x2_ref[...] = own.astype(jnp.float32)
+    n = QROWS // 2
+    enc_out[...] = own_enc[pl.ds(pl.multiple_of(half * n, n), n), :]
     h1_out[...] = h1_ref[pl.ds(first, QROWS), :]
 
     def self_body(w_ref, wkv_ref, q_ref, kv_ref, p_ref, o_ref):
@@ -1347,25 +1335,31 @@
     plan.sent()
 
 
-def forward(lengths, arrays):
+def forward(lengths, feeds, packs, inputs, encoder):
+    x, enc = shape_of(inputs.shape[1:], LOW), shape_of(encoder.shape[1:], LOW)
+    arrays = list(feeds) + list(packs) + [x, enc]
     rows = [a.shape[0] for a in arrays]
     wide = [gathered(a, o) for a, o in zip(arrays, GATHER_ORDERS)]
     vm = pltpu.VMEM
     return comm_call(
         functools.partial(forward_kernel, rows), "forward", 1,
-        (lengths,) + tuple(arrays), [SCALARS] + [INSIDE] * 9,
+        (lengths,) + tuple(feeds) + tuple(packs) + (inputs, encoder),
+        [SCALARS] + [HBM] * 3 + [INSIDE] * 4 + [HBM] * 2,
         wide[:6]
         + [shape_of((8, WIDTH), F32), shape_of((QROWS, WIDTH), F32),
            shape_of((QROWS, WIDTH), F32), shape_of((QROWS, WIDTH), LOW),
-           shape_of((QROWS, WIDTH), LOW),
+           shape_of((QROWS, WIDTH), LOW), shape_of((QROWS, WIDTH), LOW),
+           shape_of((QROWS // 2, WIDTH), LOW),
            shape_of((4, QROWS, 256), LOW), shape_of((4, KEYS, 256), LOW),
            shape_of((4, 2, KEYS, 512), LOW), shape_of((4, QROWS, 256), LOW),
            shape_of((4, QROWS, 256), LOW), shape_of((4, ENC_ROWS, 256), LOW),
            shape_of((4, 2, ENC_ROWS, 512), LOW), shape_of((4, QROWS, 256), LOW)],
-        [HBM] * 6 + [INSIDE] * 5 + [HBM] * 8,
+        [HBM] * 6 + [INSIDE] * 7 + [HBM] * 8,
         [vm(w.shape, w.dtype) for w in wide[6:]]
         + [vm((8, SPAN), jnp.int32), vm((KEYS, WIDTH), LOW), vm((KEYS, 512), F32),
            vm((2, CHUNK, SPAN), F32), vm((256, QROWS), F32)]
+        + [vm(a.shape, LOW) for a in arrays[:3] + arrays[7:]]
+        + [pltpu.SemaphoreType.DMA((5,))]
         + Gather.scratch(9),
     )
 
@@ -1380,7 +1374,7 @@
     shards, refs = refs[16:19], refs[19:]
     dkv1_out, dkv2_out, rows_out, g2_ref, dh_ref, near_ref, gw1, gw2 = refs[:8]
     dkv1, dkv2, g_ref, gt_ref, ht_ref, dc_ref, d_ref, ds_ref, qt_ref, strip_ref = refs[8:18]
-    scratch = refs[18:]
+    line_ref, scratch = refs[18], refs[19:]
     place = Place()
     plan = Scatter(place, FEED_ORDERS, rows, grads, shards, scratch[: len(room)])
     scratch = scratch[len(room) :]
@@ -1390,10 +1384,10 @@
     lines.start()
     plan.start()
     steps = [step for _, step in plan.steps()]
-    begin = len(steps) // 10
+    begin = int(len(steps) * BACKWARD_SPLIT[0])
     for step in steps[:begin]:
         step()
-    chunks, rest = split_steps(steps[begin:], 8, 0.0, 0.6)
+    chunks, rest = split_steps(steps[begin:], 8, *BACKWARD_SPLIT[1:])
 
     def load_grad(ref, h_ref):
         g = ref[...].astype(jnp.bfloat16)
@@ -1445,7 +1439,10 @@
                         piece = strip_ref[b, 8 * g : 8 * g + 8, :]
                         shift = 120 - 8 * g
                         total = total + (pltpu.roll(piece, shift, 1) if shift else piece)
-                    near_ref[t, 2 * a + b] = total
+                    line = total[0:1]
+                    for r in range(1, 8):
+                        line = line + pltpu.roll(total[r : r + 1], SPAN - r, 1)
+                    line_ref[pl.ds(t * 4 + 2 * a + b, 1), :] = line
                 return
             if c == 0:
                 strip_ref[...] = jnp.zeros_like(strip_ref)
@@ -1460,6 +1457,13 @@
         self_body, grid=(4,), in_specs=specs(KEYS), out_specs=[part((1, WIDTH, 512))]
     )(w1, q1, kv1, p1, o1, gw1)
     share.start()
+    distance = lax.broadcasted_iota(jnp.int32, (1, SPAN), 1) - (SPAN - 264) + here()[2]
+    bucket = bucket_index(jnp.maximum(distance, 0))
+    chosen = lax.broadcasted_iota(jnp.int32, (LANES, SPAN), 0) == bucket
+    near_ref[...] = lax.dot_general(
+        line_ref[...], chosen.astype(jnp.float32), LAST, precision=TOP_PRECISION,
+        preferred_element_type=jnp.float32,
+    )
     ordered = [(i / max(len(rest), 1), step) for i, step in enumerate(rest)]
     ordered += [(0.05 + 0.9 * at, step) for at, step in share.steps()]
     ordered += [(0.1 * at, step) for at, step in lines.steps()]
@@ -1472,9 +1476,9 @@
 
 
 def backward(grads, out, g3, x2, h2, h1, gains, w1, w2, saved1, saved2):
-    rows = [a.shape[1] // 8 for a in grads]
+    rows = [shard_shape(a)[0] for a in grads]
     own = [KEYS // 4, ENC_ROWS // 4]
-    room = Scatter.scratch(grads, rows, FEED_ORDERS)
+    room = Scatter.scratch(grads, FEED_ORDERS)
     vm = pltpu.VMEM
     return comm_call(
         functools.partial(backward_kernel, rows, own, room), "backward", 2,
@@ -1483,17 +1487,99 @@
         scattered(grads)
         + [shape_of((4, r, 256), LOW) for r in own]
         + [gathered(out, "z"), shape_of((QROWS + 8, WIDTH), F32), shape_of((QROWS, WIDTH), F32),
-           shape_of((4, 4, 8, SPAN), F32), shape_of(w1.shape, LOW), shape_of(w2.shape, LOW)],
+           shape_of((16, LANES), F32), shape_of(w1.shape, LOW), shape_of(w2.shape, LOW)],
         [INSIDE] * 5 + [HBM] + [INSIDE] * 3 + [HBM] * 2,
         [vm((4, KEYS, 256), LOW), vm((4, ENC_ROWS, 256), LOW), vm((QROWS, WIDTH), LOW),
          vm((WIDTH, QROWS), LOW), vm((WIDTH, QROWS), LOW), vm((QROWS, WIDTH), F32),
          vm((KEYS, 512), F32), vm((KEYS, 512), LOW), vm((256, QROWS), F32),
-         vm((2, CHUNK, SPAN), F32)]
+         vm((2, CHUNK, SPAN), F32), vm((16, SPAN), F32)]
         + room + Share.scratch(own) + Gather.scratch(1),
     )
 
 
 HEAD_ORDERS = ("zyx", "zxy", "zyx", "zxy")
+
+
+def finish_kernel(rows, room, *refs):
+    gw1, gw2, w3 = refs[:3]
+    dkv, dkvc, dh_ref, g2_ref, x_ref, h1_ref, enc_ref, gains_ref, gn3_ref, table_ref = refs[3:13]
+    shards, (gx_out, genc_out) = refs[13:17], refs[17:19]
+    gw3, small, gx_ref, genc_ref, ht_ref, et_ref, dsum_ref, de_ref = refs[19:27]
+    scratch = refs[27:]
+    place = Place()
+    plan = Scatter(
+        place, HEAD_ORDERS, rows, (gw1, gw2, gw3, small), shards, scratch[: len(room)]
+    )
+    lines = Gather(
+        place, ("z", "z"), (QROWS, QROWS // 2), (gx_ref, genc_ref), (gx_out, genc_out),
+        scratch[len(room) :],
+    )
+    greet(place)
+    plan.start(range(2))
+    ready = [step for _, step in plan.steps(lambda j: j < 2)]
+    chunks, rest = split_steps(ready, 4, *FINISH_SPLIT)
+    ht_ref[...] = jnp.transpose(h1_ref[...])
+    et_ref[...] = jnp.transpose(enc_ref[...])
+    dsum_ref[...] = dh_ref[...]
+    de_ref[...] = jnp.zeros_like(de_ref)
+
+    def body(ws_ref, wc_ref):
+        t = pl.program_id(0)
+        gw3[t, :, pl.ds(0, 256)] = mm(ht_ref[...], dkv[t]).astype(jnp.bfloat16)
+        gw3[t, :, pl.ds(256, 256)] = mm(et_ref[...], dkvc[t]).astype(jnp.bfloat16)
+        dsum_ref[...] += mm(dkv[t], ws_ref[0], LAST)
+        de_ref[...] += mm(dkvc[t], wc_ref[0], LAST)
+        at_step(t, chunks)
+
+    pltpu.emit_pipeline(
+        body, grid=(4,), in_specs=[part((1, WIDTH, 256)), part((1, WIDTH, 256), 1)]
+    )(w3, w3)
+    back, gn1 = norm_back(
+        x_ref[...].astype(jnp.float32), gains_ref[pl.ds(0, 1), :], dsum_ref[...]
+    )
+    gx_ref[...] = (g2_ref[pl.ds(0, QROWS), :] + back).astype(jnp.bfloat16)
+    genc_ref[...] = de_ref[...].astype(jnp.bfloat16)
+    lines.start()
+    small[...] = jnp.zeros_like(small)
+    gain_grads = (gn1, g2_ref[pl.ds(QROWS, 1), :], gn3_ref[...])
+    table = table_ref[...]
+    for r in range(8):
+        shifted = pltpu.roll(table, (LANES - 4 * r) % LANES, 1) if r else table
+        for t in range(4):
+            for k in range(3):
+                small[t, pl.ds(r * SMALL_ROWS + k, 1), :] = gain_grads[k][
+                    :, r * LANES : (r + 1) * LANES
+                ]
+            small[t, pl.ds(r * SMALL_ROWS + 4, 4), :] = shifted[4 * t : 4 * t + 4]
+    plan.start(range(2, 4))
+    ordered = [(0.6 * i / len(rest), step) for i, step in enumerate(rest)]
+    ordered += [(0.1 + 0.9 * at, step) for at, step in plan.steps(lambda j: j >= 2)]
+    ordered += [(0.9 * at, step) for at, step in lines.steps()]
+    ordered.sort(key=lambda s: s[0])
+    for _, step in ordered:
+        step()
+    lines.finish()
+    plan.finish()
+
+
+def finish(gw1, gw2, w3, dkv, dkvc, dh, g2, x, h1, enc, gains, gn3, table):
+    whole_small = shape_of((4, 8 * SMALL_ROWS, LANES), F32)
+    arrays = (gw1, gw2, shape_of(w3.shape, LOW), whole_small)
+    rows = [shard_shape(a)[0] for a in arrays]
+    room = Scatter.scratch(arrays, HEAD_ORDERS)
+    vm = pltpu.VMEM
+    lines = [shape_of(a.shape, LOW) for a in (x, enc)]
+    return comm_call(
+        functools.partial(finish_kernel, rows, room), "finish", 3,
+        (gw1, gw2, w3, dkv, dkvc, dh, g2, x, h1, enc, gains, gn3, table),
+        [HBM] * 3 + [INSIDE] * 10,
+        scattered(arrays) + [gathered(a, "z") for a in lines],
+        [INSIDE] * 4 + [HBM] * 2,
+        [vm(a.shape, a.dtype) for a in arrays[2:]] + [vm(a.shape, a.dtype) for a in lines]
+        + [vm((WIDTH, QROWS), LOW), vm((WIDTH, QROWS // 2), LOW), vm((QROWS, WIDTH), F32),
+           vm((QROWS // 2, WIDTH), F32)]
+        + room + Gather.scratch(2),
+    )
 
 
 def small_rows(gains, table):
@@ -1508,64 +1594,35 @@
     norm_cross, cross_query, cross_key_matrix, cross_value_matrix, cross_out,
     norm_feed, feed_gate, feed_up, feed_out,
 ):
-    y = lax.axis_index("ctx")
-    t = lax.axis_index("tp")
-    seq, half = lax.div(t, 2), lax.rem(t, 2)
-    first = y * (2 * QROWS) + half * QROWS
-    info = jnp.stack([first, lax.dynamic_index_in_dim(lengths, seq, 0, False)])
-    x_seq = lax.dynamic_index_in_dim(inputs, seq, 0, False)
-    enc_seq = lax.dynamic_index_in_dim(encoder, seq, 0, False)
-    x_own = lax.dynamic_slice_in_dim(x_seq, half * QROWS, QROWS, 0)
-    cot = lax.dynamic_slice(cotangent, (seq, half * QROWS, 0), (1, QROWS, WIDTH))[0]
-    packed = (
-        feed_gate, feed_up, feed_out,
+    packs = (
         jnp.concatenate([self_query, self_out], axis=1),
         jnp.concatenate([cross_query, cross_out], axis=1),
         jnp.concatenate(
             [self_key_matrix, self_value_matrix, cross_key_matrix, cross_value_matrix], axis=1
         ),
         small_rows((norm_self, norm_cross, norm_feed), bias_table),
-        x_seq, enc_seq,
     )
     (
-        wg, wu, wo, w1, w2, w3, gains, x2, x3, h1, h2, q1, kv1, p1, o1, q2, kv2, p2, o2,
-    ) = forward(lengths, packed)
-    distance = jnp.maximum(
-        first + jnp.arange(SPAN)[None, :] - (SPAN - 264) - jnp.arange(8)[:, None], 0
-    )
-    bucket = bucket_index(distance)
-    out, g3, gg, gu, go, gn3 = feed(info, x3, cot, gains, wg, wu, wo)
-    gg, gu, go, dkv, dkvc, out, g2, dh, near, gw1, gw2 = backward(
+        wg, wu, wo, w1, w2, w3, gains, x2, x3, h1, h2, x_own, enc_own,
+        q1, kv1, p1, o1, q2, kv2, p2, o2,
+    ) = forward(lengths, (feed_gate.T, feed_up.T, feed_out.T), packs, inputs, encoder)
+    out, g3, gg, gu, go, gn3 = feed(
+        jnp.stack(here()), lengths, x3, cotangent, gains, wg, wu, wo
+    )
+    gg, gu, go, dkv, dkvc, out, g2, dh, table, gw1, gw2 = backward(
         (gg, gu, go), out, g3, x2, h2, h1, gains, w1, w2, (q1, kv1, p1, o1), (q2, kv2, p2, o2)
     )
-    gn2 = g2[QROWS : QROWS + 1]
-    enc_own = lax.dynamic_slice_in_dim(enc_seq, half * (QROWS // 2), QROWS // 2, 0)
-    gx, genc, gw3, gn1 = last_grads(
-        dh, dkv, x_own, h1, gains, g2, w3, dkvc, enc_own
-    )
-    one_hot = (bucket[:, :, None] == jnp.arange(BUCKETS, dtype=jnp.int32)).astype(F32)
-    grad_table = jnp.einsum(
-        "hrm,rmb->bh", near.reshape(16, 8, SPAN), one_hot, precision=TOP_PRECISION
-    )
-    gain_grads = jnp.concatenate([gn1, gn2, gn3], axis=0).reshape(3, 8, LANES)
-    gain_grads = jnp.broadcast_to(jnp.transpose(gain_grads, (1, 0, 2))[None], (4, 8, 3, LANES))
-    table_grads = jnp.transpose(grad_table.reshape(8, 4, 4, 4), (2, 0, 1, 3)).reshape(4, 8, 1, 16)
-    table_grads = jnp.pad(table_grads, ((0, 0), (0, 0), (0, 0), (0, LANES - 16)))
-    small_grads = jnp.pad(
-        jnp.concatenate([gain_grads, table_grads], axis=2),
-        ((0, 0), (0, 0), (0, SMALL_ROWS - 4), (0, 0)),
-    ).reshape(4, 8 * SMALL_ROWS, LANES)
-    gw1, gw2, gw3, gs, gx, genc = scatter_and_rows(
-        (gw1, gw2, gw3, small_grads), HEAD_ORDERS, (gx, genc), "scatter_heads"
+    gw1, gw2, gw3, gs, gx, genc = finish(
+        gw1, gw2, w3, dkv, dkvc, dh, g2, x_own, h1, enc_own, gains, gn3, table
     )
     return (
         out.reshape(inputs.shape),
         gx.reshape(inputs.shape).astype(F32),
         genc.reshape(encoder.shape).astype(F32),
         gs[0], gw1[:, :256], gw3[:, :128], gw3[:, 128:256], gw1[:, 256:],
-        gs[3, :16].reshape(4, 4),
+        jnp.transpose(gs[4:8, :4]),
         gs[1], gw2[:, :256], gw3[:, 256:384], gw3[:, 384:], gw2[:, 256:],
-        gs[2], gg, gu, go,
+        gs[2], gg.T, gu.T, go.T,
     )
 
 

time: 458 us -> 439 us (0.959)
  the two profiles are of different devices: /device:TPU:10 before, /device:TPU:0 now
where the time goes in v5:
time: 439 us; the launch traced here: 430 us
  Pallas kernels  407 us (93%)
  local copies, waits for them, and re-layouts  12 us (3%)
  other arithmetic  10.4 us (2%)
    pallas_call x3, Pallas kernels, comm_call(): pl.pallas_call(kernel, out_shape=outs, in_specs=in_specs, out_specs=out_s...  382 us
    pallas_call x1, Pallas kernels, feed(): pl.pallas_call(feed_kernel, grid_spec=pltpu.PrefetchScalarGridSpec(num_sc...  24.8 us

profile of v5, /device:TPU:0, one launch (start us, length us, event | category | flops | bytes accessed | tf_op | source)
XLA Modules:
  0.0 430.4 jit_solution(4115502946351645932)
XLA Ops:
  0.7 0.6 pad_add_fusion.at
  1.2 0.8 convert_element_type.43
  2.0 0.7 fusion.1
  2.7 0.6 pad_convert_fusion.refs_7_
  3.3 1.5 pad_maximum_fusion.2.refs_6_
  4.8 1.6 pad_maximum_fusion
  6.4 153.3 %forward.1 = (bf16[4,704,1024]{2,1,0:T(8,128)(2,1)}, bf16[4,704,1024]{2,1,0:T(8,128)(2,1)}, bf16[4,704,1024]{2,1,0:T(8,128)(2,1)}, bf16[4,1024,512]{2,1,0:T(8,12...) custom-call(s32[2]{0:T(128)} %lengths.1, ...), custom_call_target="tpu_custom_call" | custom-call | tf_op jit(solution)/shard_map/forward/pallas_call | solution.py:931
  159.8 24.8 %feed.1 = (bf16[256,1024]{1,0:T(8,128)(2,1)}, f32[256,1024]{1,0:T(8,128)}, bf16[4,704,1024]{2,1,0:T(8,128)(2,1)}, bf16[4,704,1024]{2,1,0:T(8,128)(2,1)}, bf16[4,...) custom-call(s32[3]{0:T(128)} %pad_add_fusion.at, s32[2]{0:T(128)} %lengths.1, f32[256,1024]{1,0:T(8,128)} %get-tuple-element.62.x3_ref, ...), custom_call_target="tpu_custom_call" | custom-call | flops 12999999488 | bytes 40000000 | tf_op jit(solution)/shard_map/feed/pallas_call | solution.py:1178
  184.6 131.7 %backward.1 = (f32[704,128]{1,0:T(8,128)}, f32[704,128]{1,0:T(8,128)}, f32[704,128]{1,0:T(8,128)}, bf16[4,256,256]{2,1,0:T(8,128)(2,1)}, bf16[4,128,256]{2,1,0:T...) custom-call(bf16[4,704,1024]{2,1,0:T(8,128)(2,1)} %get-tuple-element, ...), custom_call_target="tpu_custom_call" | custom-call | tf_op jit(solution)/shard_map/backward/pallas_call | solution.py:931
  316.3 97.0 %finish.1 = (f32[128,512]{1,0:T(8,128)}, f32[128,512]{1,0:T(8,128)}, f32[128,512]{1,0:T(8,128)}, f32[16,128]{1,0:T(8,128)}, bf16[4,256,1024]{2,1,0:T(8,128)(2,1)}, /*index=5*/bf16[4,128,1024]{2,1,0:T(8,128)(2,1)}) custom-call(bf16[4,1024,512]{2,1,0:T(8,128)(2,1)} %get-tuple-element.86.refs_0_, bf16[4,1024,512]{2,1,0:T(8,128)(2,1)} %get-tuple-element.87.refs_1_, ...), custom_call_target="tpu_custom_call" | custom-call | tf_op jit(solution)/shard_map/finish/pallas_call | solution.py:931
  413.3 0.0 copy-start
  413.3 1.4 slice_bitcast_fusion.1
  414.6 0.7 slice_bitcast_fusion
  415.3 0.7 copy.37
  416.0 1.6 fusion.3
  417.6 1.7 fusion.4
  419.3 1.7 fusion.2
  421.0 0.0 copy-start.1
  421.0 2.9 bitcast_convert_fusion.1
  423.9 0.0 copy-done
  423.9 0.0 copy-start.4
  423.9 0.0 copy-start.3
  423.9 2.5 bitcast_convert_fusion
  426.4 0.0 copy-done.1
  426.4 0.0 copy-start.2
  426.4 1.3 copy.42
  427.7 0.0 copy-done.4
  427.7 0.7 copy.43
  428.5 0.0 copy-done.3
  428.5 0.7 copy.44
  429.2 0.0 copy-done.2
  429.2 0.7 copy.45
Async XLA Ops:
  413.3 10.7 %copy-start = (bf16[4,256,1024]{2,1,0:T(8,128)(2,1)S(1)}, bf16[4,256,1024]{2,1,0:T(8,128)(2,1)}, u32[]{:S(2)}) copy-start(bf16[4,256,1024]{2,1,0:T(8,128)(2,1)} %get-tuple-element.97) | copy-start | bytes 6291460
  421.0 5.4 %copy-start.1 = (bf16[4,256,1024]{2,1,0:T(8,128)(2,1)S(1)}, bf16[4,256,1024]{2,1,0:T(8,128)(2,1)}, u32[]{:S(2)}) copy-start(bf16[4,256,1024]{2,1,0:T(8,128)(2,1)} %get-tuple-element.85) | copy-start | bytes 6291460
  423.9 3.8 copy-start.4
  423.9 4.5 %copy-start.3 = (f32[704,128]{1,0:T(8,128)S(1)}, f32[704,128]{1,0:T(8,128)}, u32[]{:S(2)}) copy-start(f32[704,128]{1,0:T(8,128)} %get-tuple-element.104) | copy-start | bytes 1081348
  426.4 2.8 copy-start.2

commit v6 on v5

--- a/solution.py
+++ b/solution.py
@@ -1205,7 +1205,8 @@
 
 FORWARD_SPLIT = (0.0, 0.7)
 BACKWARD_SPLIT = (0.1, 0.0, 0.6)
-FINISH_SPLIT = (0.0, 0.0)
+SHARED = 0.5
+LAST_SPLIT = (0.0, 0.6)
 GATHER_ORDERS = ("zyx", "zyx", "xzy", "yzx", "zxy", "yzx", "zxy", "y", "y")
 SMALL_ROWS = 16
 
@@ -1369,12 +1370,12 @@
 
 def backward_kernel(rows, own, room, *refs):
     grads, refs = refs[:3], refs[3:]
-    out_ref, g3_ref, x2_ref, h2_ref, h1_ref, gains_ref = refs[:6]
-    w1, w2, q1, kv1, p1, o1, q2, kv2, p2, o2 = refs[6:16]
-    shards, refs = refs[16:19], refs[19:]
-    dkv1_out, dkv2_out, rows_out, g2_ref, dh_ref, near_ref, gw1, gw2 = refs[:8]
-    dkv1, dkv2, g_ref, gt_ref, ht_ref, dc_ref, d_ref, ds_ref, qt_ref, strip_ref = refs[8:18]
-    line_ref, scratch = refs[18], refs[19:]
+    out_ref, g3_ref, x2_ref, h2_ref, h1_ref, gains_ref, x_ref, enc_ref, gn3_ref = refs[:9]
+    w1, w2, w3, q1, kv1, p1, o1, q2, kv2, p2, o2 = refs[9:20]
+    shards, refs = refs[20:23], refs[23:]
+    rows_out, gx_ref, genc_ref, small, gw1, gw2, gw3 = refs[:7]
+    dkv1, dkv2, g_ref, gt_ref, ht_ref, dc_ref, d_ref, ds_ref, qt_ref, strip_ref = refs[7:17]
+    line_ref, g2_ref, dh_ref, dkv1_out, dkv2_out, et_ref, scratch = *refs[17:23], refs[23:]
     place = Place()
     plan = Scatter(place, FEED_ORDERS, rows, grads, shards, scratch[: len(room)])
     scratch = scratch[len(room) :]
@@ -1423,9 +1424,9 @@
         cross_body, grid=(4,), in_specs=specs(ENC_ROWS), out_specs=[part((1, WIDTH, 512))]
     )(w2, q2, kv2, p2, o2, gw2)
     back, gain_grad = norm_back(x2_ref[...], gains_ref[pl.ds(1, 1), :], dc_ref[...])
-    g2_ref[pl.ds(0, QROWS), :] = g3_ref[...] + back
-    g2_ref[pl.ds(QROWS, 1), :] = gain_grad
-    load_grad(g2_ref.at[pl.ds(0, QROWS)], h1_ref)
+    g2_ref[...] = g3_ref[...] + back
+    gain_grads = [None, gain_grad, gn3_ref[...]]
+    load_grad(g2_ref, h1_ref)
     dh_ref[...] = jnp.zeros_like(dh_ref)
 
     def self_body(w_ref, q_ref, kv_ref, p_ref, o_ref, gw_ref):
@@ -1460,7 +1461,7 @@
     distance = lax.broadcasted_iota(jnp.int32, (1, SPAN), 1) - (SPAN - 264) + here()[2]
     bucket = bucket_index(jnp.maximum(distance, 0))
     chosen = lax.broadcasted_iota(jnp.int32, (LANES, SPAN), 0) == bucket
-    near_ref[...] = lax.dot_general(
+    table = lax.dot_general(
         line_ref[...], chosen.astype(jnp.float32), LAST, precision=TOP_PRECISION,
         preferred_element_type=jnp.float32,
     )
@@ -1468,81 +1469,32 @@
     ordered += [(0.05 + 0.9 * at, step) for at, step in share.steps()]
     ordered += [(0.1 * at, step) for at, step in lines.steps()]
     ordered.sort(key=lambda s: s[0])
-    for _, step in ordered:
+    for _, step in [s for s in ordered if s[0] <= SHARED]:
         step()
-    lines.finish()
-    share.finish()
-    plan.finish()
-
-
-def backward(grads, out, g3, x2, h2, h1, gains, w1, w2, saved1, saved2):
-    rows = [shard_shape(a)[0] for a in grads]
-    own = [KEYS // 4, ENC_ROWS // 4]
-    room = Scatter.scratch(grads, FEED_ORDERS)
-    vm = pltpu.VMEM
-    return comm_call(
-        functools.partial(backward_kernel, rows, own, room), "backward", 2,
-        tuple(grads) + (out, g3, x2, h2, h1, gains, w1, w2) + tuple(saved1) + tuple(saved2),
-        [HBM] * 3 + [INSIDE] * 6 + [HBM] * 10,
-        scattered(grads)
-        + [shape_of((4, r, 256), LOW) for r in own]
-        + [gathered(out, "z"), shape_of((QROWS + 8, WIDTH), F32), shape_of((QROWS, WIDTH), F32),
-           shape_of((16, LANES), F32), shape_of(w1.shape, LOW), shape_of(w2.shape, LOW)],
-        [INSIDE] * 5 + [HBM] + [INSIDE] * 3 + [HBM] * 2,
-        [vm((4, KEYS, 256), LOW), vm((4, ENC_ROWS, 256), LOW), vm((QROWS, WIDTH), LOW),
-         vm((WIDTH, QROWS), LOW), vm((WIDTH, QROWS), LOW), vm((QROWS, WIDTH), F32),
-         vm((KEYS, 512), F32), vm((KEYS, 512), LOW), vm((256, QROWS), F32),
-         vm((2, CHUNK, SPAN), F32), vm((16, SPAN), F32)]
-        + room + Share.scratch(own) + Gather.scratch(1),
-    )
-
-
-HEAD_ORDERS = ("zyx", "zxy", "zyx", "zxy")
-
-
-def finish_kernel(rows, room, *refs):
-    gw1, gw2, w3 = refs[:3]
-    dkv, dkvc, dh_ref, g2_ref, x_ref, h1_ref, enc_ref, gains_ref, gn3_ref, table_ref = refs[3:13]
-    shards, (gx_out, genc_out) = refs[13:17], refs[17:19]
-    gw3, small, gx_ref, genc_ref, ht_ref, et_ref, dsum_ref, de_ref = refs[19:27]
-    scratch = refs[27:]
-    place = Place()
-    plan = Scatter(
-        place, HEAD_ORDERS, rows, (gw1, gw2, gw3, small), shards, scratch[: len(room)]
-    )
-    lines = Gather(
-        place, ("z", "z"), (QROWS, QROWS // 2), (gx_ref, genc_ref), (gx_out, genc_out),
-        scratch[len(room) :],
-    )
-    greet(place)
-    plan.start(range(2))
-    ready = [step for _, step in plan.steps(lambda j: j < 2)]
-    chunks, rest = split_steps(ready, 4, *FINISH_SPLIT)
-    ht_ref[...] = jnp.transpose(h1_ref[...])
+    chunks, rest = split_steps([s[1] for s in ordered if s[0] > SHARED], 4, *LAST_SPLIT)
     et_ref[...] = jnp.transpose(enc_ref[...])
-    dsum_ref[...] = dh_ref[...]
-    de_ref[...] = jnp.zeros_like(de_ref)
-
-    def body(ws_ref, wc_ref):
+    n = QROWS // 2
+    dc_ref[pl.ds(0, n), :] = jnp.zeros((n, WIDTH), jnp.float32)
+
+    def last_body(ws_ref, wc_ref, gw_ref):
         t = pl.program_id(0)
-        gw3[t, :, pl.ds(0, 256)] = mm(ht_ref[...], dkv[t]).astype(jnp.bfloat16)
-        gw3[t, :, pl.ds(256, 256)] = mm(et_ref[...], dkvc[t]).astype(jnp.bfloat16)
-        dsum_ref[...] += mm(dkv[t], ws_ref[0], LAST)
-        de_ref[...] += mm(dkvc[t], wc_ref[0], LAST)
+        dkv, dkvc = dkv1_out[t], dkv2_out[t]
+        gw_ref[0, :, :256] = mm(ht_ref[...], dkv).astype(jnp.bfloat16)
+        gw_ref[0, :, 256:] = mm(et_ref[...], dkvc).astype(jnp.bfloat16)
+        dh_ref[...] += mm(dkv, ws_ref[0], LAST)
+        dc_ref[pl.ds(0, n), :] += mm(dkvc, wc_ref[0], LAST)
         at_step(t, chunks)
 
     pltpu.emit_pipeline(
-        body, grid=(4,), in_specs=[part((1, WIDTH, 256)), part((1, WIDTH, 256), 1)]
-    )(w3, w3)
-    back, gn1 = norm_back(
-        x_ref[...].astype(jnp.float32), gains_ref[pl.ds(0, 1), :], dsum_ref[...]
-    )
-    gx_ref[...] = (g2_ref[pl.ds(0, QROWS), :] + back).astype(jnp.bfloat16)
-    genc_ref[...] = de_ref[...].astype(jnp.bfloat16)
-    lines.start()
+        last_body, grid=(4,), in_specs=[part((1, WIDTH, 256)), part((1, WIDTH, 256), 1)],
+        out_specs=[part((1, WIDTH, 512))],
+    )(w3, w3, gw3)
+    back, gain_grads[0] = norm_back(
+        x_ref[...].astype(jnp.float32), gains_ref[pl.ds(0, 1), :], dh_ref[...]
+    )
+    gx_ref[...] = (g2_ref[...] + back).astype(jnp.bfloat16)
+    genc_ref[...] = dc_ref[pl.ds(0, n), :].astype(jnp.bfloat16)
     small[...] = jnp.zeros_like(small)
-    gain_grads = (gn1, g2_ref[pl.ds(QROWS, 1), :], gn3_ref[...])
-    table = table_ref[...]
     for r in range(8):
         shifted = pltpu.roll(table, (LANES - 4 * r) % LANES, 1) if r else table
         for t in range(4):
@@ -1551,34 +1503,70 @@
                     :, r * LANES : (r + 1) * LANES
                 ]
             small[t, pl.ds(r * SMALL_ROWS + 4, 4), :] = shifted[4 * t : 4 * t + 4]
-    plan.start(range(2, 4))
-    ordered = [(0.6 * i / len(rest), step) for i, step in enumerate(rest)]
-    ordered += [(0.1 + 0.9 * at, step) for at, step in plan.steps(lambda j: j >= 2)]
-    ordered += [(0.9 * at, step) for at, step in lines.steps()]
-    ordered.sort(key=lambda s: s[0])
-    for _, step in ordered:
+    for step in rest:
+        step()
+    lines.finish()
+    share.finish()
+    plan.finish()
+
+
+def backward(grads, out, g3, x2, h2, h1, gains, x, enc, gn3, w1, w2, w3, saved1, saved2):
+    rows = [shard_shape(a)[0] for a in grads]
+    own = [KEYS // 4, ENC_ROWS // 4]
+    room = Scatter.scratch(grads, FEED_ORDERS)
+    vm = pltpu.VMEM
+    return comm_call(
+        functools.partial(backward_kernel, rows, own, room), "backward", 2,
+        tuple(grads) + (out, g3, x2, h2, h1, gains, x, enc, gn3, w1, w2, w3)
+        + tuple(saved1) + tuple(saved2),
+        [HBM] * 3 + [INSIDE] * 9 + [HBM] * 11,
+        scattered(grads)
+        + [gathered(out, "z"), shape_of(x.shape, LOW), shape_of(enc.shape, LOW),
+           shape_of((4, 8 * SMALL_ROWS, LANES), F32), shape_of(w1.shape, LOW),
+           shape_of(w2.shape, LOW), shape_of(w3.shape, LOW)],
+        [INSIDE] * 3 + [HBM] + [INSIDE] * 3 + [HBM] * 3,
+        [vm((4, KEYS, 256), LOW), vm((4, ENC_ROWS, 256), LOW), vm((QROWS, WIDTH), LOW),
+         vm((WIDTH, QROWS), LOW), vm((WIDTH, QROWS), LOW), vm((QROWS, WIDTH), F32),
+         vm((KEYS, 512), F32), vm((KEYS, 512), LOW), vm((256, QROWS), F32),
+         vm((2, CHUNK, SPAN), F32), vm((16, SPAN), F32), vm((QROWS, WIDTH), F32),
+         vm((QROWS, WIDTH), F32)]
+        + [vm((4, r, 256), LOW) for r in own] + [vm((WIDTH, enc.shape[0]), LOW)]
+        + room + Share.scratch(own) + Gather.scratch(1),
+    )
+
+
+HEAD_ORDERS = ("zyx", "zxy", "zyx", "zxy")
+
+
+def finish_kernel(rows, room, *refs):
+    ins, sent, out, landed, scratch = refs[:4], refs[4:6], refs[6], refs[7:9], refs[9:]
+    place = Place()
+    shards = [out.at[j] for j in range(3)]
+    shards.append(out.at[3, pl.ds(0, SMALL_ROWS), pl.ds(0, LANES)])
+    plan = Scatter(place, HEAD_ORDERS, rows, ins, shards, scratch[: len(room)])
+    lines = Gather(
+        place, ("z", "z"), (QROWS, QROWS // 2), sent, landed, scratch[len(room) :]
+    )
+    greet(place)
+    lines.start()
+    plan.start()
+    steps = list(plan.steps()) + [(0.8 * at, step) for at, step in lines.steps()]
+    steps.sort(key=lambda s: s[0])
+    for _, step in steps:
         step()
     lines.finish()
     plan.finish()
 
 
-def finish(gw1, gw2, w3, dkv, dkvc, dh, g2, x, h1, enc, gains, gn3, table):
-    whole_small = shape_of((4, 8 * SMALL_ROWS, LANES), F32)
-    arrays = (gw1, gw2, shape_of(w3.shape, LOW), whole_small)
+def finish(arrays, lines):
     rows = [shard_shape(a)[0] for a in arrays]
     room = Scatter.scratch(arrays, HEAD_ORDERS)
-    vm = pltpu.VMEM
-    lines = [shape_of(a.shape, LOW) for a in (x, enc)]
     return comm_call(
         functools.partial(finish_kernel, rows, room), "finish", 3,
-        (gw1, gw2, w3, dkv, dkvc, dh, g2, x, h1, enc, gains, gn3, table),
-        [HBM] * 3 + [INSIDE] * 10,
-        scattered(arrays) + [gathered(a, "z") for a in lines],
-        [INSIDE] * 4 + [HBM] * 2,
-        [vm(a.shape, a.dtype) for a in arrays[2:]] + [vm(a.shape, a.dtype) for a in lines]
-        + [vm((WIDTH, QROWS), LOW), vm((WIDTH, QROWS // 2), LOW), vm((QROWS, WIDTH), F32),
-           vm((QROWS // 2, WIDTH), F32)]
-        + room + Gather.scratch(2),
+        tuple(arrays) + tuple(lines), [HBM] * 4 + [INSIDE] * 2,
+        [shape_of((4, LANES, 512), F32)] + [gathered(a, "z") for a in lines],
+        [INSIDE] + [HBM] * 2,
+        room + Gather.scratch(2),
     )
 
 
@@ -1609,20 +1597,20 @@
     out, g3, gg, gu, go, gn3 = feed(
         jnp.stack(here()), lengths, x3, cotangent, gains, wg, wu, wo
     )
-    gg, gu, go, dkv, dkvc, out, g2, dh, table, gw1, gw2 = backward(
-        (gg, gu, go), out, g3, x2, h2, h1, gains, w1, w2, (q1, kv1, p1, o1), (q2, kv2, p2, o2)
-    )
-    gw1, gw2, gw3, gs, gx, genc = finish(
-        gw1, gw2, w3, dkv, dkvc, dh, g2, x_own, h1, enc_own, gains, gn3, table
-    )
+    gg, gu, go, out, gx, genc, small, gw1, gw2, gw3 = backward(
+        (gg, gu, go), out, g3, x2, h2, h1, gains, x_own, enc_own, gn3, w1, w2, w3,
+        (q1, kv1, p1, o1), (q2, kv2, p2, o2),
+    )
+    heads, gx, genc = finish((gw1, gw2, gw3, small), (gx, genc))
     return (
         out.reshape(inputs.shape),
         gx.reshape(inputs.shape).astype(F32),
         genc.reshape(encoder.shape).astype(F32),
-        gs[0], gw1[:, :256], gw3[:, :128], gw3[:, 128:256], gw1[:, 256:],
-        jnp.transpose(gs[4:8, :4]),
-        gs[1], gw2[:, :256], gw3[:, 256:384], gw3[:, 384:], gw2[:, 256:],
-        gs[2], gg.T, gu.T, go.T,
+        heads[3, 0, :128], heads[0, :, :256], heads[2, :, :128], heads[2, :, 128:256],
+        heads[0, :, 256:], jnp.transpose(heads[3, 4:8, :4]),
+        heads[3, 1, :128], heads[1, :, :256], heads[2, :, 256:384], heads[2, :, 384:],
+        heads[1, :, 256:],
+        heads[3, 2, :128], gg.T, gu.T, go.T,
     )
 
 

time: 439 us -> 432 us (0.984)
  the two profiles are of different devices: /device:TPU:0 before, /device:TPU:12 now
where the time goes in v6:
time: 432 us; the launch traced here: 423 us
  Pallas kernels  401 us (93%)
  local copies, waits for them, and re-layouts  10.5 us (2%)
  other arithmetic  10.4 us (2%)
    pallas_call x3, Pallas kernels, comm_call(): pl.pallas_call(kernel, out_shape=outs, in_specs=in_specs, out_specs=out_s...  376 us
    pallas_call x1, Pallas kernels, feed(): pl.pallas_call(feed_kernel, grid_spec=pltpu.PrefetchScalarGridSpec(num_sc...  24.8 us

profile of v6, /device:TPU:12, one launch (start us, length us, event | category | flops | bytes accessed | tf_op | source)
XLA Modules:
  0.0 423.2 jit_solution(8891808645182689289)
XLA Ops:
  0.7 0.6 pad_add_fusion.at
  1.2 0.8 convert_element_type.43
  2.0 0.7 fusion.1
  2.7 0.6 pad_convert_fusion.refs_7_
  3.3 1.5 pad_maximum_fusion.2.refs_6_
  4.8 1.6 pad_maximum_fusion
  6.4 148.2 %forward.1 = (bf16[4,704,1024]{2,1,0:T(8,128)(2,1)}, bf16[4,704,1024]{2,1,0:T(8,128)(2,1)}, bf16[4,704,1024]{2,1,0:T(8,128)(2,1)}, bf16[4,1024,512]{2,1,0:T(8,12...) custom-call(s32[2]{0:T(128)} %lengths.1, ...), custom_call_target="tpu_custom_call" | custom-call | tf_op jit(solution)/shard_map/forward/pallas_call | solution.py:931
  154.7 24.8 %feed.1 = (bf16[256,1024]{1,0:T(8,128)(2,1)}, f32[256,1024]{1,0:T(8,128)}, bf16[4,704,1024]{2,1,0:T(8,128)(2,1)}, bf16[4,704,1024]{2,1,0:T(8,128)(2,1)}, bf16[4,...) custom-call(s32[3]{0:T(128)} %pad_add_fusion.at, s32[2]{0:T(128)} %lengths.1, f32[256,1024]{1,0:T(8,128)} %get-tuple-element.58.x3_ref, ...), custom_call_target="tpu_custom_call" | custom-call | flops 12999999488 | bytes 40000000 | tf_op jit(solution)/shard_map/feed/pallas_call | solution.py:1178
  179.5 138.1 %backward.1 = (f32[704,128]{1,0:T(8,128)}, f32[704,128]{1,0:T(8,128)}, f32[704,128]{1,0:T(8,128)}, bf16[4,256,1024]{2,1,0:T(8,128)(2,1)}, bf16[256,1024]{1,0:T(8...) custom-call(bf16[4,704,1024]{2,1,0:T(8,128)(2,1)} %get-tuple-element, ...), custom_call_target="tpu_custom_call" | custom-call | tf_op jit(solution)/shard_map/backward/pallas_call | solution.py:931
  317.6 89.9 %finish.1 = (f32[4,128,512]{2,1,0:T(8,128)}, bf16[4,256,1024]{2,1,0:T(8,128)(2,1)}, bf16[4,128,1024]{2,1,0:T(8,128)(2,1)}) custom-call(bf16[4,1024,512]{2,1,0:T(8,128)(2,1)} %get-tuple-element.86.refs_0_, bf16[4,1024,512]{2,1,0:T(8,128)(2,1)} %get-tuple-element.87.refs_1_, bf16[4,1024,512]{2,1,0:T(8,128)(2,1)} %get-tuple-element.88.refs_2_, ...), custom_call_target="tpu_custom_call" | custom-call | tf_op jit(solution)/shard_map/finish/pallas_call | solution.py:931
  407.6 0.0 copy-start
  407.6 1.4 slice_bitcast_fusion.9
  408.9 0.7 slice_bitcast_fusion.8
  409.6 0.7 copy.37
  410.3 1.6 slice_bitcast_fusion.4
  411.9 1.9 slice_bitcast_fusion
  413.8 0.0 copy-start.1
  413.8 2.9 bitcast_convert_fusion.1
  416.7 0.0 copy-done
  416.7 0.0 copy-start.4
  416.7 0.0 copy-start.3
  416.7 2.5 bitcast_convert_fusion
  419.2 0.0 copy-done.1
  419.2 0.0 copy-start.2
  419.2 1.3 copy.42
  420.5 0.0 copy-done.4
  420.5 0.7 copy.43
  421.3 0.0 copy-done.3
  421.3 0.7 copy.44
  422.0 0.0 copy-done.2
  422.0 0.7 copy.45
Async XLA Ops:
  407.6 9.2 %copy-start = (bf16[4,256,1024]{2,1,0:T(8,128)(2,1)S(1)}, bf16[4,256,1024]{2,1,0:T(8,128)(2,1)}, u32[]{:S(2)}) copy-start(bf16[4,256,1024]{2,1,0:T(8,128)(2,1)} %get-tuple-element.92) | copy-start | bytes 6291460
  413.8 5.4 %copy-start.1 = (bf16[4,256,1024]{2,1,0:T(8,128)(2,1)S(1)}, bf16[4,256,1024]{2,1,0:T(8,128)(2,1)}, u32[]{:S(2)}) copy-start(bf16[4,256,1024]{2,1,0:T(8,128)(2,1)} %get-tuple-element.85) | copy-start | bytes 6291460
  416.7 3.8 copy-start.4
  416.7 4.5 %copy-start.3 = (f32[704,128]{1,0:T(8,128)S(1)}, f32[704,128]{1,0:T(8,128)}, u32[]{:S(2)}) copy-start(f32[704,128]{1,0:T(8,128)} %get-tuple-element.96) | copy-start | bytes 1081348
  419.2 2.8 copy-start.2

commit v7 on v6

--- a/solution.py
+++ b/solution.py
@@ -674,7 +674,7 @@
 
 
 def add_rows(out, terms, rows):
-    step = min(rows, 64 if out.shape[-1] <= LANES else 32)
+    step = min(rows, 32)
 
     def body(q, carry):
         at = pl.ds(pl.multiple_of(q * step, step), step)
@@ -1009,16 +1009,22 @@
             s_ref[rows, :] = s
             top = jnp.max(s, axis=0, keepdims=True)
             peak = top if peak is None else jnp.maximum(peak, top)
-        total = jnp.zeros_like(peak)
-        for c in range(keys // CHUNK):
-            rows = pl.ds(c * CHUNK, CHUNK)
+
+        def expose(c, total):
+            rows = pl.ds(pl.multiple_of(c * CHUNK, CHUNK), CHUNK)
             e = jnp.exp(s_ref[rows, :] - peak)
             s_ref[rows, :] = e
-            total = total + jnp.sum(e, axis=0, keepdims=True)
+            return total + jnp.sum(e, axis=0, keepdims=True)
+
+        total = lax.fori_loop(0, keys // CHUNK, expose, jnp.zeros_like(peak))
         inverse = 1.0 / total
-        for c in range(keys // CHUNK):
-            rows = pl.ds(c * CHUNK, CHUNK)
+
+        def scale(c, carry):
+            rows = pl.ds(pl.multiple_of(c * CHUNK, CHUNK), CHUNK)
             p_ref[0, a, rows, :] = (s_ref[rows, :] * inverse).astype(jnp.bfloat16)
+            return carry
+
+        lax.fori_loop(0, keys // CHUNK, scale, 0)
         ot = mm(v, p_ref[0, a], ROWS_OF)
         ot_ref[a * 128 : a * 128 + 64, :] = ot[:, :QROWS]
         ot_ref[a * 128 + 64 : a * 128 + 128, :] = ot[:, QROWS:]
@@ -1055,7 +1061,7 @@
     return jnp.transpose(qt_ref[...]).astype(jnp.bfloat16)
 
 
-def self_step(first, length, h1_ref, w_ref, wkv_ref, near_of, q_ref, kv_ref, p_ref, o_ref, work):
+def self_step(first, length, h1_ref, w_ref, wkv_ref, q_ref, kv_ref, p_ref, o_ref, work):
     s_ref, strip_ref, ot_ref = work
     kv = mm(h1_ref[...], wkv_ref[0]).astype(jnp.bfloat16)
     kv_ref[0] = kv
@@ -1067,16 +1073,11 @@
 
     def add_bias(a, c, s):
         if c is None:
-            for b in range(2):
-                near = near_of(2 * a + b)
-                for g in range(16):
-                    shift = (SPAN - (120 - 8 * g)) % SPAN
-                    strip_ref[b, 8 * g : 8 * g + 8, :] = (
-                        pltpu.roll(near, shift, 1) if shift else near
-                    )
             return None
         cols = pl.ds(CHUNK * (7 - c), QROWS)
-        bias = jnp.concatenate([strip_ref[0, :, cols], strip_ref[1, :, cols]], axis=1)
+        bias = jnp.concatenate(
+            [strip_ref[2 * a, :, cols], strip_ref[2 * a + 1, :, cols]], axis=1
+        )
         key = lax.broadcasted_iota(jnp.int32, s.shape, 0) + c * CHUNK
         return jnp.where(key <= last_key, s + bias, MASKED)
 
@@ -1286,18 +1287,26 @@
     def self_body(w_ref, wkv_ref, q_ref, kv_ref, p_ref, o_ref):
         t = pl.program_id(0)
 
-        def near_of(head):
-            rows_of = [small[t, pl.ds(r * SMALL_ROWS + 3, 1), :] for r in range(8)]
+        def spread(head, carry):
+            rows_of = [
+                pltpu.roll(small[t, pl.ds(r * SMALL_ROWS + 3, 1), :], LANES - head, 1)
+                for r in range(8)
+            ]
             bucket = bucket_ref[...]
             near = jnp.zeros((8, SPAN), jnp.float32)
             for i in range(BUCKETS):
-                lane = (i % 4) * 4 + head
-                value = rows_of[i // 4][:, lane : lane + 1]
-                near = jnp.where(bucket == i, value, near)
-            return near
-
+                lane = (i % 4) * 4
+                near = jnp.where(bucket == i, rows_of[i // 4][:, lane : lane + 1], near)
+            for g in range(16):
+                shift = (SPAN - (120 - 8 * g)) % SPAN
+                strip_ref[head, 8 * g : 8 * g + 8, :] = (
+                    pltpu.roll(near, shift, 1) if shift else near
+                )
+            return carry
+
+        lax.fori_loop(0, 4, spread, 0)
         x2_ref[...] += self_step(
-            first, length, h1_ref, w_ref, wkv_ref, near_of, q_ref, kv_ref, p_ref, o_ref,
+            first, length, h1_ref, w_ref, wkv_ref, q_ref, kv_ref, p_ref, o_ref,
             (s_ref, strip_ref, ot_ref),
         )
         at_step(t, chunks[:4])
@@ -1315,11 +1324,13 @@
     h2_ref[...] = norm_rows(x2_ref[...], gains_ref[pl.ds(1, 1), :]).astype(jnp.bfloat16)
 
     def cross_body(w_ref, wkv_ref, q_ref, kv_ref, p_ref, o_ref):
+        t = pl.program_id(0)
         enc = jnp.concatenate([enc_all[0], enc_all[1]], axis=0)
         x3_ref[...] += cross_step(
-            h2_ref, enc, w_ref, wkv_ref, q_ref, kv_ref, p_ref, o_ref, (s_ref, ot_ref)
+            h2_ref, enc, w_ref, wkv_ref, q_ref, kv_ref, p_ref, o_ref,
+            (s_ref, ot_ref),
         )
-        at_step(pl.program_id(0), chunks[4:])
+        at_step(t, chunks[4:])
 
     pltpu.emit_pipeline(
         cross_body,
@@ -1358,7 +1369,7 @@
         [HBM] * 6 + [INSIDE] * 7 + [HBM] * 8,
         [vm(w.shape, w.dtype) for w in wide[6:]]
         + [vm((8, SPAN), jnp.int32), vm((KEYS, WIDTH), LOW), vm((KEYS, 512), F32),
-           vm((2, CHUNK, SPAN), F32), vm((256, QROWS), F32)]
+           vm((4, CHUNK, SPAN), F32), vm((256, QROWS), F32)]
         + [vm(a.shape, LOW) for a in arrays[:3] + arrays[7:]]
         + [pltpu.SemaphoreType.DMA((5,))]
         + Gather.scratch(9),
@@ -1396,13 +1407,14 @@
         gt_ref[...] = jnp.transpose(g)
         ht_ref[...] = jnp.transpose(h_ref[...])
 
-    def heads(t, w_ref, q_ref, kv_ref, p_ref, o_ref, gw_ref, dkv, d_sum, keys, take_bias):
+    def heads(t, w_ref, q_ref, kv_ref, p_ref, o_ref, gw_ref, dkv, d_sum, keys, take_bias, todo):
         do = mm(g_ref[...], w_ref[0, :, QROWS:]).astype(jnp.bfloat16)
         gw_ref[0, :, QROWS:] = mm(gt_ref[...], o_ref[0]).astype(jnp.bfloat16)
         dq = attend_back(
             q_ref[0], kv_ref[0], p_ref, do, dkv.at[pl.ds(t, 1)], d_ref, ds_ref, qt_ref, keys,
             take_bias,
         )
+        at_step(t, todo)
         gw_ref[0, :, :QROWS] = mm(ht_ref[...], dq).astype(jnp.bfloat16)
         d_sum[...] += mm(dq, w_ref[0, :, :QROWS], LAST)
 
@@ -1417,8 +1429,7 @@
 
     def cross_body(w_ref, q_ref, kv_ref, p_ref, o_ref, gw_ref):
         t = pl.program_id(0)
-        heads(t, w_ref, q_ref, kv_ref, p_ref, o_ref, gw_ref, dkv2, dc_ref, ENC_ROWS, None)
-        at_step(t, chunks[:4])
+        heads(t, w_ref, q_ref, kv_ref, p_ref, o_ref, gw_ref, dkv2, dc_ref, ENC_ROWS, None, chunks[:4])
 
     pltpu.emit_pipeline(
         cross_body, grid=(4,), in_specs=specs(ENC_ROWS), out_specs=[part((1, WIDTH, 512))]
@@ -1451,8 +1462,7 @@
             strip_ref[0, :, cols] += ds[:, :QROWS]
             strip_ref[1, :, cols] += ds[:, QROWS:]
 
-        heads(t, w_ref, q_ref, kv_ref, p_ref, o_ref, gw_ref, dkv1, dh_ref, KEYS, take_bias)
-        at_step(t, chunks[4:])
+        heads(t, w_ref, q_ref, kv_ref, p_ref, o_ref, gw_ref, dkv1, dh_ref, KEYS, take_bias, chunks[4:])
 
     pltpu.emit_pipeline(
         self_body, grid=(4,), in_specs=specs(KEYS), out_specs=[part((1, WIDTH, 512))]

time: 432 us -> 435 us (level)
  Pallas kernels: 401 us -> 406 us
    pallas_call x3, Pallas kernels: 376 us -> 381 us  [comm_call(): pl.pallas_call(kernel, out_shape=outs, in_specs=in_specs, out_specs=out_s...]
where the time goes in v7:
time: 435 us; the launch traced here: 428 us
  Pallas kernels  406 us (93%)
  local copies, waits for them, and re-layouts  10.5 us (2%)
  other arithmetic  10.4 us (2%)
    pallas_call x3, Pallas kernels, comm_call(): pl.pallas_call(kernel, out_shape=outs, in_specs=in_specs, out_specs=out_s...  381 us
    pallas_call x1, Pallas kernels, feed(): pl.pallas_call(feed_kernel, grid_spec=pltpu.PrefetchScalarGridSpec(num_sc...  24.8 us

profile of v7, /device:TPU:12, one launch (start us, length us, event | category | flops | bytes accessed | tf_op | source)
XLA Modules:
  0.0 427.6 jit_solution(4458253745111240635)
XLA Ops:
  0.7 0.6 pad_add_fusion.at
  1.2 0.8 convert_element_type.43
  2.0 0.7 fusion.1
  2.7 0.6 pad_convert_fusion.refs_7_
  3.3 1.5 pad_maximum_fusion.2.refs_6_
  4.8 1.6 pad_maximum_fusion
  6.4 150.4 %forward.1 = (bf16[4,704,1024]{2,1,0:T(8,128)(2,1)}, bf16[4,704,1024]{2,1,0:T(8,128)(2,1)}, bf16[4,704,1024]{2,1,0:T(8,128)(2,1)}, bf16[4,1024,512]{2,1,0:T(8,12...) custom-call(s32[2]{0:T(128)} %lengths.1, ...), custom_call_target="tpu_custom_call" | custom-call | tf_op jit(solution)/shard_map/forward/pallas_call | solution.py:931
  156.9 24.8 %feed.1 = (bf16[256,1024]{1,0:T(8,128)(2,1)}, f32[256,1024]{1,0:T(8,128)}, bf16[4,704,1024]{2,1,0:T(8,128)(2,1)}, bf16[4,704,1024]{2,1,0:T(8,128)(2,1)}, bf16[4,...) custom-call(s32[3]{0:T(128)} %pad_add_fusion.at, s32[2]{0:T(128)} %lengths.1, f32[256,1024]{1,0:T(8,128)} %get-tuple-element.58.x3_ref, ...), custom_call_target="tpu_custom_call" | custom-call | flops 12999999488 | bytes 40000000 | tf_op jit(solution)/shard_map/feed/pallas_call | solution.py:1179
  181.7 140.9 %backward.1 = (f32[704,128]{1,0:T(8,128)}, f32[704,128]{1,0:T(8,128)}, f32[704,128]{1,0:T(8,128)}, bf16[4,256,1024]{2,1,0:T(8,128)(2,1)}, bf16[256,1024]{1,0:T(8...) custom-call(bf16[4,704,1024]{2,1,0:T(8,128)(2,1)} %get-tuple-element, ...), custom_call_target="tpu_custom_call" | custom-call | tf_op jit(solution)/shard_map/backward/pallas_call | solution.py:931
  322.7 89.5 %finish.1 = (f32[4,128,512]{2,1,0:T(8,128)}, bf16[4,256,1024]{2,1,0:T(8,128)(2,1)}, bf16[4,128,1024]{2,1,0:T(8,128)(2,1)}) custom-call(bf16[4,1024,512]{2,1,0:T(8,128)(2,1)} %get-tuple-element.86.refs_0_, bf16[4,1024,512]{2,1,0:T(8,128)(2,1)} %get-tuple-element.87.refs_1_, bf16[4,1024,512]{2,1,0:T(8,128)(2,1)} %get-tuple-element.88.refs_2_, ...), custom_call_target="tpu_custom_call" | custom-call | tf_op jit(solution)/shard_map/finish/pallas_call | solution.py:931
  412.2 0.0 copy-start
  412.2 1.4 slice_bitcast_fusion.9
  413.5 0.7 slice_bitcast_fusion.8
  414.2 0.7 copy.37
  414.9 1.6 slice_bitcast_fusion.4
  416.5 1.9 slice_bitcast_fusion
  418.4 0.0 copy-start.1
  418.4 2.9 bitcast_convert_fusion.1
  421.4 0.0 copy-done
  421.4 0.0 copy-start.4
  421.4 0.0 copy-start.3
  421.4 2.5 bitcast_convert_fusion
  423.8 0.0 copy-done.1
  423.8 0.0 copy-start.2
  423.8 1.3 copy.42
  425.2 0.0 copy-done.4
  425.2 0.7 copy.43
  425.9 0.0 copy-done.3
  425.9 0.7 copy.44
  426.6 0.0 copy-done.2
  426.6 0.7 copy.45
Async XLA Ops:
  412.2 9.2 %copy-start = (bf16[4,256,1024]{2,1,0:T(8,128)(2,1)S(1)}, bf16[4,256,1024]{2,1,0:T(8,128)(2,1)}, u32[]{:S(2)}) copy-start(bf16[4,256,1024]{2,1,0:T(8,128)(2,1)} %get-tuple-element.92) | copy-start | bytes 6291460
  418.4 5.4 %copy-start.1 = (bf16[4,256,1024]{2,1,0:T(8,128)(2,1)S(1)}, bf16[4,256,1024]{2,1,0:T(8,128)(2,1)}, u32[]{:S(2)}) copy-start(bf16[4,256,1024]{2,1,0:T(8,128)(2,1)} %get-tuple-element.85) | copy-start | bytes 6291460
  421.4 3.8 copy-start.4
  421.4 4.5 %copy-start.3 = (f32[704,128]{1,0:T(8,128)S(1)}, f32[704,128]{1,0:T(8,128)}, u32[]{:S(2)}) copy-start(f32[704,128]{1,0:T(8,128)} %get-tuple-element.96) | copy-start | bytes 1081348
  423.8 2.8 copy-start.2
